TPU v7x, 32 devices: a whole 2x2x4 slice. The times are simulated.
32 devices in a mesh: grp: 2 (over y), lat: 4 (over z), lon: 2 (over x), ch: 2 (over core).
Axes of the slice: x: 2, y: 2, z: 4, core: 2. Of those that a mesh axis runs over, the one named last changes fastest.
Arguments:
- noisy_state: bfloat16 [256, 32, 512], P(('grp', 'ch'), 'lat', 'lon'), parts along dimension 0, may hold values from -6 to 6
- kernel_in: bfloat16 [3, 3, 128, 128], replicated, may hold values from -0.1875 to 0.1875
- bias_in: float32 [128], replicated, may hold values from -4 to 4
- kernel_out: bfloat16 [3, 3, 128, 128], replicated, may hold values from -0.1875 to 0.1875
- interp_weight: bfloat16 [64, 128, 128], P(('grp', 'lat', 'lon')), parts along dimension 0, may hold values from -0.5 to 0.5
- observed: bfloat16 [64, 128, 128], P(('grp', 'lat', 'lon'), 'ch'), parts along dimension 0, may hold values from -6 to 6
- obs_precision: bfloat16 [64, 128], P(('grp', 'lat', 'lon')), parts along dimension 0, may hold values from 0.29882812 to 3
- dest_tile: int32 [64], P(('grp', 'lat', 'lon')), parts along dimension 0, may hold values from 0 to 3, as said below
- row_offset: int32 [64], P(('grp', 'lat', 'lon')), parts along dimension 0, may hold values from 0 to 4
- col_offset: int32 [64], P(('grp', 'lat', 'lon')), parts along dimension 0, may hold values from 0 to 224
Outputs:
- next_state: float32 [256, 32, 512], P(('grp', 'ch'), 'lat', 'lon'), parts along dimension 0
- innovation: bfloat16 [64, 128, 128], P(('grp', 'lat', 'lon'), 'ch'), parts along dimension 0
There are 2 independent parts, one for each index of `grp`. A program takes and returns all parts, laid end to end along the dimension named above; an argument that names none is the same for every part. Nothing has to cross between parts.
Inputs may be any that keep to these rules, and one draw needn't show every extreme that they name: `dest_tile`: the 4 blocks of one device name any one latitude tile at most 2 times; a block's tile lies in the longitude column of the device that holds the block.
All inputs are finite; a program needn't handle non-finite values.
Results may differ from a plain program's by a relative error of at most 0.0085.
Values may be sent and summed in bfloat16 or wider, within the bound.
No kernel may reach another device: no remote copies, remote signals or barrier semaphores. Data moves between devices by JAX's collectives and lax.ppermute only.
A program may use at most 64 MiB of HBM per device.

v0:
```python
import jax
import jax.numpy as jnp
from jax import lax
from jax.experimental import pallas as pl
from jax.experimental.pallas import tpu as pltpu
from jax.sharding import PartitionSpec as P


PH = 4
PW = 32
CAP = 2
TAIL = 16
META = 16

keep_rate = 0.6
blend_rate = 0.4
guide_rate = 0.3

F32 = jnp.float32
BF16 = jnp.bfloat16
VMEM = pltpu.VMEM
SMEM = pltpu.SMEM
HBM = pltpu.MemorySpace.HBM
OUT = "out"


def call(kernel, outs, ins, scratch, aliases={}):
    near = lambda v, space: v if space == OUT else space(v.shape, v.dtype)
    spec = lambda space: pl.BlockSpec(memory_space=VMEM if space == OUT else space)
    run = pl.pallas_call(
        kernel,
        out_shape=[near(v, space) for v, space in outs],
        in_specs=[spec(space) for space in ins],
        out_specs=[spec(space) for _, space in outs],
        scratch_shapes=scratch,
        compiler_params=pltpu.CompilerParams(vmem_limit_bytes=24 * 1024 * 1024),
        input_output_aliases=aliases,
    )

    def apply(*args):
        return run(
            *(pltpu.with_memory_space_constraint(a, space) if space in (VMEM, HBM) else a for a, space in zip(args, ins))
        )

    return apply


def place_taps(w_ref, tap_of):
    c = w_ref.shape[0] // 4
    for b in range(3):
        for a in range(3):
            tap = tap_of(a, b)
            for row in range(2):
                at = (2 * b + row) * c
                w_ref[(a + row) * c : (a + row + 1) * c, at : at + c] = tap
        w_ref[3 * c : 4 * c, 2 * b * c : (2 * b + 1) * c] = jnp.zeros((c, c), BF16)
        w_ref[0:c, (2 * b + 1) * c : (2 * b + 2) * c] = jnp.zeros((c, c), BF16)


def weights_kernel(kin_ref, kout_ref, w1_ref, w2_ref):
    for w_ref, k_ref in ((w1_ref, kin_ref), (w2_ref, kout_ref)):
        place_taps(w_ref, lambda a, b: k_ref[a, b].astype(F32).T.astype(BF16))


def tail_of(row_ref, width):
    lane_rows = lax.broadcasted_iota(jnp.int32, (TAIL, row_ref.shape[-1]), 0)
    first = row_ref[0:TAIL, :].astype(F32)
    last = row_ref[width - TAIL : width, :].astype(F32)
    zero = jnp.zeros_like(first)
    return jnp.where(lane_rows < 2, first, jnp.where(lane_rows >= TAIL - 2, last, zero)).astype(BF16)


def write_tails(x_ref, tail_ref):
    for h in range(x_ref.shape[0]):
        tail_ref[h] = tail_of(x_ref.at[h], x_ref.shape[1])


def edge_kernel(x_ref, tail_ref, edge_ref):
    rows, width, _ = x_ref.shape
    first = lax.axis_index("ch") * (rows - 2)
    for i in range(2):
        edge_ref[i, 0:width, :] = x_ref[first + i]
        edge_ref[i, width : width + TAIL, :] = tail_ref[first + i]


def pack_kernel(
    dest_hbm,
    row_hbm,
    col_hbm,
    weight_hbm,
    obs_hbm,
    precision_hbm,
    noisy_hbm,
    chunk_ref,
    near_ref,
    dest_ref,
    row_ref,
    col_ref,
    weight_ref,
    obs_ref,
    precision_ref,
    scale_ref,
    sems,
):
    pairs = (
        (dest_hbm, dest_ref),
        (row_hbm, row_ref),
        (col_hbm, col_ref),
        (weight_hbm, weight_ref),
        (obs_hbm, obs_ref),
        (precision_hbm, precision_ref),
        (noisy_hbm, near_ref),
    )
    copies = [pltpu.make_async_copy(source, target, sems.at[n]) for n, (source, target) in enumerate(pairs)]
    for copy in copies:
        copy.start()
    core = lax.axis_index("ch")
    blocks, obs, _ = weight_ref.shape
    half = obs_ref.shape[1]
    first_meta = obs + CAP * half

    def clear(slot, _):
        chunk_ref[slot] = jnp.zeros(chunk_ref.shape[1:], BF16)
        return 0

    lax.fori_loop(0, chunk_ref.shape[0], clear, 0)
    for copy in copies[:-1]:
        copy.wait()
    scale_ref[...] = precision_ref[...].astype(F32)
    meta_rows = lax.broadcasted_iota(jnp.int32, (META, obs), 0)

    def pack(b, _):
        dest = dest_ref[b]
        rank = lax.fori_loop(0, b, lambda j, n: n + (dest_ref[j] == dest).astype(jnp.int32), 0)
        chunk_ref[dest, pl.ds(pl.multiple_of(obs + rank * half, 16), half), :] = obs_ref[b]

        @pl.when(rank == core)
        def _():
            chunk_ref[dest, 0:obs, :] = weight_ref[b]
            row = row_ref[b].astype(F32)
            high = lax.div(col_ref[b], 16).astype(F32)
            low = lax.rem(col_ref[b], 16).astype(F32)
            meta = jnp.where(
                meta_rows == 0,
                jnp.broadcast_to(scale_ref[pl.ds(b, 1), :], (META, obs)),
                jnp.where(meta_rows == 1, row, jnp.where(meta_rows == 2, high, low)),
            )
            chunk_ref[dest, first_meta : first_meta + META, :] = meta.astype(BF16)

        return 0

    lax.fori_loop(0, blocks, pack, 0)
    copies[-1].wait()


def prep_kernel(own_ref, other_ref, x_ref, tail_ref, flat_ref):
    core = lax.axis_index("ch")
    half, rows, width = own_ref.shape

    def place(ref, first):
        for part in range(width // 128):
            piece = ref[:, :, part * 128 : (part + 1) * 128].astype(F32)
            flat_ref[part, pl.ds(pl.multiple_of(first * rows, 8), half * rows), :] = piece.reshape(half * rows, 128)

    place(own_ref, core * half)
    place(other_ref, (1 - core) * half)
    for h in range(rows):
        for part in range(width // 128):
            plane = flat_ref[part, pl.ds(h, 2 * half, stride=rows), :]
            x_ref[h, part * 128 : (part + 1) * 128, :] = plane.T.astype(BF16)
    write_tails(x_ref, tail_ref)


def fill_extended(ext_ref, x_ref, tail_ref, mine_ref, other_ref):
    rows, width = x_ref.shape[0], x_ref.shape[1]
    core = lax.axis_index("ch")
    for i in range(2):
        ext_ref[core * (rows + 2) + i] = mine_ref[i]
        ext_ref[(1 - core) * (rows + 2) + i] = other_ref[i]
    for h in range(rows):
        ext_ref[h + 2, 0:width, :] = x_ref[h]
        ext_ref[h + 2, width : width + TAIL, :] = tail_ref[h]


def row_pair(src_ref, w_ref, first):
    c = src_ref.shape[-1]
    wide = src_ref.shape[1]
    lhs = jnp.concatenate([src_ref[first + k] for k in range(4)], axis=1)
    y = jnp.dot(lhs, w_ref[...], preferred_element_type=F32)
    out = []
    for row in range(2):
        left, mid, right = (y[:, (2 * b + row) * c : (2 * b + row + 1) * c] for b in range(3))
        out.append(pltpu.roll(left, 1, 0) + mid + pltpu.roll(right, wide - 1, 0))
    return out


def inside(ext_row, ext_rows):
    at = lax.axis_index("lat")
    last = lax.axis_size("lat") - 1
    return ((ext_row > 0) | (at > 0)) & ((ext_row < ext_rows - 1) | (at < last))


def own_pair(first, second):
    core = lax.axis_index("ch")
    half = first.shape[-1] // 2
    lane = lax.broadcasted_iota(jnp.int32, first.shape, len(first.shape) - 1)
    stays = jnp.where(core == 0, first, second)
    moves = pltpu.roll(jnp.where(core == 0, second, first), half, len(first.shape) - 1)
    low = (lane < half).astype(jnp.int32)
    return jnp.where(low == 1 - core, stays, moves)


def forward_kernel(
    x_ref,
    tail_ref,
    mine_ref,
    other_ref,
    w1_ref,
    w2_ref,
    bias_ref,
    block_ref,
    other_block_ref,
    slope_ref,
    base_ref,
    g_ref,
    gtail_ref,
    inn_ref,
    ext_ref,
    hidden_ref,
    den_ref,
    field_ref,
    turned_ref,
    value_ref,
    scale_ref,
    code_ref,
):
    core = lax.axis_index("ch")
    rows, width, c = x_ref.shape
    half = inn_ref.shape[1]
    sources, obs = block_ref.shape[0], block_ref.shape[2]
    fill_extended(ext_ref, x_ref, tail_ref, mine_ref, other_ref)

    def read(source, cap, first, count):
        at = slice(first, first + count)
        return jnp.where(core == cap, block_ref[source, at, :], other_block_ref[source, at, :])

    def locate(source, cap):
        meta = read(source, cap, obs + c, META).astype(F32)
        code = meta[1:2, :] * 65536.0 + meta[2:3, :] * 16.0 + meta[3:4, :]
        code_ref[source * CAP + cap] = jnp.max(code).astype(jnp.int32)

    def turn(source, cap):
        slot = source * CAP + cap
        turned_ref[slot] = read(source, cap, 0, obs).T
        at = slice(obs + cap * half, obs + (cap + 1) * half)
        mine, theirs = block_ref[source, at, :], other_block_ref[source, at, :]
        low, high = jnp.where(core == 0, mine, theirs), jnp.where(core == 0, theirs, mine)
        value_ref[slot] = jnp.concatenate([low, high], axis=0).T
        row = read(source, cap, obs + c, META).astype(F32)[0:1, :]
        scale_ref[slot] = jnp.broadcast_to(row, (c, obs)).T

    def each(task, first, last):
        if last - first <= 8:
            for source in range(first, last):
                for cap in range(CAP):
                    task(source, cap)
            return

        def step(source, _):
            for cap in range(CAP):
                task(source, cap)
            return 0

        lax.fori_loop(first, last, step, 0)

    each(locate, 0, sources)
    bias = bias_ref[...]
    for g in range((rows + 2) // 2):
        for i, y in enumerate(row_pair(ext_ref, w1_ref, 2 * g)):
            r = 2 * g + i
            pre = y + bias
            s = 1.0 / (1.0 + jnp.exp(-pre))
            slope_ref[r] = s * (1.0 + pre * (1.0 - s))
            hidden_ref[r] = jnp.where(inside(r, rows + 2), pre * s, 0.0).astype(BF16)
    groups = rows // 2
    for g in range(groups):
        each(turn, sources * g // groups, sources * (g + 1) // groups)
        for i, y in enumerate(row_pair(hidden_ref, w2_ref, 2 * g)):
            r = 2 * g + i
            noisy = x_ref[r].astype(F32)
            den_ref[r] = (noisy + y[0:width, :]).astype(BF16).astype(F32)
            field_ref[r] = jnp.zeros((width, c), F32)

    def observe(source, cap):
        slot = source * CAP + cap
        code = code_ref[slot]
        row = lax.shift_right_logical(code, 16)
        col = lax.bitwise_and(code, 65535)
        patch = jnp.concatenate([den_ref[row + i, pl.ds(col, PW), :] for i in range(PH)], axis=0).astype(BF16)
        predicted = jnp.dot(read(source, cap, 0, obs), patch, preferred_element_type=F32)
        residual = predicted - value_ref[slot].astype(F32)
        weighted = (residual * scale_ref[slot]).astype(BF16)
        pulled = jnp.dot(turned_ref[slot], weighted, preferred_element_type=F32)
        for i in range(PH):
            field_ref[row + i, pl.ds(col, PW), :] += pulled[i * PW : (i + 1) * PW, :]
        turned = residual.astype(BF16).T
        inn_ref[slot] = jnp.where(core == 0, turned[0:half], turned[half : 2 * half])

    each(observe, 0, sources)

    for g in range(groups):
        base = []
        for r in (2 * g, 2 * g + 1):
            field = field_ref[r]
            noisy = ext_ref[r + 2, 0:width, :].astype(F32)
            base.append(keep_rate * noisy + blend_rate * den_ref[r] - guide_rate * field)
            g_ref[r] = field.astype(BF16)
        base_ref[g] = own_pair(*base)
    write_tails(g_ref, gtail_ref)


def backward_kernel(
    x_ref,
    tail_ref,
    mine_ref,
    other_ref,
    kin_ref,
    kout_ref,
    base_ref,
    slope_ref,
    back_ref,
    dest_hbm,
    next_ref,
    inn_hbm,
    ext_ref,
    grad_ref,
    flat_ref,
    w3_ref,
    w4_ref,
    dest_ref,
    dest_sem,
    inn_sems,
):
    dest_copy = pltpu.make_async_copy(dest_hbm, dest_ref, dest_sem)
    dest_copy.start()
    rows, width, c = x_ref.shape
    wide = ext_ref.shape[1]
    half = next_ref.shape[0]
    fill_extended(ext_ref, x_ref, tail_ref, mine_ref, other_ref)
    place_taps(w3_ref, lambda a, b: kout_ref[2 - a, 2 - b])
    zero = jnp.zeros((c, c), F32)
    for b in range(3):
        taps = [zero] + [kin_ref[2 - a, 2 - b].astype(F32) for a in range(3)] + [zero]
        for k in range(4):
            w4_ref[k * c : (k + 1) * c, b * c : (b + 1) * c] = own_pair(taps[k + 1], taps[k]).astype(BF16)

    for g in range((rows + 2) // 2):
        for i, y in enumerate(row_pair(ext_ref, w3_ref, 2 * g)):
            r = 2 * g + i
            grad_ref[r] = jnp.where(inside(r, rows + 2), y * slope_ref[r], 0.0).astype(BF16)

    dest_copy.wait()

    def give(b):
        dest = dest_ref[b]
        rank = lax.fori_loop(0, b, lambda j, n: n + (dest_ref[j] == dest).astype(jnp.int32), 0)
        return pltpu.make_async_copy(back_ref.at[dest * CAP + rank], inn_hbm.at[b], inn_sems.at[b])

    def start(b, _):
        give(b).start()
        return 0

    def finish(b, _):
        pltpu.make_async_copy(back_ref.at[0], inn_hbm.at[b], inn_sems.at[b]).wait()
        return 0

    lax.fori_loop(0, inn_hbm.shape[0], start, 0)
    for g in range(rows // 2):
        lhs = jnp.concatenate([grad_ref[2 * g + k] for k in range(4)], axis=1)
        y = jnp.dot(lhs, w4_ref[...], preferred_element_type=F32)
        y = pltpu.roll(y[:, 0:c], 1, 0) + y[:, c : 2 * c] + pltpu.roll(y[:, 2 * c : 3 * c], wide - 1, 0)
        out = base_ref[g] - guide_rate * y[0:width, :]
        for part in range(width // 128):
            plane = out[part * 128 : (part + 1) * 128, :].T
            for i in range(2):
                flat_ref[part, pl.ds(2 * g + i, half, stride=rows), :] = plane[i * half : (i + 1) * half]
    for part in range(width // 128):
        next_ref[:, :, part * 128 : (part + 1) * 128] = flat_ref[part].reshape(half, rows, 128)
    lax.fori_loop(0, inn_hbm.shape[0], finish, 0)


def swapped(value):
    return lax.ppermute(value, "ch", [(0, 1), (1, 0)])


def from_row_neighbour(value):
    lats = lax.axis_size("lat")
    steps = ((0, -1), (1, 1))
    pairs = [
        (i * 2 + core, (i + step) * 2 + 1 - core) for i in range(lats) for core, step in steps if 0 <= i + step < lats
    ]
    return lax.ppermute(value, ("lat", "ch"), pairs)


def from_lon_neighbours(value):
    lons = lax.axis_size("lon")
    move = lambda step: lax.ppermute(value, "lon", [(j, (j + step) % lons) for j in range(lons)])
    if lons == 2:
        return move(1)
    at = lax.broadcasted_iota(jnp.int32, (1, TAIL, 1), 1)
    return jnp.where(at < TAIL // 2, move(-1), move(1))


def exchanged(x, tail, along):
    _, width, c = x.shape
    beside = from_lon_neighbours(tail)
    (edge,) = call(edge_kernel, [(shape((2, width + TAIL, c), BF16), VMEM)], [VMEM] * 2, [])(x, beside)
    mine = from_row_neighbour(edge)
    mine, along = lax.optimization_barrier((mine, along))
    return (beside, mine, swapped(mine)), along


def shape(dims, dtype):
    return jax.ShapeDtypeStruct(dims, dtype)


def body(
    noisy_state,
    kernel_in,
    bias_in,
    kernel_out,
    interp_weight,
    observed,
    obs_precision,
    dest_tile,
    row_offset,
    col_offset,
):
    half, rows, width = noisy_state.shape
    c = kernel_in.shape[-1]
    blocks, obs, _ = interp_weight.shape
    lats = lax.axis_size("lat")
    slots = lats * CAP
    wide = width + TAIL
    other = swapped(noisy_state)
    chunk_shape = shape((lats, obs + CAP * half + META, obs), BF16)
    chunk, near = call(
        pack_kernel,
        [(chunk_shape, VMEM), (shape(noisy_state.shape, BF16), VMEM)],
        [HBM] * 7,
        [
            SMEM((blocks,), jnp.int32),
            SMEM((blocks,), jnp.int32),
            SMEM((blocks,), jnp.int32),
            VMEM(interp_weight.shape, BF16),
            VMEM(observed.shape, BF16),
            VMEM(obs_precision.shape, BF16),
            VMEM(obs_precision.shape, F32),
            pltpu.SemaphoreType.DMA((7,)),
        ],
    )(dest_tile, row_offset, col_offset, interp_weight, observed, obs_precision, noisy_state)
    block = lax.all_to_all(chunk, "lat", split_axis=0, concat_axis=0, tiled=True)
    tail_shape = shape((rows, TAIL, c), BF16)
    x, tail = call(
        prep_kernel,
        [(shape((rows, width, c), BF16), VMEM), (tail_shape, VMEM)],
        [VMEM] * 2,
        [VMEM((width // 128, c * rows, 128), F32)],
    )(near, other)
    w1, w2 = call(weights_kernel, [(shape((4 * c, 6 * c), BF16), VMEM)] * 2, [VMEM] * 2, [])(kernel_in, kernel_out)
    halo, block = exchanged(x, tail, block)
    slope, base, g, tail, inn = call(
        forward_kernel,
        [
            (shape((rows + 2, wide, c), F32), VMEM),
            (shape((rows // 2, width, c), F32), VMEM),
            (shape((rows, width, c), BF16), VMEM),
            (tail_shape, VMEM),
            (shape((slots, half, obs), BF16), VMEM),
        ],
        [VMEM] * 9,
        [
            VMEM((rows + 4, wide, c), BF16),
            VMEM((rows + 2, wide, c), BF16),
            VMEM((rows, width, c), F32),
            VMEM((rows, width, c), F32),
            VMEM((slots, obs, obs), BF16),
            VMEM((slots, obs, c), BF16),
            VMEM((slots, obs, c), F32),
            SMEM((slots,), jnp.int32),
        ],
        {0: 2, 1: 3},
    )(x, *halo, w1, w2, bias_in.reshape(1, c), block, swapped(block))
    halo, _ = exchanged(g, tail, ())
    back = lax.all_to_all(inn, "lat", split_axis=0, concat_axis=0, tiled=True)
    next_state, innovation = call(
        backward_kernel,
        [(shape((half, rows, width), F32), OUT), (shape(observed.shape, BF16), HBM)],
        [VMEM] * 9 + [HBM],
        [
            VMEM((rows + 4, wide, c), BF16),
            VMEM((rows + 2, wide, c), BF16),
            VMEM((width // 128, half * rows, 128), F32),
            VMEM((4 * c, 6 * c), BF16),
            VMEM((4 * c, 3 * c), BF16),
            SMEM((blocks,), jnp.int32),
            pltpu.SemaphoreType.DMA,
            pltpu.SemaphoreType.DMA((blocks,)),
        ],
    )(g, *halo, kernel_in, kernel_out, base, slope, back, dest_tile)
    return next_state, innovation


def solution(mesh):
    return jax.shard_map(
        body,
        mesh=mesh,
        in_specs=(
            P(("grp", "ch"), "lat", "lon"),
            P(),
            P(),
            P(),
            P(("grp", "lat", "lon"), None, None),
            P(("grp", "lat", "lon"), "ch", None),
            P(("grp", "lat", "lon"), None),
            P(("grp", "lat", "lon")),
            P(("grp", "lat", "lon")),
            P(("grp", "lat", "lon")),
        ),
        out_specs=(P(("grp", "ch"), "lat", "lon"), P(("grp", "lat", "lon"), "ch", None)),
        check_vma=False,
    )
```

profile of v0, /device:TPU:0, one launch (start us, length us, event | category | flops | bytes accessed | tf_op | source)
XLA Modules:
  0.0 46.2 jit_solution(15210869603774640473)
XLA Ops:
  0.6 0.0 copy-start.1
  0.6 0.0 copy-start
  0.7 0.0 copy-start.3
  0.7 0.6 %collective-permute-start = (bf16[64,8,256]{2,1,0:T(8,128)(2,1)}, bf16[64,8,256]{2,1,0:T(8,128)(2,1)S(1)}, u32[]{:S(2)}, u32[]{:S(2)}) collective-permute-start(bf16[64,8,256]{2,1,0:T(8,128)(2,1)} %noisy_hbm.1), channel_id=1, source_target_pairs={{0,1},{1,0},{2,3},{3,2},{4,5},{5,4},{6,7},{7,6},{8,9},{9,8},{10,11... | collective-permute-start | bytes 786440 | tf_op jit(solution)/shard_map/ppermute | solution.py:393
  1.2 1.8 %shard_map.113 = (bf16[4,272,128]{2,1,0:T(8,128)(2,1)}, bf16[64,8,256]{2,1,0:T(8,128)(2,1)S(1)}) custom-call(s32[4]{0:T(128)} %dest_hbm.3, s32[4]{0:T(128)} %row_hbm.1, s32[4]{0:T(128)} %col_hbm.1, bf16[4,128,128]{2,1,0:T(8,128)(2,1)} %weight_hbm.1, bf16[4,64,128]{2,1,0:T(8,128)(2,1)} %obs_hbm.1, bf16[4,128]{1,0:T(4,128)(2,1)} %precision_hbm.1, ...), custom_call_target="tpu_custom_call" | custom-call | tf_op jit(solution)/shard_map/pallas_call | solution.py:41
  3.1 5.9 %all-to-all-start = ((bf16[4,272,128]{2,1,0:T(8,128)(2,1)}), bf16[4,272,128]{2,1,0:T(8,128)(2,1)S(1)}, u32[]{:S(2)}, u32[]{:S(2)}) async-start(bf16[4,272,128]{2,1,0:T(8,128)(2,1)} %get-tuple-element.18), calls=%async_computation | async-start | bytes 557056 | tf_op jit(solution)/shard_map/all_to_all | solution.py:462
  9.0 0.0 collective-permute-done.other_ref
  9.0 0.3 shard_map.114
  9.3 1.6 %collective-permute-start.1 = (bf16[8,16,128]{2,1,0:T(8,128)(2,1)S(1)}, bf16[8,16,128]{2,1,0:T(8,128)(2,1)S(1)}, u32[]{:S(2)}, u32[]{:S(2)}) collective-permute-start(bf16[8,16,128]{2,1,0:T(8,128)(2,1)S(1)} %get-tuple-element.17), channel_id=1, source_target_pairs={{0,2},{2,0},{1,3},{3,1},{4,6},{6,4},{5,7},{7,5},{8,10},{10,8},{9,1... | collective-permute-start | bytes 98312 | tf_op jit(solution)/shard_map/ppermute | solution.py:407
  10.9 2.4 %collective-permute-done.1.tail_ref = bf16[8,16,128]{2,1,0:T(8,128)(2,1)S(1)} collective-permute-done((bf16[8,16,128]{2,1,0:T(8,128)(2,1)S(1)}, bf16[8,16,128]{2,1,0:T(8,128)(2,1)S(1)}, u32[]{:S(2)}, u32[]{:S(2)}) %collective-permute-start.1) | collective-permute-done | bytes 32800 | tf_op jit(solution)/shard_map/ppermute | solution.py:407
  13.3 0.7 %collective-permute-start.2 = (bf16[2,272,128]{2,1,0:T(8,128)(2,1)S(1)}, bf16[2,272,128]{2,1,0:T(8,128)(2,1)S(1)}, u32[]{:S(2)}, u32[]{:S(2)}) collective-permute-start(bf16[2,272,128]{2,1,0:T(8,128)(2,1)S(1)} %shard_map.115), channel_id=1, source_target_pairs={{1,4},{4,1},{5,8},{8,5},{9,12},{12,9},{3,6},{6,3},{7,10},{10,7},{1... | collective-permute-start | bytes 417800 | tf_op jit(solution)/shard_map/ppermute | solution.py:402
  14.0 4.8 %all-to-all-done.block_ref = bf16[4,272,128]{2,1,0:T(8,128)(2,1)S(1)} async-done(((bf16[4,272,128]{2,1,0:T(8,128)(2,1)}), bf16[4,272,128]{2,1,0:T(8,128)(2,1)S(1)}, u32[]{:S(2)}, u32[]{:S(2)}) %all-to-all-start) | async-done | bytes 278560 | tf_op jit(solution)/shard_map/all_to_all | solution.py:462
  18.8 0.0 collective-permute-done.2.mine_ref
  18.8 1.3 %collective-permute-start.4 = (bf16[4,272,128]{2,1,0:T(8,128)(2,1)S(1)}, bf16[4,272,128]{2,1,0:T(8,128)(2,1)S(1)}, u32[]{:S(2)}, u32[]{:S(2)}) collective-permute-start(bf16[4,272,128]{2,1,0:T(8,128)(2,1)S(1)} %all-to-all-done.block_ref), channel_id=1, source_target_pairs={{0,1},{1,0},{2,3},{3,2},{4,5},{5,4},{6,7},{7,6},{8,9},{9,8},{10,11... | collective-permute-start | bytes 835592 | tf_op jit(solution)/shard_map/ppermute | solution.py:393
  20.1 0.0 collective-permute-start.3
  20.1 0.0 copy-done.1
  20.2 0.0 copy-done
  20.2 0.3 shard_map.116
  20.4 1.1 %collective-permute-done.3.other_ref = bf16[2,272,128]{2,1,0:T(8,128)(2,1)S(1)} collective-permute-done((bf16[2,272,128]{2,1,0:T(8,128)(2,1)S(1)}, bf16[2,272,128]{2,1,0:T(8,128)(2,1)S(1)}, u32[]{:S(2)}, u32[]{:S(2)}) %collective-permute-start.3) | collective-permute-done | bytes 139296 | tf_op jit(solution)/shard_map/ppermute | solution.py:393
  21.5 0.0 collective-permute-done.4.other_block_ref
  21.5 0.0 copy-done.3
  21.5 3.9 %shard_map.117 = (f32[10,272,128]{2,1,0:T(8,128)S(1)}, f32[4,256,128]{2,1,0:T(8,128)S(1)}, bf16[8,256,128]{2,1,0:T(8,128)(2,1)S(1)}, bf16[8,16,128]{2,1,0:T(8,128)(2,1)S(1)}, bf16[8,64,128]{2,1,0:T(8,128)(2,1)S(1)}) custom-call(bf16[8,256,128]{2,1,0:T(8,128)(2,1)S(1)} %get-tuple-element.16.x_ref, ...), custom_call_target="tpu_custom_call", output_to_operand_aliasing={{2}: (0, {}), {3}: (1, {})} | custom-call | tf_op jit(solution)/shard_map/pallas_call | solution.py:41
  25.4 0.0 copy-start.2
  25.4 1.5 %collective-permute-start.5 = (bf16[8,16,128]{2,1,0:T(8,128)(2,1)S(1)}, bf16[8,16,128]{2,1,0:T(8,128)(2,1)S(1)}, u32[]{:S(2)}, u32[]{:S(2)}) collective-permute-start(bf16[8,16,128]{2,1,0:T(8,128)(2,1)S(1)} %get-tuple-element.24), channel_id=1, source_target_pairs={{0,2},{2,0},{1,3},{3,1},{4,6},{6,4},{5,7},{7,5},{8,10},{10,8},{9,1... | collective-permute-start | bytes 98312 | tf_op jit(solution)/shard_map/ppermute | solution.py:407
  26.9 2.4 %collective-permute-done.5.tail_ref = bf16[8,16,128]{2,1,0:T(8,128)(2,1)S(1)} collective-permute-done((bf16[8,16,128]{2,1,0:T(8,128)(2,1)S(1)}, bf16[8,16,128]{2,1,0:T(8,128)(2,1)S(1)}, u32[]{:S(2)}, u32[]{:S(2)}) %collective-permute-start.5) | collective-permute-done | bytes 32800 | tf_op jit(solution)/shard_map/ppermute | solution.py:407
  29.4 0.7 %collective-permute-start.6 = (bf16[2,272,128]{2,1,0:T(8,128)(2,1)S(1)}, bf16[2,272,128]{2,1,0:T(8,128)(2,1)S(1)}, u32[]{:S(2)}, u32[]{:S(2)}) collective-permute-start(bf16[2,272,128]{2,1,0:T(8,128)(2,1)S(1)} %shard_map.118), channel_id=1, source_target_pairs={{1,4},{4,1},{5,8},{8,5},{9,12},{12,9},{3,6},{6,3},{7,10},{10,7},{1... | collective-permute-start | bytes 417800 | tf_op jit(solution)/shard_map/ppermute | solution.py:402
  30.1 0.0 copy-done.2
  30.1 6.3 %all-to-all-start.1 = ((bf16[8,64,128]{2,1,0:T(8,128)(2,1)}), bf16[8,64,128]{2,1,0:T(8,128)(2,1)S(1)}, u32[]{:S(2)}, u32[]{:S(2)}) async-start(bf16[8,64,128]{2,1,0:T(8,128)(2,1)} %copy-done.2), calls=%async_computation.1 | async-start | bytes 262144 | tf_op jit(solution)/shard_map/all_to_all | solution.py:495
  36.4 0.0 collective-permute-done.6.mine_ref
  36.4 0.4 collective-permute-start.7
  36.8 6.1 %all-to-all-done.1.back_ref = bf16[8,64,128]{2,1,0:T(8,128)(2,1)S(1)} async-done(((bf16[8,64,128]{2,1,0:T(8,128)(2,1)}), bf16[8,64,128]{2,1,0:T(8,128)(2,1)S(1)}, u32[]{:S(2)}, u32[]{:S(2)}) %all-to-all-start.1) | async-done | bytes 131104 | tf_op jit(solution)/shard_map/all_to_all | solution.py:495
  42.9 0.0 collective-permute-done.7.other_ref
  42.9 3.3 %shard_map.119 = (f32[64,8,256]{2,1,0:T(8,128)}, bf16[4,64,128]{2,1,0:T(8,128)(2,1)}) custom-call(bf16[8,256,128]{2,1,0:T(8,128)(2,1)S(1)} %get-tuple-element.23.x_ref, bf16[8,16,128]{2,1,0:T(8,128)(2,1)S(1)} %collective-permute-done.5.tail_ref, bf16[2,272,128]{2,1,0:T(8,128)(2,1)S(1)} %collective-permute-done.6.mine_ref, ...), custom_call_target="tpu_custom_call" | custom-call | tf_op jit(solution)/shard_map/pallas_call | solution.py:41
  (2 shorter events, 0.0 us)
Async XLA Ops:
  0.6 19.5 %copy-start.1 = (bf16[3,3,128,128]{3,2,1,0:T(8,128)(2,1)S(1)}, bf16[3,3,128,128]{3,2,1,0:T(8,128)(2,1)}, u32[]{:S(2)}) copy-start(bf16[3,3,128,128]{3,2,1,0:T(8,128)(2,1)} %kout_ref.3) | copy-start | bytes 884740
  0.6 19.5 %copy-start = (bf16[3,3,128,128]{3,2,1,0:T(8,128)(2,1)S(1)}, bf16[3,3,128,128]{3,2,1,0:T(8,128)(2,1)}, u32[]{:S(2)}) copy-start(bf16[3,3,128,128]{3,2,1,0:T(8,128)(2,1)} %kin_ref.3) | copy-start | bytes 884740
  0.7 20.9 %copy-start.3 = (f32[128]{0:T(128)S(1)}, f32[128]{0:T(128)}, u32[]{:S(2)}) copy-start(f32[128]{0:T(128)} %param.12) | copy-start | bytes 1540
  0.7 8.3 %collective-permute-start = (bf16[64,8,256]{2,1,0:T(8,128)(2,1)}, bf16[64,8,256]{2,1,0:T(8,128)(2,1)S(1)}, u32[]{:S(2)}, u32[]{:S(2)}) collective-permute-start(bf16[64,8,256]{2,1,0:T(8,128)(2,1)} %noisy_hbm.1), channel_id=1, source_target_pairs={{0,1},{1,0},{2,3},{3,2},{4,5},{5,4},{6,7},{7,6},{8,9},{9,8},{10,11... | collective-permute-start | bytes 786440 | tf_op jit(solution)/shard_map/ppermute | solution.py:393
  3.1 15.8 %all-to-all-start = ((bf16[4,272,128]{2,1,0:T(8,128)(2,1)}), bf16[4,272,128]{2,1,0:T(8,128)(2,1)S(1)}, u32[]{:S(2)}, u32[]{:S(2)}) async-start(bf16[4,272,128]{2,1,0:T(8,128)(2,1)} %get-tuple-element.18), calls=%async_computation | async-start | bytes 557056 | tf_op jit(solution)/shard_map/all_to_all | solution.py:462
  9.3 4.0 %collective-permute-start.1 = (bf16[8,16,128]{2,1,0:T(8,128)(2,1)S(1)}, bf16[8,16,128]{2,1,0:T(8,128)(2,1)S(1)}, u32[]{:S(2)}, u32[]{:S(2)}) collective-permute-start(bf16[8,16,128]{2,1,0:T(8,128)(2,1)S(1)} %get-tuple-element.17), channel_id=1, source_target_pairs={{0,2},{2,0},{1,3},{3,1},{4,6},{6,4},{5,7},{7,5},{8,10},{10,8},{9,1... | collective-permute-start | bytes 98312 | tf_op jit(solution)/shard_map/ppermute | solution.py:407
  13.3 5.5 %collective-permute-start.2 = (bf16[2,272,128]{2,1,0:T(8,128)(2,1)S(1)}, bf16[2,272,128]{2,1,0:T(8,128)(2,1)S(1)}, u32[]{:S(2)}, u32[]{:S(2)}) collective-permute-start(bf16[2,272,128]{2,1,0:T(8,128)(2,1)S(1)} %shard_map.115), channel_id=1, source_target_pairs={{1,4},{4,1},{5,8},{8,5},{9,12},{12,9},{3,6},{6,3},{7,10},{10,7},{1... | collective-permute-start | bytes 417800 | tf_op jit(solution)/shard_map/ppermute | solution.py:402
  18.8 2.7 %collective-permute-start.4 = (bf16[4,272,128]{2,1,0:T(8,128)(2,1)S(1)}, bf16[4,272,128]{2,1,0:T(8,128)(2,1)S(1)}, u32[]{:S(2)}, u32[]{:S(2)}) collective-permute-start(bf16[4,272,128]{2,1,0:T(8,128)(2,1)S(1)} %all-to-all-done.block_ref), channel_id=1, source_target_pairs={{0,1},{1,0},{2,3},{3,2},{4,5},{5,4},{6,7},{7,6},{8,9},{9,8},{10,11... | collective-permute-start | bytes 835592 | tf_op jit(solution)/shard_map/ppermute | solution.py:393
  20.1 1.4 %collective-permute-start.3 = (bf16[2,272,128]{2,1,0:T(8,128)(2,1)S(1)}, bf16[2,272,128]{2,1,0:T(8,128)(2,1)S(1)}, u32[]{:S(2)}, u32[]{:S(2)}) collective-permute-start(bf16[2,272,128]{2,1,0:T(8,128)(2,1)S(1)} %collective-permute-done.2.mine_ref), channel_id=1, source_target_pairs={{0,1},{1,0},{2,3},{3,2},{4,5},{5,4},{6,7},{7,6},{8,9},{9,8},{10,11... | collective-permute-start | bytes 417800 | tf_op jit(solution)/shard_map/ppermute | solution.py:393
  25.4 4.7 %copy-start.2 = (bf16[8,64,128]{2,1,0:T(8,128)(2,1)}, bf16[8,64,128]{2,1,0:T(8,128)(2,1)S(1)}, u32[]{:S(2)}) copy-start(bf16[8,64,128]{2,1,0:T(8,128)(2,1)S(1)} %get-tuple-element.27) | copy-start | bytes 393220
  25.4 4.0 %collective-permute-start.5 = (bf16[8,16,128]{2,1,0:T(8,128)(2,1)S(1)}, bf16[8,16,128]{2,1,0:T(8,128)(2,1)S(1)}, u32[]{:S(2)}, u32[]{:S(2)}) collective-permute-start(bf16[8,16,128]{2,1,0:T(8,128)(2,1)S(1)} %get-tuple-element.24), channel_id=1, source_target_pairs={{0,2},{2,0},{1,3},{3,1},{4,6},{6,4},{5,7},{7,5},{8,10},{10,8},{9,1... | collective-permute-start | bytes 98312 | tf_op jit(solution)/shard_map/ppermute | solution.py:407
  29.4 7.0 %collective-permute-start.6 = (bf16[2,272,128]{2,1,0:T(8,128)(2,1)S(1)}, bf16[2,272,128]{2,1,0:T(8,128)(2,1)S(1)}, u32[]{:S(2)}, u32[]{:S(2)}) collective-permute-start(bf16[2,272,128]{2,1,0:T(8,128)(2,1)S(1)} %shard_map.118), channel_id=1, source_target_pairs={{1,4},{4,1},{5,8},{8,5},{9,12},{12,9},{3,6},{6,3},{7,10},{10,7},{1... | collective-permute-start | bytes 417800 | tf_op jit(solution)/shard_map/ppermute | solution.py:402
  30.1 12.8 %all-to-all-start.1 = ((bf16[8,64,128]{2,1,0:T(8,128)(2,1)}), bf16[8,64,128]{2,1,0:T(8,128)(2,1)S(1)}, u32[]{:S(2)}, u32[]{:S(2)}) async-start(bf16[8,64,128]{2,1,0:T(8,128)(2,1)} %copy-done.2), calls=%async_computation.1 | async-start | bytes 262144 | tf_op jit(solution)/shard_map/all_to_all | solution.py:495
  36.4 6.5 %collective-permute-start.7 = (bf16[2,272,128]{2,1,0:T(8,128)(2,1)S(1)}, bf16[2,272,128]{2,1,0:T(8,128)(2,1)S(1)}, u32[]{:S(2)}, u32[]{:S(2)}) collective-permute-start(bf16[2,272,128]{2,1,0:T(8,128)(2,1)S(1)} %collective-permute-done.6.mine_ref), channel_id=1, source_target_pairs={{0,1},{1,0},{2,3},{3,2},{4,5},{5,4},{6,7},{7,6},{8,9},{9,8},{10,11... | collective-permute-start | bytes 417800 | tf_op jit(solution)/shard_map/ppermute | solution.py:393
where the time goes:
time: 46.5 us; the launch traced here: 46.2 us
  starting transfers between devices  18.9 us (41%)
  waiting for transfers between devices  16.9 us (36%)
  Pallas kernels  9.6 us (21%)
  between operations  0.73 us (2%)
    pallas_call x7, Pallas kernels, apply(): run(*(pltpu.with_memory_space_constraint(a, space) if space in (VMEM, HBM...  9.6 us
    all_to_all x1, starting transfers between devices, body(): back = lax.all_to_all(inn, 'lat', split_axis=0, concat_axis=0, tiled=True)  6.27 us
    all_to_all x1, waiting for transfers between devices, body(): back = lax.all_to_all(inn, 'lat', split_axis=0, concat_axis=0, tiled=True)  6.09 us
    all_to_all x1, starting transfers between devices, body(): lax.all_to_all(chunk, 'lat', split_axis=0, concat_axis=0, tiled=True)  5.93 us
    ppermute x2, waiting for transfers between devices, from_lon_neighbours(): lax.ppermute(value, 'lon', [(j, (j + step) % lons) for j in range(lons)])  4.87 us
    all_to_all x1, waiting for transfers between devices, body(): lax.all_to_all(chunk, 'lat', split_axis=0, concat_axis=0, tiled=True)  4.83 us
    ppermute x2, starting transfers between devices, from_lon_neighbours(): lax.ppermute(value, 'lon', [(j, (j + step) % lons) for j in range(lons)])  3.09 us
    ppermute x4, starting transfers between devices, swapped(): return lax.ppermute(value, 'ch', [(0, 1), (1, 0)])  2.32 us
  transfers between devices with their start and end apart: 10, of which 5 were waited for; matrix products, arithmetic and copies ran while one was open for 0% of the time, Pallas kernels for 5%

commit v1 on v0

--- a/solution.py
+++ b/solution.py
@@ -57,9 +57,29 @@
         w_ref[0:c, (2 * b + 1) * c : (2 * b + 2) * c] = jnp.zeros((c, c), BF16)
 
 
-def weights_kernel(kin_ref, kout_ref, w1_ref, w2_ref):
+def forward_taps(w1_ref, w2_ref, kin_ref, kout_ref):
     for w_ref, k_ref in ((w1_ref, kin_ref), (w2_ref, kout_ref)):
         place_taps(w_ref, lambda a, b: k_ref[a, b].astype(F32).T.astype(BF16))
+
+
+def own_pair(first, second):
+    core = lax.axis_index("ch")
+    half = first.shape[-1] // 2
+    lane = lax.broadcasted_iota(jnp.int32, first.shape, len(first.shape) - 1)
+    stays = jnp.where(core == 0, first, second)
+    moves = pltpu.roll(jnp.where(core == 0, second, first), half, len(first.shape) - 1)
+    low = (lane < half).astype(jnp.int32)
+    return jnp.where(low == 1 - core, stays, moves)
+
+
+def backward_taps(w3_ref, w4_ref, kin_ref, kout_ref):
+    c = kin_ref.shape[-1]
+    place_taps(w3_ref, lambda a, b: kout_ref[2 - a, 2 - b])
+    zero = jnp.zeros((c, c), F32)
+    for b in range(3):
+        taps = [zero] + [kin_ref[2 - a, 2 - b].astype(F32) for a in range(3)] + [zero]
+        for k in range(4):
+            w4_ref[k * c : (k + 1) * c, b * c : (b + 1) * c] = own_pair(taps[k + 1], taps[k]).astype(BF16)
 
 
 def tail_of(row_ref, width):
@@ -171,17 +191,6 @@
     write_tails(x_ref, tail_ref)
 
 
-def fill_extended(ext_ref, x_ref, tail_ref, mine_ref, other_ref):
-    rows, width = x_ref.shape[0], x_ref.shape[1]
-    core = lax.axis_index("ch")
-    for i in range(2):
-        ext_ref[core * (rows + 2) + i] = mine_ref[i]
-        ext_ref[(1 - core) * (rows + 2) + i] = other_ref[i]
-    for h in range(rows):
-        ext_ref[h + 2, 0:width, :] = x_ref[h]
-        ext_ref[h + 2, width : width + TAIL, :] = tail_ref[h]
-
-
 def row_pair(src_ref, w_ref, first):
     c = src_ref.shape[-1]
     wide = src_ref.shape[1]
@@ -194,30 +203,123 @@
     return out
 
 
+def own_row_pair(src_ref, w_ref, base, first):
+    c = src_ref.shape[-1]
+    wide = src_ref.shape[1]
+    width = base.shape[0]
+    lhs = jnp.concatenate([src_ref[first + k] for k in range(4)], axis=1)
+    y = jnp.dot(lhs, w_ref[...], preferred_element_type=F32)
+    y = pltpu.roll(y[:, 0:c], 1, 0) + y[:, c : 2 * c] + pltpu.roll(y[:, 2 * c : 3 * c], wide - 1, 0)
+    out = base - guide_rate * y[0:width, :]
+    return [out[at : at + 128, :].T for at in range(0, width, 128)]
+
+
 def inside(ext_row, ext_rows):
     at = lax.axis_index("lat")
     last = lax.axis_size("lat") - 1
     return ((ext_row > 0) | (at > 0)) & ((ext_row < ext_rows - 1) | (at < last))
 
 
-def own_pair(first, second):
+def activate(y, bias):
+    pre = y + bias
+    s = 1.0 / (1.0 + jnp.exp(-pre))
+    return pre * s, s * (1.0 + pre * (1.0 - s))
+
+
+def copy_row(target_ref, at, x_ref, tail_ref, row):
+    width = x_ref.shape[1]
+    target_ref[at, 0:width, :] = x_ref[row]
+    target_ref[at, width : width + TAIL, :] = tail_ref[row]
+
+
+def fill_end(ext_ref, end, x_ref, tail_ref, halo_ref):
+    rows = x_ref.shape[0]
+    for i in range(2):
+        ext_ref[2 * end + i] = halo_ref[i]
+        copy_row(ext_ref, 2 * (1 - end) + i, x_ref, tail_ref, (rows - 2) * end + i)
+
+
+def fill_between(between_ref, end, new, kept_ref):
+    for i in range(2):
+        between_ref[2 * end + i] = new[i]
+        between_ref[2 * (1 - end) + i] = kept_ref[2 * end + i]
+
+
+def forward_middle_kernel(
+    x_ref,
+    tail_ref,
+    kin_ref,
+    kout_ref,
+    bias_ref,
+    slope_hbm,
+    kept_ref,
+    den_ref,
+    ext_ref,
+    hidden_ref,
+    w1_ref,
+    w2_ref,
+    slope_ref,
+    save_sem,
+):
+    rows, width, _ = x_ref.shape
+    forward_taps(w1_ref, w2_ref, kin_ref, kout_ref)
+    for h in range(rows):
+        copy_row(ext_ref, h, x_ref, tail_ref, h)
+    bias = bias_ref[...]
+    for g in range((rows - 2) // 2):
+        for i, y in enumerate(row_pair(ext_ref, w1_ref, 2 * g)):
+            hidden, slope = activate(y, bias)
+            slope_ref[2 * g + i] = slope
+            hidden_ref[2 * g + i] = hidden.astype(BF16)
+    save = pltpu.make_async_copy(slope_ref, slope_hbm, save_sem)
+    save.start()
+    for i in range(2):
+        kept_ref[i] = hidden_ref[i]
+        kept_ref[2 + i] = hidden_ref[rows - 4 + i]
+    for g in range((rows - 4) // 2):
+        for i, y in enumerate(row_pair(hidden_ref, w2_ref, 2 * g)):
+            den_ref[2 * g + i] = (x_ref[2 + 2 * g + i].astype(F32) + y[0:width, :]).astype(BF16)
+    save.wait()
+
+
+def forward_end(end, x_ref, tail_ref, halo_ref, kept_ref, w1_ref, w2_ref, bias_ref, slope_ref, ext_ref, between_ref):
+    rows, width, _ = x_ref.shape
+    fill_end(ext_ref, end, x_ref, tail_ref, halo_ref)
+    bias = bias_ref[...]
+    new = []
+    for i, y in enumerate(row_pair(ext_ref, w1_ref, 0)):
+        hidden, slope = activate(y, bias)
+        slope_ref[i] = slope
+        new.append(jnp.where(inside(rows * end + i, rows + 2), hidden, 0.0).astype(BF16))
+    fill_between(between_ref, end, new, kept_ref)
+    return [
+        (x_ref[(rows - 2) * end + i].astype(F32) + y[0:width, :]).astype(BF16)
+        for i, y in enumerate(row_pair(between_ref, w2_ref, 0))
+    ]
+
+
+def forward_own_kernel(
+    x_ref, tail_ref, halo_ref, kept_ref, kin_ref, kout_ref, bias_ref, slope_ref, den_ref, w1_ref, w2_ref, ext_ref, between_ref
+):
+    forward_taps(w1_ref, w2_ref, kin_ref, kout_ref)
     core = lax.axis_index("ch")
-    half = first.shape[-1] // 2
-    lane = lax.broadcasted_iota(jnp.int32, first.shape, len(first.shape) - 1)
-    stays = jnp.where(core == 0, first, second)
-    moves = pltpu.roll(jnp.where(core == 0, second, first), half, len(first.shape) - 1)
-    low = (lane < half).astype(jnp.int32)
-    return jnp.where(low == 1 - core, stays, moves)
+    den = forward_end(
+        core, x_ref, tail_ref, halo_ref, kept_ref, w1_ref, w2_ref, bias_ref, slope_ref, ext_ref, between_ref
+    )
+    for i in range(2):
+        den_ref[i] = den[i]
 
 
 def forward_kernel(
     x_ref,
     tail_ref,
-    mine_ref,
-    other_ref,
+    halo_ref,
+    kept_ref,
     w1_ref,
     w2_ref,
     bias_ref,
+    den_middle_ref,
+    den_own_ref,
     block_ref,
     other_block_ref,
     slope_ref,
@@ -226,7 +328,7 @@
     gtail_ref,
     inn_ref,
     ext_ref,
-    hidden_ref,
+    between_ref,
     den_ref,
     field_ref,
     turned_ref,
@@ -238,7 +340,6 @@
     rows, width, c = x_ref.shape
     half = inn_ref.shape[1]
     sources, obs = block_ref.shape[0], block_ref.shape[2]
-    fill_extended(ext_ref, x_ref, tail_ref, mine_ref, other_ref)
 
     def read(source, cap, first, count):
         at = slice(first, first + count)
@@ -259,37 +360,33 @@
         row = read(source, cap, obs + c, META).astype(F32)[0:1, :]
         scale_ref[slot] = jnp.broadcast_to(row, (c, obs)).T
 
-    def each(task, first, last):
-        if last - first <= 8:
-            for source in range(first, last):
+    def each(task):
+        if sources <= 4:
+            for source in range(sources):
                 for cap in range(CAP):
                     task(source, cap)
             return
 
-        def step(source, _):
+        def one(source, _):
             for cap in range(CAP):
                 task(source, cap)
             return 0
 
-        lax.fori_loop(first, last, step, 0)
-
-    each(locate, 0, sources)
-    bias = bias_ref[...]
-    for g in range((rows + 2) // 2):
-        for i, y in enumerate(row_pair(ext_ref, w1_ref, 2 * g)):
-            r = 2 * g + i
-            pre = y + bias
-            s = 1.0 / (1.0 + jnp.exp(-pre))
-            slope_ref[r] = s * (1.0 + pre * (1.0 - s))
-            hidden_ref[r] = jnp.where(inside(r, rows + 2), pre * s, 0.0).astype(BF16)
-    groups = rows // 2
-    for g in range(groups):
-        each(turn, sources * g // groups, sources * (g + 1) // groups)
-        for i, y in enumerate(row_pair(hidden_ref, w2_ref, 2 * g)):
-            r = 2 * g + i
-            noisy = x_ref[r].astype(F32)
-            den_ref[r] = (noisy + y[0:width, :]).astype(BF16).astype(F32)
-            field_ref[r] = jnp.zeros((width, c), F32)
+        lax.fori_loop(0, sources, one, 0)
+
+    each(locate)
+    each(turn)
+    end = 1 - core
+    den = forward_end(
+        end, x_ref, tail_ref, halo_ref, kept_ref, w1_ref, w2_ref, bias_ref, slope_ref, ext_ref, between_ref
+    )
+    for i in range(2):
+        den_ref[(rows - 2) * end + i] = den[i].astype(F32)
+        den_ref[(rows - 2) * core + i] = den_own_ref[i].astype(F32)
+    for h in range(rows - 4):
+        den_ref[2 + h] = den_middle_ref[h].astype(F32)
+    for r in range(rows):
+        field_ref[r] = jnp.zeros((width, c), F32)
 
     def observe(source, cap):
         slot = source * CAP + cap
@@ -306,34 +403,97 @@
         turned = residual.astype(BF16).T
         inn_ref[slot] = jnp.where(core == 0, turned[0:half], turned[half : 2 * half])
 
-    each(observe, 0, sources)
-
-    for g in range(groups):
+    each(observe)
+
+    for g in range(rows // 2):
         base = []
         for r in (2 * g, 2 * g + 1):
             field = field_ref[r]
-            noisy = ext_ref[r + 2, 0:width, :].astype(F32)
-            base.append(keep_rate * noisy + blend_rate * den_ref[r] - guide_rate * field)
+            base.append(keep_rate * x_ref[r].astype(F32) + blend_rate * den_ref[r] - guide_rate * field)
             g_ref[r] = field.astype(BF16)
         base_ref[g] = own_pair(*base)
     write_tails(g_ref, gtail_ref)
 
 
+def backward_middle_kernel(
+    x_ref,
+    tail_ref,
+    kin_ref,
+    kout_ref,
+    base_ref,
+    slope_hbm,
+    kept_ref,
+    out_ref,
+    ext_ref,
+    grad_ref,
+    w3_ref,
+    w4_ref,
+    slope_ref,
+    load_sems,
+):
+    rows = x_ref.shape[0]
+
+    def load(g):
+        at = pl.ds(2 * g, 2)
+        return pltpu.make_async_copy(slope_hbm.at[at], slope_ref.at[at], load_sems.at[g])
+
+    for g in range((rows - 2) // 2):
+        load(g).start()
+    backward_taps(w3_ref, w4_ref, kin_ref, kout_ref)
+    for h in range(rows):
+        copy_row(ext_ref, h, x_ref, tail_ref, h)
+    for g in range((rows - 2) // 2):
+        pair = row_pair(ext_ref, w3_ref, 2 * g)
+        load(g).wait()
+        for i, y in enumerate(pair):
+            grad_ref[2 * g + i] = (y * slope_ref[2 * g + i]).astype(BF16)
+    for i in range(2):
+        kept_ref[i] = grad_ref[i]
+        kept_ref[2 + i] = grad_ref[rows - 4 + i]
+    for g in range((rows - 4) // 2):
+        for part, plane in enumerate(own_row_pair(grad_ref, w4_ref, base_ref[1 + g], 2 * g)):
+            out_ref[g, part] = plane
+
+
+def backward_end(end, x_ref, tail_ref, halo_ref, kept_ref, w3_ref, w4_ref, base_ref, slope_ref, ext_ref, between_ref):
+    rows = x_ref.shape[0]
+    fill_end(ext_ref, end, x_ref, tail_ref, halo_ref)
+    new = [
+        jnp.where(inside(rows * end + i, rows + 2), y * slope_ref[i], 0.0).astype(BF16)
+        for i, y in enumerate(row_pair(ext_ref, w3_ref, 0))
+    ]
+    fill_between(between_ref, end, new, kept_ref)
+    return own_row_pair(between_ref, w4_ref, base_ref[(rows // 2 - 1) * end], 0)
+
+
+def backward_own_kernel(
+    x_ref, tail_ref, halo_ref, kept_ref, kin_ref, kout_ref, base_ref, slope_ref, out_ref, ext_ref, between_ref, w3_ref, w4_ref
+):
+    backward_taps(w3_ref, w4_ref, kin_ref, kout_ref)
+    planes = backward_end(
+        lax.axis_index("ch"), x_ref, tail_ref, halo_ref, kept_ref, w3_ref, w4_ref, base_ref, slope_ref, ext_ref, between_ref
+    )
+    for part, plane in enumerate(planes):
+        out_ref[part] = plane
+
+
 def backward_kernel(
     x_ref,
     tail_ref,
-    mine_ref,
-    other_ref,
+    halo_ref,
+    kept_ref,
     kin_ref,
     kout_ref,
     base_ref,
     slope_ref,
+    out_middle_ref,
+    out_own_ref,
     back_ref,
     dest_hbm,
     next_ref,
     inn_hbm,
     ext_ref,
-    grad_ref,
+    between_ref,
     flat_ref,
     w3_ref,
     w4_ref,
@@ -343,31 +503,30 @@
 ):
     dest_copy = pltpu.make_async_copy(dest_hbm, dest_ref, dest_sem)
     dest_copy.start()
-    rows, width, c = x_ref.shape
-    wide = ext_ref.shape[1]
+    core = lax.axis_index("ch")
+    rows = x_ref.shape[0]
     half = next_ref.shape[0]
-    fill_extended(ext_ref, x_ref, tail_ref, mine_ref, other_ref)
-    place_taps(w3_ref, lambda a, b: kout_ref[2 - a, 2 - b])
-    zero = jnp.zeros((c, c), F32)
-    for b in range(3):
-        taps = [zero] + [kin_ref[2 - a, 2 - b].astype(F32) for a in range(3)] + [zero]
-        for k in range(4):
-            w4_ref[k * c : (k + 1) * c, b * c : (b + 1) * c] = own_pair(taps[k + 1], taps[k]).astype(BF16)
-
-    for g in range((rows + 2) // 2):
-        for i, y in enumerate(row_pair(ext_ref, w3_ref, 2 * g)):
-            r = 2 * g + i
-            grad_ref[r] = jnp.where(inside(r, rows + 2), y * slope_ref[r], 0.0).astype(BF16)
-
+    parts = flat_ref.shape[0]
+
+    def put(pair, part, plane):
+        for i in range(2):
+            flat_ref[part, pl.ds(2 * pair + i, half, stride=rows), :] = plane[i * half : (i + 1) * half]
+
+    backward_taps(w3_ref, w4_ref, kin_ref, kout_ref)
+    planes = backward_end(
+        1 - core, x_ref, tail_ref, halo_ref, kept_ref, w3_ref, w4_ref, base_ref, slope_ref, ext_ref, between_ref
+    )
+    for part in range(parts):
+        for g in range((rows - 4) // 2):
+            put(1 + g, part, out_middle_ref[g, part])
+        put((rows // 2 - 1) * core, part, out_own_ref[part])
+        put((rows // 2 - 1) * (1 - core), part, planes[part])
     dest_copy.wait()
 
-    def give(b):
+    def start(b, _):
         dest = dest_ref[b]
         rank = lax.fori_loop(0, b, lambda j, n: n + (dest_ref[j] == dest).astype(jnp.int32), 0)
-        return pltpu.make_async_copy(back_ref.at[dest * CAP + rank], inn_hbm.at[b], inn_sems.at[b])
-
-    def start(b, _):
-        give(b).start()
+        pltpu.make_async_copy(back_ref.at[dest * CAP + rank], inn_hbm.at[b], inn_sems.at[b]).start()
         return 0
 
     def finish(b, _):
@@ -375,16 +534,7 @@
         return 0
 
     lax.fori_loop(0, inn_hbm.shape[0], start, 0)
-    for g in range(rows // 2):
-        lhs = jnp.concatenate([grad_ref[2 * g + k] for k in range(4)], axis=1)
-        y = jnp.dot(lhs, w4_ref[...], preferred_element_type=F32)
-        y = pltpu.roll(y[:, 0:c], 1, 0) + y[:, c : 2 * c] + pltpu.roll(y[:, 2 * c : 3 * c], wide - 1, 0)
-        out = base_ref[g] - guide_rate * y[0:width, :]
-        for part in range(width // 128):
-            plane = out[part * 128 : (part + 1) * 128, :].T
-            for i in range(2):
-                flat_ref[part, pl.ds(2 * g + i, half, stride=rows), :] = plane[i * half : (i + 1) * half]
-    for part in range(width // 128):
+    for part in range(parts):
         next_ref[:, :, part * 128 : (part + 1) * 128] = flat_ref[part].reshape(half, rows, 128)
     lax.fori_loop(0, inn_hbm.shape[0], finish, 0)
 
@@ -404,20 +554,23 @@
 
 def from_lon_neighbours(value):
     lons = lax.axis_size("lon")
-    move = lambda step: lax.ppermute(value, "lon", [(j, (j + step) % lons) for j in range(lons)])
+
+    def move(step):
+        pairs = [(j * 2 + core, (j + step) % lons * 2 + 1 - core) for j in range(lons) for core in range(2)]
+        return lax.ppermute(value, ("lon", "ch"), pairs)
+
     if lons == 2:
         return move(1)
     at = lax.broadcasted_iota(jnp.int32, (1, TAIL, 1), 1)
     return jnp.where(at < TAIL // 2, move(-1), move(1))
 
 
-def exchanged(x, tail, along):
+def exchanged(x, tail):
     _, width, c = x.shape
     beside = from_lon_neighbours(tail)
     (edge,) = call(edge_kernel, [(shape((2, width + TAIL, c), BF16), VMEM)], [VMEM] * 2, [])(x, beside)
     mine = from_row_neighbour(edge)
-    mine, along = lax.optimization_barrier((mine, along))
-    return (beside, mine, swapped(mine)), along
+    return beside, mine
 
 
 def shape(dims, dtype):
@@ -467,21 +620,43 @@
         [VMEM] * 2,
         [VMEM((width // 128, c * rows, 128), F32)],
     )(near, other)
-    w1, w2 = call(weights_kernel, [(shape((4 * c, 6 * c), BF16), VMEM)] * 2, [VMEM] * 2, [])(kernel_in, kernel_out)
-    halo, block = exchanged(x, tail, block)
-    slope, base, g, tail, inn = call(
+    bias = bias_in.reshape(1, c)
+    pair = shape((2, wide, c), F32)
+    taps = shape((4 * c, 6 * c), BF16)
+    own_taps = shape((4 * c, 3 * c), BF16)
+    kept_shape = shape((4, wide, c), BF16)
+    four_rows, most_rows, all_rows = VMEM((4, wide, c), BF16), VMEM((rows - 2, wide, c), BF16), VMEM((rows, wide, c), BF16)
+    most_slopes = VMEM((rows - 2, wide, c), F32)
+    keep = lambda dims, dtype: VMEM(dims.shape, dtype)
+
+    beside, mine = exchanged(x, tail)
+    slope_middle, kept, den_middle = call(
+        forward_middle_kernel,
+        [(shape((rows - 2, wide, c), F32), HBM), (kept_shape, VMEM), (shape((rows - 4, width, c), BF16), VMEM)],
+        [VMEM] * 5,
+        [all_rows, most_rows, keep(taps, BF16), keep(taps, BF16), most_slopes, pltpu.SemaphoreType.DMA],
+    )(x, beside, kernel_in, kernel_out, bias)
+    mine, block, kept, slope_middle, den_middle = lax.optimization_barrier((mine, block, kept, slope_middle, den_middle))
+    others = swapped(mine)
+    slope_own, den_own, w1, w2 = call(
+        forward_own_kernel,
+        [(pair, VMEM), (shape((2, width, c), BF16), VMEM), (taps, VMEM), (taps, VMEM)],
+        [VMEM] * 7,
+        [four_rows, four_rows],
+    )(x, beside, mine, kept, kernel_in, kernel_out, bias)
+    slope_other, base, g, tail, inn = call(
         forward_kernel,
         [
-            (shape((rows + 2, wide, c), F32), VMEM),
+            (pair, VMEM),
             (shape((rows // 2, width, c), F32), VMEM),
             (shape((rows, width, c), BF16), VMEM),
             (tail_shape, VMEM),
             (shape((slots, half, obs), BF16), VMEM),
         ],
-        [VMEM] * 9,
+        [VMEM] * 11,
         [
-            VMEM((rows + 4, wide, c), BF16),
-            VMEM((rows + 2, wide, c), BF16),
+            four_rows,
+            four_rows,
             VMEM((rows, width, c), F32),
             VMEM((rows, width, c), F32),
             VMEM((slots, obs, obs), BF16),
@@ -490,24 +665,47 @@
             SMEM((slots,), jnp.int32),
         ],
         {0: 2, 1: 3},
-    )(x, *halo, w1, w2, bias_in.reshape(1, c), block, swapped(block))
-    halo, _ = exchanged(g, tail, ())
+    )(x, beside, others, kept, w1, w2, bias, den_middle, den_own, block, swapped(block))
+
     back = lax.all_to_all(inn, "lat", split_axis=0, concat_axis=0, tiled=True)
+    beside, mine = exchanged(g, tail)
+    parts = width // 128
+    kept, out_middle = call(
+        backward_middle_kernel,
+        [(kept_shape, VMEM), (shape(((rows - 4) // 2, parts, c, 128), F32), VMEM)],
+        [VMEM] * 5 + [HBM],
+        [
+            all_rows,
+            most_rows,
+            keep(taps, BF16),
+            keep(own_taps, BF16),
+            most_slopes,
+            pltpu.SemaphoreType.DMA(((rows - 2) // 2,)),
+        ],
+    )(g, beside, kernel_in, kernel_out, base, slope_middle)
+    mine, kept, out_middle = lax.optimization_barrier((mine, kept, out_middle))
+    others = swapped(mine)
+    (out_own,) = call(
+        backward_own_kernel,
+        [(shape((parts, c, 128), F32), VMEM)],
+        [VMEM] * 8,
+        [four_rows, four_rows, keep(taps, BF16), keep(own_taps, BF16)],
+    )(g, beside, mine, kept, kernel_in, kernel_out, base, slope_own)
     next_state, innovation = call(
         backward_kernel,
         [(shape((half, rows, width), F32), OUT), (shape(observed.shape, BF16), HBM)],
-        [VMEM] * 9 + [HBM],
+        [VMEM] * 11 + [HBM],
         [
-            VMEM((rows + 4, wide, c), BF16),
-            VMEM((rows + 2, wide, c), BF16),
-            VMEM((width // 128, half * rows, 128), F32),
-            VMEM((4 * c, 6 * c), BF16),
-            VMEM((4 * c, 3 * c), BF16),
+            four_rows,
+            four_rows,
+            VMEM((parts, half * rows, 128), F32),
+            keep(taps, BF16),
+            keep(own_taps, BF16),
             SMEM((blocks,), jnp.int32),
             pltpu.SemaphoreType.DMA,
             pltpu.SemaphoreType.DMA((blocks,)),
         ],
-    )(g, *halo, kernel_in, kernel_out, base, slope, back, dest_tile)
+    )(g, beside, others, kept, kernel_in, kernel_out, base, slope_other, out_middle, out_own, back, dest_tile)
     return next_state, innovation
 
 

time: 46.5 us -> 43.5 us (0.935)
  waiting for transfers between devices: 16.9 us -> 9.64 us
  Pallas kernels: 9.6 us -> 14 us
    pallas_call x7 -> x10, Pallas kernels: 9.6 us -> 14 us  [apply(): run(*(pltpu.with_memory_space_constraint(a, space) if space in (VMEM, HBM...]
    all_to_all x1, waiting for transfers between devices: 6.09 us -> 2.46 us  [body(): back = lax.all_to_all(inn, 'lat', split_axis=0, concat_axis=0, tiled=True)]
    all_to_all x1, waiting for transfers between devices: 4.83 us -> 2.96 us  [body(): lax.all_to_all(chunk, 'lat', split_axis=0, concat_axis=0, tiled=True)]
    ppermute x2, waiting for transfers between devices: 4.87 us -> 3.92 us  [move(): return lax.ppermute(value, ('lon', 'ch'), pairs)]
    ppermute x4, waiting for transfers between devices: 1.1 us -> 0.3 us  [swapped(): return lax.ppermute(value, 'ch', [(0, 1), (1, 0)])]
  transfers between devices with their start and end apart: 10 -> 10, of which waited for: 5 -> 5; matrix products, arithmetic and copies ran while one was open for 0% -> 0% of each run, Pallas kernels for 5% -> 21%
where the time goes in v1:
time: 43.5 us; the launch traced here: 43.1 us
  starting transfers between devices  18.5 us (43%)
  Pallas kernels  14 us (32%)
  waiting for transfers between devices  9.64 us (22%)
  between operations  0.72 us (2%)
    pallas_call x10, Pallas kernels, apply(): run(*(pltpu.with_memory_space_constraint(a, space) if space in (VMEM, HBM...  14 us
    all_to_all x1, starting transfers between devices, body(): back = lax.all_to_all(inn, 'lat', split_axis=0, concat_axis=0, tiled=True)  6.4 us
    all_to_all x1, starting transfers between devices, body(): lax.all_to_all(chunk, 'lat', split_axis=0, concat_axis=0, tiled=True)  5.88 us
    ppermute x2, waiting for transfers between devices, move(): return lax.ppermute(value, ('lon', 'ch'), pairs)  3.92 us
    all_to_all x1, waiting for transfers between devices, body(): lax.all_to_all(chunk, 'lat', split_axis=0, concat_axis=0, tiled=True)  2.96 us
    ppermute x2, starting transfers between devices, move(): return lax.ppermute(value, ('lon', 'ch'), pairs)  2.83 us
    all_to_all x1, waiting for transfers between devices, body(): back = lax.all_to_all(inn, 'lat', split_axis=0, concat_axis=0, tiled=True)  2.46 us
    ppermute x4, starting transfers between devices, swapped(): return lax.ppermute(value, 'ch', [(0, 1), (1, 0)])  1.96 us
  transfers between devices with their start and end apart: 10, of which 5 were waited for; matrix products, arithmetic and copies ran while one was open for 0% of the time, Pallas kernels for 21%

profile of v1, /device:TPU:0, one launch (start us, length us, event | category | flops | bytes accessed | tf_op | source)
XLA Modules:
  0.0 43.1 jit_solution(11546456752330899203)
XLA Ops:
  0.6 0.6 %collective-permute-start = (bf16[64,8,256]{2,1,0:T(8,128)(2,1)}, bf16[64,8,256]{2,1,0:T(8,128)(2,1)S(1)}, u32[]{:S(2)}, u32[]{:S(2)}) collective-permute-start(bf16[64,8,256]{2,1,0:T(8,128)(2,1)} %noisy_hbm.1), channel_id=1, source_target_pairs={{0,1},{1,0},{2,3},{3,2},{4,5},{5,4},{6,7},{7,6},{8,9},{9,8},{10,11... | collective-permute-start | bytes 786440 | tf_op jit(solution)/shard_map/ppermute | solution.py:543
  1.2 1.8 %shard_map.113 = (bf16[4,272,128]{2,1,0:T(8,128)(2,1)}, bf16[64,8,256]{2,1,0:T(8,128)(2,1)S(1)}) custom-call(s32[4]{0:T(128)} %dest_hbm.3, s32[4]{0:T(128)} %row_hbm.1, s32[4]{0:T(128)} %col_hbm.1, bf16[4,128,128]{2,1,0:T(8,128)(2,1)} %weight_hbm.1, bf16[4,64,128]{2,1,0:T(8,128)(2,1)} %obs_hbm.1, bf16[4,128]{1,0:T(4,128)(2,1)} %precision_hbm.1, ...), custom_call_target="tpu_custom_call" | custom-call | tf_op jit(solution)/shard_map/pallas_call | solution.py:41
  3.0 5.9 %all-to-all-start = ((bf16[4,272,128]{2,1,0:T(8,128)(2,1)}), bf16[4,272,128]{2,1,0:T(8,128)(2,1)S(1)}, u32[]{:S(2)}, u32[]{:S(2)}) async-start(bf16[4,272,128]{2,1,0:T(8,128)(2,1)} %get-tuple-element.31), calls=%async_computation | async-start | bytes 557056 | tf_op jit(solution)/shard_map/all_to_all | solution.py:615
  8.9 0.0 collective-permute-done.other_ref
  8.9 0.3 shard_map.114
  9.2 1.4 %collective-permute-start.1 = (bf16[8,16,128]{2,1,0:T(8,128)(2,1)S(1)}, bf16[8,16,128]{2,1,0:T(8,128)(2,1)S(1)}, u32[]{:S(2)}, u32[]{:S(2)}) collective-permute-start(bf16[8,16,128]{2,1,0:T(8,128)(2,1)S(1)} %get-tuple-element.30), channel_id=1, source_target_pairs={{0,3},{1,2},{2,1},{3,0},{4,7},{5,6},{6,5},{7,4},{8,11},{9,10},{10,... | collective-permute-start | bytes 98312 | tf_op jit(solution)/shard_map/ppermute | solution.py:560
  10.6 2.0 %collective-permute-done.1.tail_ref = bf16[8,16,128]{2,1,0:T(8,128)(2,1)S(1)} collective-permute-done((bf16[8,16,128]{2,1,0:T(8,128)(2,1)S(1)}, bf16[8,16,128]{2,1,0:T(8,128)(2,1)S(1)}, u32[]{:S(2)}, u32[]{:S(2)}) %collective-permute-start.1) | collective-permute-done | bytes 32800 | tf_op jit(solution)/shard_map/ppermute | solution.py:560
  12.7 0.0 copy-start
  12.7 0.0 copy-start.1
  12.7 0.0 copy-start.2
  12.7 0.8 %collective-permute-start.2 = (bf16[2,272,128]{2,1,0:T(8,128)(2,1)S(1)}, bf16[2,272,128]{2,1,0:T(8,128)(2,1)S(1)}, u32[]{:S(2)}, u32[]{:S(2)}) collective-permute-start(bf16[2,272,128]{2,1,0:T(8,128)(2,1)S(1)} %shard_map.115), channel_id=1, source_target_pairs={{1,4},{4,1},{5,8},{8,5},{9,12},{12,9},{3,6},{6,3},{7,10},{10,7},{1... | collective-permute-start | bytes 417800 | tf_op jit(solution)/shard_map/ppermute | solution.py:552
  13.5 0.1 copy-done
  13.6 0.1 copy-done.1
  13.7 0.0 copy-done.2
  13.7 2.2 %shard_map.116 = (f32[6,272,128]{2,1,0:T(8,128)}, bf16[4,272,128]{2,1,0:T(8,128)(2,1)S(1)}, bf16[4,256,128]{2,1,0:T(8,128)(2,1)S(1)}) custom-call(bf16[8,256,128]{2,1,0:T(8,128)(2,1)S(1)} %get-tuple-element.29.x_ref, bf16[8,16,128]{2,1,0:T(8,128)(2,1)S(1)} %collective-permute-done.1.tail_ref, bf16[3,3,128,128]{3,2,1,0:T(8,128)(2,1)S(1)} %copy-done, ...), custom_call_target="tpu_custom_call" | custom-call | tf_op jit(solution)/shard_map/pallas_call | solution.py:41
  15.9 3.0 %all-to-all-done.block_ref = bf16[4,272,128]{2,1,0:T(8,128)(2,1)S(1)} async-done(((bf16[4,272,128]{2,1,0:T(8,128)(2,1)}), bf16[4,272,128]{2,1,0:T(8,128)(2,1)S(1)}, u32[]{:S(2)}, u32[]{:S(2)}) %all-to-all-start) | async-done | bytes 278560 | tf_op jit(solution)/shard_map/all_to_all | solution.py:615
  18.8 0.0 collective-permute-done.2.halo_ref
  18.8 1.3 %collective-permute-start.4 = (bf16[4,272,128]{2,1,0:T(8,128)(2,1)S(1)}, bf16[4,272,128]{2,1,0:T(8,128)(2,1)S(1)}, u32[]{:S(2)}, u32[]{:S(2)}) collective-permute-start(bf16[4,272,128]{2,1,0:T(8,128)(2,1)S(1)} %all-to-all-done.block_ref), channel_id=1, source_target_pairs={{0,1},{1,0},{2,3},{3,2},{4,5},{5,4},{6,7},{7,6},{8,9},{9,8},{10,11... | collective-permute-start | bytes 835592 | tf_op jit(solution)/shard_map/ppermute | solution.py:543
  20.1 0.0 collective-permute-start.3
  20.1 1.1 %shard_map.117 = (f32[2,272,128]{2,1,0:T(8,128)S(1)}, bf16[2,256,128]{2,1,0:T(8,128)(2,1)S(1)}, bf16[512,768]{1,0:T(8,128)(2,1)S(1)}, bf16[512,768]{1,0:T(8,128)(2,1)S(1)}) custom-call(bf16[8,256,128]{2,1,0:T(8,128)(2,1)S(1)} %get-tuple-element.29.x_ref, bf16[8,16,128]{2,1,0:T(8,128)(2,1)S(1)} %collective-permute-done.1.tail_ref, ...), custom_call_target="tpu_custom_call" | custom-call | tf_op jit(solution)/shard_map/pallas_call | solution.py:41
  21.2 0.3 collective-permute-done.3.halo_ref
  21.5 0.0 collective-permute-done.4.other_block_ref
  21.5 2.3 %shard_map.118 = (f32[2,272,128]{2,1,0:T(8,128)S(1)}, f32[4,256,128]{2,1,0:T(8,128)S(1)}, bf16[8,256,128]{2,1,0:T(8,128)(2,1)S(1)}, bf16[8,16,128]{2,1,0:T(8,128)(2,1)S(1)}, bf16[8,64,128]{2,1,0:T(8,128)(2,1)}) custom-call(bf16[8,256,128]{2,1,0:T(8,128)(2,1)S(1)} %get-tuple-element.29.x_ref, ...), custom_call_target="tpu_custom_call", output_to_operand_aliasing={{2}: (0, {}), {3}: (1, {})} | custom-call | tf_op jit(solution)/shard_map/pallas_call | solution.py:41
  23.8 1.5 %collective-permute-start.5 = (bf16[8,16,128]{2,1,0:T(8,128)(2,1)S(1)}, bf16[8,16,128]{2,1,0:T(8,128)(2,1)S(1)}, u32[]{:S(2)}, u32[]{:S(2)}) collective-permute-start(bf16[8,16,128]{2,1,0:T(8,128)(2,1)S(1)} %get-tuple-element.43), channel_id=1, source_target_pairs={{0,3},{1,2},{2,1},{3,0},{4,7},{5,6},{6,5},{7,4},{8,11},{9,10},{10,... | collective-permute-start | bytes 98312 | tf_op jit(solution)/shard_map/ppermute | solution.py:560
  25.3 1.9 %collective-permute-done.5.tail_ref = bf16[8,16,128]{2,1,0:T(8,128)(2,1)S(1)} collective-permute-done((bf16[8,16,128]{2,1,0:T(8,128)(2,1)S(1)}, bf16[8,16,128]{2,1,0:T(8,128)(2,1)S(1)}, u32[]{:S(2)}, u32[]{:S(2)}) %collective-permute-start.5) | collective-permute-done | bytes 32800 | tf_op jit(solution)/shard_map/ppermute | solution.py:560
  27.2 0.7 %collective-permute-start.6 = (bf16[2,272,128]{2,1,0:T(8,128)(2,1)S(1)}, bf16[2,272,128]{2,1,0:T(8,128)(2,1)S(1)}, u32[]{:S(2)}, u32[]{:S(2)}) collective-permute-start(bf16[2,272,128]{2,1,0:T(8,128)(2,1)S(1)} %shard_map.119), channel_id=1, source_target_pairs={{1,4},{4,1},{5,8},{8,5},{9,12},{12,9},{3,6},{6,3},{7,10},{10,7},{1... | collective-permute-start | bytes 417800 | tf_op jit(solution)/shard_map/ppermute | solution.py:552
  27.8 6.4 %all-to-all-start.1 = ((bf16[8,64,128]{2,1,0:T(8,128)(2,1)}), bf16[8,64,128]{2,1,0:T(8,128)(2,1)S(1)}, u32[]{:S(2)}, u32[]{:S(2)}) async-start(bf16[8,64,128]{2,1,0:T(8,128)(2,1)} %get-tuple-element.53), calls=%async_computation.1 | async-start | bytes 262144 | tf_op jit(solution)/shard_map/all_to_all | solution.py:670
  34.2 2.9 %shard_map.120 = (bf16[4,272,128]{2,1,0:T(8,128)(2,1)S(1)}, f32[2,2,128,128]{3,2,1,0:T(8,128)S(1)}) custom-call(bf16[8,256,128]{2,1,0:T(8,128)(2,1)S(1)} %get-tuple-element.42.x_ref, bf16[8,16,128]{2,1,0:T(8,128)(2,1)S(1)} %collective-permute-done.5.tail_ref, bf16[3,3,128,128]{3,2,1,0:T(8,128)(2,1)S(1)} %copy-done, bf16[3,3,128,128]{3,2,1,0:T(8,128)(2,1)S(1)} %copy-done.1, ...), custom_call_target="tpu_custom_call" | custom-call | tf_op jit(solution)/shard_map/pallas_call | solution.py:41
  37.2 0.0 collective-permute-done.6.halo_ref
  37.2 0.1 collective-permute-start.7
  37.3 0.9 %shard_map.121.out_own_ref = f32[2,128,128]{2,1,0:T(8,128)S(1)} custom-call(bf16[8,256,128]{2,1,0:T(8,128)(2,1)S(1)} %get-tuple-element.42.x_ref, bf16[8,16,128]{2,1,0:T(8,128)(2,1)S(1)} %collective-permute-done.5.tail_ref, bf16[2,272,128]{2,1,0:T(8,128)(2,1)S(1)} %collective-permute-done.6.halo_ref, bf16[4,272,128]{2,1,0:T(8,128)(2,1)S(1)} %get-tuple-element.49.kept_ref, ...), custom_call_target="tpu_custom_call" | custom-call | tf_op jit(solution)/shard_map/pallas_call | solution.py:41
  38.2 2.5 %all-to-all-done.1.back_ref = bf16[8,64,128]{2,1,0:T(8,128)(2,1)S(1)} async-done(((bf16[8,64,128]{2,1,0:T(8,128)(2,1)}), bf16[8,64,128]{2,1,0:T(8,128)(2,1)S(1)}, u32[]{:S(2)}, u32[]{:S(2)}) %all-to-all-start.1) | async-done | bytes 131104 | tf_op jit(solution)/shard_map/all_to_all | solution.py:670
  40.7 0.0 collective-permute-done.7.halo_ref
  40.7 2.4 %shard_map.122 = (f32[64,8,256]{2,1,0:T(8,128)}, bf16[4,64,128]{2,1,0:T(8,128)(2,1)}) custom-call(bf16[8,256,128]{2,1,0:T(8,128)(2,1)S(1)} %get-tuple-element.42.x_ref, bf16[8,16,128]{2,1,0:T(8,128)(2,1)S(1)} %collective-permute-done.5.tail_ref, bf16[2,272,128]{2,1,0:T(8,128)(2,1)S(1)} %collective-permute-done.7.halo_ref, ...), custom_call_target="tpu_custom_call" | custom-call | tf_op jit(solution)/shard_map/pallas_call | solution.py:41
  (2 shorter events, 0.0 us)
Async XLA Ops:
  0.6 8.3 %collective-permute-start = (bf16[64,8,256]{2,1,0:T(8,128)(2,1)}, bf16[64,8,256]{2,1,0:T(8,128)(2,1)S(1)}, u32[]{:S(2)}, u32[]{:S(2)}) collective-permute-start(bf16[64,8,256]{2,1,0:T(8,128)(2,1)} %noisy_hbm.1), channel_id=1, source_target_pairs={{0,1},{1,0},{2,3},{3,2},{4,5},{5,4},{6,7},{7,6},{8,9},{9,8},{10,11... | collective-permute-start | bytes 786440 | tf_op jit(solution)/shard_map/ppermute | solution.py:543
  3.0 15.8 %all-to-all-start = ((bf16[4,272,128]{2,1,0:T(8,128)(2,1)}), bf16[4,272,128]{2,1,0:T(8,128)(2,1)S(1)}, u32[]{:S(2)}, u32[]{:S(2)}) async-start(bf16[4,272,128]{2,1,0:T(8,128)(2,1)} %get-tuple-element.31), calls=%async_computation | async-start | bytes 557056 | tf_op jit(solution)/shard_map/all_to_all | solution.py:615
  9.2 3.4 %collective-permute-start.1 = (bf16[8,16,128]{2,1,0:T(8,128)(2,1)S(1)}, bf16[8,16,128]{2,1,0:T(8,128)(2,1)S(1)}, u32[]{:S(2)}, u32[]{:S(2)}) collective-permute-start(bf16[8,16,128]{2,1,0:T(8,128)(2,1)S(1)} %get-tuple-element.30), channel_id=1, source_target_pairs={{0,3},{1,2},{2,1},{3,0},{4,7},{5,6},{6,5},{7,4},{8,11},{9,10},{10,... | collective-permute-start | bytes 98312 | tf_op jit(solution)/shard_map/ppermute | solution.py:560
  12.7 1.0 %copy-start = (bf16[3,3,128,128]{3,2,1,0:T(8,128)(2,1)S(1)}, bf16[3,3,128,128]{3,2,1,0:T(8,128)(2,1)}, u32[]{:S(2)}) copy-start(bf16[3,3,128,128]{3,2,1,0:T(8,128)(2,1)} %kin_ref.9) | copy-start | bytes 884740
  12.7 1.0 %copy-start.1 = (bf16[3,3,128,128]{3,2,1,0:T(8,128)(2,1)S(1)}, bf16[3,3,128,128]{3,2,1,0:T(8,128)(2,1)}, u32[]{:S(2)}) copy-start(bf16[3,3,128,128]{3,2,1,0:T(8,128)(2,1)} %kout_ref.9) | copy-start | bytes 884740
  12.7 1.0 %copy-start.2 = (f32[128]{0:T(128)S(1)}, f32[128]{0:T(128)}, u32[]{:S(2)}) copy-start(f32[128]{0:T(128)} %param.12) | copy-start | bytes 1540
  12.7 6.1 %collective-permute-start.2 = (bf16[2,272,128]{2,1,0:T(8,128)(2,1)S(1)}, bf16[2,272,128]{2,1,0:T(8,128)(2,1)S(1)}, u32[]{:S(2)}, u32[]{:S(2)}) collective-permute-start(bf16[2,272,128]{2,1,0:T(8,128)(2,1)S(1)} %shard_map.115), channel_id=1, source_target_pairs={{1,4},{4,1},{5,8},{8,5},{9,12},{12,9},{3,6},{6,3},{7,10},{10,7},{1... | collective-permute-start | bytes 417800 | tf_op jit(solution)/shard_map/ppermute | solution.py:552
  18.8 2.7 %collective-permute-start.4 = (bf16[4,272,128]{2,1,0:T(8,128)(2,1)S(1)}, bf16[4,272,128]{2,1,0:T(8,128)(2,1)S(1)}, u32[]{:S(2)}, u32[]{:S(2)}) collective-permute-start(bf16[4,272,128]{2,1,0:T(8,128)(2,1)S(1)} %all-to-all-done.block_ref), channel_id=1, source_target_pairs={{0,1},{1,0},{2,3},{3,2},{4,5},{5,4},{6,7},{7,6},{8,9},{9,8},{10,11... | collective-permute-start | bytes 835592 | tf_op jit(solution)/shard_map/ppermute | solution.py:543
  20.1 1.4 %collective-permute-start.3 = (bf16[2,272,128]{2,1,0:T(8,128)(2,1)S(1)}, bf16[2,272,128]{2,1,0:T(8,128)(2,1)S(1)}, u32[]{:S(2)}, u32[]{:S(2)}) collective-permute-start(bf16[2,272,128]{2,1,0:T(8,128)(2,1)S(1)} %collective-permute-done.2.halo_ref), channel_id=1, source_target_pairs={{0,1},{1,0},{2,3},{3,2},{4,5},{5,4},{6,7},{7,6},{8,9},{9,8},{10,11... | collective-permute-start | bytes 417800 | tf_op jit(solution)/shard_map/ppermute | solution.py:543
  23.8 3.3 %collective-permute-start.5 = (bf16[8,16,128]{2,1,0:T(8,128)(2,1)S(1)}, bf16[8,16,128]{2,1,0:T(8,128)(2,1)S(1)}, u32[]{:S(2)}, u32[]{:S(2)}) collective-permute-start(bf16[8,16,128]{2,1,0:T(8,128)(2,1)S(1)} %get-tuple-element.43), channel_id=1, source_target_pairs={{0,3},{1,2},{2,1},{3,0},{4,7},{5,6},{6,5},{7,4},{8,11},{9,10},{10,... | collective-permute-start | bytes 98312 | tf_op jit(solution)/shard_map/ppermute | solution.py:560
  27.2 10.0 %collective-permute-start.6 = (bf16[2,272,128]{2,1,0:T(8,128)(2,1)S(1)}, bf16[2,272,128]{2,1,0:T(8,128)(2,1)S(1)}, u32[]{:S(2)}, u32[]{:S(2)}) collective-permute-start(bf16[2,272,128]{2,1,0:T(8,128)(2,1)S(1)} %shard_map.119), channel_id=1, source_target_pairs={{1,4},{4,1},{5,8},{8,5},{9,12},{12,9},{3,6},{6,3},{7,10},{10,7},{1... | collective-permute-start | bytes 417800 | tf_op jit(solution)/shard_map/ppermute | solution.py:552
  27.8 12.8 %all-to-all-start.1 = ((bf16[8,64,128]{2,1,0:T(8,128)(2,1)}), bf16[8,64,128]{2,1,0:T(8,128)(2,1)S(1)}, u32[]{:S(2)}, u32[]{:S(2)}) async-start(bf16[8,64,128]{2,1,0:T(8,128)(2,1)} %get-tuple-element.53), calls=%async_computation.1 | async-start | bytes 262144 | tf_op jit(solution)/shard_map/all_to_all | solution.py:670
  37.2 3.5 %collective-permute-start.7 = (bf16[2,272,128]{2,1,0:T(8,128)(2,1)S(1)}, bf16[2,272,128]{2,1,0:T(8,128)(2,1)S(1)}, u32[]{:S(2)}, u32[]{:S(2)}) collective-permute-start(bf16[2,272,128]{2,1,0:T(8,128)(2,1)S(1)} %collective-permute-done.6.halo_ref), channel_id=1, source_target_pairs={{0,1},{1,0},{2,3},{3,2},{4,5},{5,4},{6,7},{7,6},{8,9},{9,8},{10,11... | collective-permute-start | bytes 417800 | tf_op jit(solution)/shard_map/ppermute | solution.py:543

commit v2 on v1

--- a/solution.py
+++ b/solution.py
@@ -103,6 +103,28 @@
         edge_ref[i, width : width + TAIL, :] = tail_ref[first + i]
 
 
+MOST_PERMUTES = 8
+
+
+def by_permutes(lats):
+    return lats <= MOST_PERMUTES and lats & (lats - 1) == 0
+
+
+def piece_of(tile):
+    if by_permutes(lax.axis_size("lat")):
+        return lax.bitwise_xor(tile, lax.axis_index("lat"))
+    return tile
+
+
+def sent(pieces):
+    lats = len(pieces)
+    if by_permutes(lats):
+        moved = [lax.ppermute(pieces[k], "lat", [(i, i ^ k) for i in range(lats)]) for k in range(1, lats)]
+        return [pieces[0], *moved]
+    whole = lax.all_to_all(jnp.stack(pieces), "lat", split_axis=0, concat_axis=0, tiled=True)
+    return [whole[k] for k in range(lats)]
+
+
 def pack_kernel(
     dest_hbm,
     row_hbm,
@@ -111,17 +133,11 @@
     obs_hbm,
     precision_hbm,
     noisy_hbm,
-    chunk_ref,
     near_ref,
-    dest_ref,
-    row_ref,
-    col_ref,
-    weight_ref,
-    obs_ref,
-    precision_ref,
-    scale_ref,
-    sems,
+    code_ref,
+    *refs,
 ):
+    *piece_refs, chunk_ref, dest_ref, row_ref, col_ref, weight_ref, obs_ref, precision_ref, scale_ref, sems = refs
     pairs = (
         (dest_hbm, dest_ref),
         (row_hbm, row_ref),
@@ -139,8 +155,8 @@
     half = obs_ref.shape[1]
     first_meta = obs + CAP * half
 
-    def clear(slot, _):
-        chunk_ref[slot] = jnp.zeros(chunk_ref.shape[1:], BF16)
+    def clear(piece, _):
+        chunk_ref[piece] = jnp.zeros(chunk_ref.shape[1:], BF16)
         return 0
 
     lax.fori_loop(0, chunk_ref.shape[0], clear, 0)
@@ -152,11 +168,13 @@
     def pack(b, _):
         dest = dest_ref[b]
         rank = lax.fori_loop(0, b, lambda j, n: n + (dest_ref[j] == dest).astype(jnp.int32), 0)
-        chunk_ref[dest, pl.ds(pl.multiple_of(obs + rank * half, 16), half), :] = obs_ref[b]
+        piece = piece_of(dest)
+        chunk_ref[piece, pl.ds(pl.multiple_of(obs + rank * half, 16), half), :] = obs_ref[b]
+        code_ref[pl.ds(b, 1), :] = jnp.full((1, 128), (piece * CAP + rank).astype(F32))
 
         @pl.when(rank == core)
         def _():
-            chunk_ref[dest, 0:obs, :] = weight_ref[b]
+            chunk_ref[piece, 0:obs, :] = weight_ref[b]
             row = row_ref[b].astype(F32)
             high = lax.div(col_ref[b], 16).astype(F32)
             low = lax.rem(col_ref[b], 16).astype(F32)
@@ -165,12 +183,20 @@
                 jnp.broadcast_to(scale_ref[pl.ds(b, 1), :], (META, obs)),
                 jnp.where(meta_rows == 1, row, jnp.where(meta_rows == 2, high, low)),
             )
-            chunk_ref[dest, first_meta : first_meta + META, :] = meta.astype(BF16)
+            chunk_ref[piece, first_meta : first_meta + META, :] = meta.astype(BF16)
 
         return 0
 
     lax.fori_loop(0, blocks, pack, 0)
+    for k, piece_ref in enumerate(piece_refs):
+        piece_ref[...] = chunk_ref[k]
     copies[-1].wait()
+
+
+def join_kernel(*refs):
+    *piece_refs, whole_ref = refs
+    for k, piece_ref in enumerate(piece_refs):
+        whole_ref[k] = piece_ref[...]
 
 
 def prep_kernel(own_ref, other_ref, x_ref, tail_ref, flat_ref):
@@ -326,19 +352,12 @@
     base_ref,
     g_ref,
     gtail_ref,
-    inn_ref,
-    ext_ref,
-    between_ref,
-    den_ref,
-    field_ref,
-    turned_ref,
-    value_ref,
-    scale_ref,
-    code_ref,
+    *refs,
 ):
+    *inn_refs, ext_ref, between_ref, den_ref, field_ref, turned_ref, value_ref, scale_ref, inn_ref, code_ref = refs
     core = lax.axis_index("ch")
     rows, width, c = x_ref.shape
-    half = inn_ref.shape[1]
+    half = inn_refs[0].shape[1]
     sources, obs = block_ref.shape[0], block_ref.shape[2]
 
     def read(source, cap, first, count):
@@ -404,6 +423,9 @@
         inn_ref[slot] = jnp.where(core == 0, turned[0:half], turned[half : 2 * half])
 
     each(observe)
+    for source, out_ref in enumerate(inn_refs):
+        for cap in range(CAP):
+            out_ref[cap] = inn_ref[source * CAP + cap]
 
     for g in range(rows // 2):
         base = []
@@ -488,55 +510,52 @@
     slope_ref,
     out_middle_ref,
     out_own_ref,
-    back_ref,
-    dest_hbm,
-    next_ref,
-    inn_hbm,
-    ext_ref,
-    between_ref,
-    flat_ref,
-    w3_ref,
-    w4_ref,
-    dest_ref,
-    dest_sem,
-    inn_sems,
+    code_ref,
+    *refs,
 ):
-    dest_copy = pltpu.make_async_copy(dest_hbm, dest_ref, dest_sem)
-    dest_copy.start()
+    *back_refs, next_hbm, inn_hbm, ext_ref, between_ref, flat_ref, w3_ref, w4_ref, next_sems, inn_sems = refs
     core = lax.axis_index("ch")
     rows = x_ref.shape[0]
-    half = next_ref.shape[0]
+    half = next_hbm.shape[0]
     parts = flat_ref.shape[0]
+
+    def give(b, _):
+        code = jnp.max(code_ref[pl.ds(b, 1), :]).astype(jnp.int32)
+        for k, back_ref in enumerate(back_refs):
+
+            @pl.when(lax.div(code, CAP) == k)
+            def _():
+                pltpu.make_async_copy(back_ref.at[lax.rem(code, CAP)], inn_hbm.at[b], inn_sems.at[b]).start()
+
+        return 0
+
+    def given(b, _):
+        pltpu.make_async_copy(back_refs[0].at[0], inn_hbm.at[b], inn_sems.at[b]).wait()
+        return 0
 
     def put(pair, part, plane):
         for i in range(2):
             flat_ref[part, pl.ds(2 * pair + i, half, stride=rows), :] = plane[i * half : (i + 1) * half]
 
+    lax.fori_loop(0, inn_hbm.shape[0], give, 0)
     backward_taps(w3_ref, w4_ref, kin_ref, kout_ref)
-    planes = backward_end(
-        1 - core, x_ref, tail_ref, halo_ref, kept_ref, w3_ref, w4_ref, base_ref, slope_ref, ext_ref, between_ref
-    )
     for part in range(parts):
         for g in range((rows - 4) // 2):
             put(1 + g, part, out_middle_ref[g, part])
         put((rows // 2 - 1) * core, part, out_own_ref[part])
-        put((rows // 2 - 1) * (1 - core), part, planes[part])
-    dest_copy.wait()
-
-    def start(b, _):
-        dest = dest_ref[b]
-        rank = lax.fori_loop(0, b, lambda j, n: n + (dest_ref[j] == dest).astype(jnp.int32), 0)
-        pltpu.make_async_copy(back_ref.at[dest * CAP + rank], inn_hbm.at[b], inn_sems.at[b]).start()
-        return 0
-
-    def finish(b, _):
-        pltpu.make_async_copy(back_ref.at[0], inn_hbm.at[b], inn_sems.at[b]).wait()
-        return 0
-
-    lax.fori_loop(0, inn_hbm.shape[0], start, 0)
-    for part in range(parts):
-        next_ref[:, :, part * 128 : (part + 1) * 128] = flat_ref[part].reshape(half, rows, 128)
-    lax.fori_loop(0, inn_hbm.shape[0], finish, 0)
+    planes = backward_end(
+        1 - core, x_ref, tail_ref, halo_ref, kept_ref, w3_ref, w4_ref, base_ref, slope_ref, ext_ref, between_ref
+    )
+    copies = []
+    for part, plane in enumerate(planes):
+        put((rows // 2 - 1) * (1 - core), part, plane)
+        source = flat_ref.at[part].reshape(half, rows, 128)
+        target = next_hbm.at[:, :, pl.ds(part * 128, 128)]
+        copies.append(pltpu.make_async_copy(source, target, next_sems.at[part]))
+        copies[-1].start()
+    for copy in copies:
+        copy.wait()
+    lax.fori_loop(0, inn_hbm.shape[0], given, 0)
 
 
 def swapped(value):
@@ -596,12 +615,13 @@
     slots = lats * CAP
     wide = width + TAIL
     other = swapped(noisy_state)
-    chunk_shape = shape((lats, obs + CAP * half + META, obs), BF16)
-    chunk, near = call(
+    piece = (obs + CAP * half + META, obs)
+    near, code, *pieces = call(
         pack_kernel,
-        [(chunk_shape, VMEM), (shape(noisy_state.shape, BF16), VMEM)],
+        [(shape(noisy_state.shape, BF16), VMEM), (shape((blocks, 128), F32), VMEM)] + [(shape(piece, BF16), VMEM)] * lats,
         [HBM] * 7,
         [
+            VMEM((lats, *piece), BF16),
             SMEM((blocks,), jnp.int32),
             SMEM((blocks,), jnp.int32),
             SMEM((blocks,), jnp.int32),
@@ -612,7 +632,7 @@
             pltpu.SemaphoreType.DMA((7,)),
         ],
     )(dest_tile, row_offset, col_offset, interp_weight, observed, obs_precision, noisy_state)
-    block = lax.all_to_all(chunk, "lat", split_axis=0, concat_axis=0, tiled=True)
+    pieces = sent(pieces)
     tail_shape = shape((rows, TAIL, c), BF16)
     x, tail = call(
         prep_kernel,
@@ -636,6 +656,7 @@
         [VMEM] * 5,
         [all_rows, most_rows, keep(taps, BF16), keep(taps, BF16), most_slopes, pltpu.SemaphoreType.DMA],
     )(x, beside, kernel_in, kernel_out, bias)
+    (block,) = call(join_kernel, [(shape((lats, *piece), BF16), VMEM)], [VMEM] * lats, [])(*pieces)
     mine, block, kept, slope_middle, den_middle = lax.optimization_barrier((mine, block, kept, slope_middle, den_middle))
     others = swapped(mine)
     slope_own, den_own, w1, w2 = call(
@@ -644,14 +665,14 @@
         [VMEM] * 7,
         [four_rows, four_rows],
     )(x, beside, mine, kept, kernel_in, kernel_out, bias)
-    slope_other, base, g, tail, inn = call(
+    slope_other, base, g, tail, *inn = call(
         forward_kernel,
         [
             (pair, VMEM),
             (shape((rows // 2, width, c), F32), VMEM),
             (shape((rows, width, c), BF16), VMEM),
             (tail_shape, VMEM),
-            (shape((slots, half, obs), BF16), VMEM),
+            *[(shape((CAP, half, obs), BF16), VMEM)] * lats,
         ],
         [VMEM] * 11,
         [
@@ -662,12 +683,13 @@
             VMEM((slots, obs, obs), BF16),
             VMEM((slots, obs, c), BF16),
             VMEM((slots, obs, c), F32),
+            VMEM((slots, half, obs), BF16),
             SMEM((slots,), jnp.int32),
         ],
         {0: 2, 1: 3},
     )(x, beside, others, kept, w1, w2, bias, den_middle, den_own, block, swapped(block))
 
-    back = lax.all_to_all(inn, "lat", split_axis=0, concat_axis=0, tiled=True)
+    back = sent(inn)
     beside, mine = exchanged(g, tail)
     parts = width // 128
     kept, out_middle = call(
@@ -693,19 +715,18 @@
     )(g, beside, mine, kept, kernel_in, kernel_out, base, slope_own)
     next_state, innovation = call(
         backward_kernel,
-        [(shape((half, rows, width), F32), OUT), (shape(observed.shape, BF16), HBM)],
-        [VMEM] * 11 + [HBM],
+        [(shape((half, rows, width), F32), HBM), (shape(observed.shape, BF16), HBM)],
+        [VMEM] * (11 + lats),
         [
             four_rows,
             four_rows,
             VMEM((parts, half * rows, 128), F32),
             keep(taps, BF16),
             keep(own_taps, BF16),
-            SMEM((blocks,), jnp.int32),
-            pltpu.SemaphoreType.DMA,
+            pltpu.SemaphoreType.DMA((parts,)),
             pltpu.SemaphoreType.DMA((blocks,)),
         ],
-    )(g, beside, others, kept, kernel_in, kernel_out, base, slope_other, out_middle, out_own, back, dest_tile)
+    )(g, beside, others, kept, kernel_in, kernel_out, base, slope_other, out_middle, out_own, code, *back)
     return next_state, innovation
 
 

time: 43.5 us -> 48.5 us (1.11)
  waiting for transfers between devices: 9.64 us -> 14 us
  starting transfers between devices: 18.5 us -> 20 us
  Pallas kernels: 14 us -> 12.9 us
    all_to_all x2 -> x0, starting transfers between devices: 12.3 us -> none  [the longest x1 6.4 us: body(): back = lax.all_to_all(inn, 'lat', split_axis=0, concat_axis=0, tiled=True)]
    ppermute x0 -> x6, starting transfers between devices: none -> 10.6 us  [sent(): lax.ppermute(pieces[k], 'lat', [(i, i ^ k) for i in range(lats)])]
    ppermute x0 -> x6, waiting for transfers between devices: none -> 9.78 us  [sent(): lax.ppermute(pieces[k], 'lat', [(i, i ^ k) for i in range(lats)])]
    all_to_all x2 -> x0, waiting for transfers between devices: 5.42 us -> none  [the longest x1 2.96 us: body(): lax.all_to_all(chunk, 'lat', split_axis=0, concat_axis=0, tiled=True)]
    ppermute x4, starting transfers between devices: 1.96 us -> 4.05 us  [swapped(): return lax.ppermute(value, 'ch', [(0, 1), (1, 0)])]
    pallas_call x10 -> x11, Pallas kernels: 14 us -> 12.9 us  [apply(): run(*(pltpu.with_memory_space_constraint(a, space) if space in (VMEM, HBM...]
    ppermute x2, starting transfers between devices: 2.83 us -> 3.94 us  [move(): return lax.ppermute(value, ('lon', 'ch'), pairs)]
  transfers between devices with their start and end apart: 10 -> 14, of which waited for: 5 -> 9; matrix products, arithmetic and copies ran while one was open for 0% -> 0% of each run, Pallas kernels for 21% -> 17%
where the time goes in v2:
time: 48.5 us; the launch traced here: 48.3 us
  starting transfers between devices  20 us (41%)
  waiting for transfers between devices  14 us (29%)
  Pallas kernels  12.9 us (27%)
  between operations  0.77 us (2%)
  local copies, waits for them, and re-layouts  0.64 us (1%)
    pallas_call x11, Pallas kernels, apply(): run(*(pltpu.with_memory_space_constraint(a, space) if space in (VMEM, HBM...  12.9 us
    ppermute x6, starting transfers between devices, sent(): lax.ppermute(pieces[k], 'lat', [(i, i ^ k) for i in range(lats)])  10.6 us
    ppermute x6, waiting for transfers between devices, sent(): lax.ppermute(pieces[k], 'lat', [(i, i ^ k) for i in range(lats)])  9.78 us
    ppermute x4, starting transfers between devices, swapped(): return lax.ppermute(value, 'ch', [(0, 1), (1, 0)])  4.05 us
    ppermute x2, starting transfers between devices, move(): return lax.ppermute(value, ('lon', 'ch'), pairs)  3.94 us
    ppermute x2, waiting for transfers between devices, move(): return lax.ppermute(value, ('lon', 'ch'), pairs)  3.77 us
    ppermute x2, starting transfers between devices, from_row_neighbour(): return lax.ppermute(value, ('lat', 'ch'), pairs)  1.47 us
  transfers between devices with their start and end apart: 14, of which 9 were waited for; matrix products, arithmetic and copies ran while one was open for 0% of the time, Pallas kernels for 17%

profile of v2, /device:TPU:0, one launch (start us, length us, event | category | flops | bytes accessed | tf_op | source)
XLA Modules:
  0.0 48.3 jit_solution(14984799505036666310)
XLA Ops:
  0.6 0.6 %collective-permute-start = (bf16[64,8,256]{2,1,0:T(8,128)(2,1)}, bf16[64,8,256]{2,1,0:T(8,128)(2,1)S(1)}, u32[]{:S(2)}, u32[]{:S(2)}) collective-permute-start(bf16[64,8,256]{2,1,0:T(8,128)(2,1)} %noisy_hbm.1), channel_id=1, source_target_pairs={{0,1},{1,0},{2,3},{3,2},{4,5},{5,4},{6,7},{7,6},{8,9},{9,8},{10,11... | collective-permute-start | bytes 786440 | tf_op jit(solution)/shard_map/ppermute | solution.py:562
  1.2 1.1 %shard_map.113 = (bf16[64,8,256]{2,1,0:T(8,128)(2,1)S(1)}, f32[4,128]{1,0:T(4,128)S(1)}, bf16[272,128]{1,0:T(8,128)(2,1)S(1)}, bf16[272,128]{1,0:T(8,128)(2,1)S(...) custom-call(s32[4]{0:T(128)} %dest_hbm.1, s32[4]{0:T(128)} %row_hbm.1, s32[4]{0:T(128)} %col_hbm.1, ...), custom_call_target="tpu_custom_call" | custom-call | tf_op jit(solution)/shard_map/pallas_call | solution.py:41
  2.3 0.2 collective-permute-done.other_ref
  2.6 0.3 shard_map.114
  2.9 2.7 %collective-permute-start.1 = (bf16[8,16,128]{2,1,0:T(8,128)(2,1)S(1)}, bf16[8,16,128]{2,1,0:T(8,128)(2,1)S(1)}, u32[]{:S(2)}, u32[]{:S(2)}) collective-permute-start(bf16[8,16,128]{2,1,0:T(8,128)(2,1)S(1)} %get-tuple-element.37), channel_id=1, source_target_pairs={{0,3},{1,2},{2,1},{3,0},{4,7},{5,6},{6,5},{7,4},{8,11},{9,10},{10,... | collective-permute-start | bytes 98312 | tf_op jit(solution)/shard_map/ppermute | solution.py:579
  5.5 1.6 %collective-permute-done.1.tail_ref = bf16[8,16,128]{2,1,0:T(8,128)(2,1)S(1)} collective-permute-done((bf16[8,16,128]{2,1,0:T(8,128)(2,1)S(1)}, bf16[8,16,128]{2,1,0:T(8,128)(2,1)S(1)}, u32[]{:S(2)}, u32[]{:S(2)}) %collective-permute-start.1) | collective-permute-done | bytes 32800 | tf_op jit(solution)/shard_map/ppermute | solution.py:579
  7.1 0.0 copy-start.1
  7.2 0.0 copy-start
  7.2 0.8 %collective-permute-start.2 = (bf16[2,272,128]{2,1,0:T(8,128)(2,1)S(1)}, bf16[2,272,128]{2,1,0:T(8,128)(2,1)S(1)}, u32[]{:S(2)}, u32[]{:S(2)}) collective-permute-start(bf16[2,272,128]{2,1,0:T(8,128)(2,1)S(1)} %shard_map.115), channel_id=1, source_target_pairs={{1,4},{4,1},{5,8},{8,5},{9,12},{12,9},{3,6},{6,3},{7,10},{10,7},{1... | collective-permute-start | bytes 417800 | tf_op jit(solution)/shard_map/ppermute | solution.py:571
  8.0 3.4 %collective-permute-start.3 = (bf16[272,128]{1,0:T(8,128)(2,1)S(1)}, bf16[272,128]{1,0:T(8,128)(2,1)S(1)}, u32[]{:S(2)}, u32[]{:S(2)}) collective-permute-start(bf16[272,128]{1,0:T(8,128)(2,1)S(1)} %get-tuple-element.39), channel_id=1, source_target_pairs={{0,4},{4,0},{8,12},{12,8},{1,5},{5,1},{9,13},{13,9},{2,6},{6,2},{1... | collective-permute-start | bytes 208904 | tf_op jit(solution)/shard_map/ppermute | solution.py:122
  11.4 2.8 %collective-permute-start.4 = (bf16[272,128]{1,0:T(8,128)(2,1)S(1)}, bf16[272,128]{1,0:T(8,128)(2,1)S(1)}, u32[]{:S(2)}, u32[]{:S(2)}) collective-permute-start(bf16[272,128]{1,0:T(8,128)(2,1)S(1)} %get-tuple-element.40), channel_id=1, source_target_pairs={{0,8},{4,12},{8,0},{12,4},{1,9},{5,13},{9,1},{13,5},{2,10},{6,14},... | collective-permute-start | bytes 208904 | tf_op jit(solution)/shard_map/ppermute | solution.py:122
  14.2 0.0 collective-permute-start.5
  14.2 1.7 %collective-permute-done.3.refs_1_ = bf16[272,128]{1,0:T(8,128)(2,1)S(1)} collective-permute-done((bf16[272,128]{1,0:T(8,128)(2,1)S(1)}, bf16[272,128]{1,0:T(8,128)(2,1)S(1)}, u32[]{:S(2)}, u32[]{:S(2)}) %collective-permute-start.3) | collective-permute-done | bytes 69664 | tf_op jit(solution)/shard_map/ppermute | solution.py:122
  15.8 1.1 %collective-permute-done.4.refs_2_ = bf16[272,128]{1,0:T(8,128)(2,1)S(1)} collective-permute-done((bf16[272,128]{1,0:T(8,128)(2,1)S(1)}, bf16[272,128]{1,0:T(8,128)(2,1)S(1)}, u32[]{:S(2)}, u32[]{:S(2)}) %collective-permute-start.4) | collective-permute-done | bytes 69664 | tf_op jit(solution)/shard_map/ppermute | solution.py:122
  16.9 4.2 %collective-permute-done.5.refs_3_ = bf16[272,128]{1,0:T(8,128)(2,1)S(1)} collective-permute-done((bf16[272,128]{1,0:T(8,128)(2,1)S(1)}, bf16[272,128]{1,0:T(8,128)(2,1)S(1)}, u32[]{:S(2)}, u32[]{:S(2)}) %collective-permute-start.5) | collective-permute-done | bytes 69664 | tf_op jit(solution)/shard_map/ppermute | solution.py:122
  21.2 0.0 copy-start.2
  21.2 0.0 copy-done.1
  21.2 0.0 copy-done
  21.2 0.6 %copy-done.2 = f32[128]{0:T(128)S(1)} copy-done((f32[128]{0:T(128)S(1)}, f32[128]{0:T(128)}, u32[]{:S(2)}) %copy-start.2) | copy-done | bytes 536
  21.8 2.2 %shard_map.117 = (f32[6,272,128]{2,1,0:T(8,128)}, bf16[4,272,128]{2,1,0:T(8,128)(2,1)S(1)}, bf16[4,256,128]{2,1,0:T(8,128)(2,1)S(1)}) custom-call(bf16[8,256,128]{2,1,0:T(8,128)(2,1)S(1)} %get-tuple-element.36.x_ref, bf16[8,16,128]{2,1,0:T(8,128)(2,1)S(1)} %collective-permute-done.1.tail_ref, bf16[3,3,128,128]{3,2,1,0:T(8,128)(2,1)S(1)} %copy-done, ...), custom_call_target="tpu_custom_call" | custom-call | tf_op jit(solution)/shard_map/pallas_call | solution.py:41
  24.0 0.0 collective-permute-done.2.halo_ref
  24.0 0.1 collective-permute-start.7
  24.1 0.5 %collective-permute-start.6 = (bf16[2,272,128]{2,1,0:T(8,128)(2,1)S(1)}, bf16[2,272,128]{2,1,0:T(8,128)(2,1)S(1)}, u32[]{:S(2)}, u32[]{:S(2)}) collective-permute-start(bf16[2,272,128]{2,1,0:T(8,128)(2,1)S(1)} %collective-permute-done.2.halo_ref), channel_id=1, source_target_pairs={{0,1},{1,0},{2,3},{3,2},{4,5},{5,4},{6,7},{7,6},{8,9},{9,8},{10,11... | collective-permute-start | bytes 417800 | tf_op jit(solution)/shard_map/ppermute | solution.py:562
  24.6 1.1 %shard_map.118 = (f32[2,272,128]{2,1,0:T(8,128)S(1)}, bf16[2,256,128]{2,1,0:T(8,128)(2,1)S(1)}, bf16[512,768]{1,0:T(8,128)(2,1)S(1)}, bf16[512,768]{1,0:T(8,128)(2,1)S(1)}) custom-call(bf16[8,256,128]{2,1,0:T(8,128)(2,1)S(1)} %get-tuple-element.36.x_ref, bf16[8,16,128]{2,1,0:T(8,128)(2,1)S(1)} %collective-permute-done.1.tail_ref, ...), custom_call_target="tpu_custom_call" | custom-call | tf_op jit(solution)/shard_map/pallas_call | solution.py:41
  25.7 0.2 collective-permute-done.6.halo_ref
  25.8 0.0 collective-permute-done.7.other_block_ref
  25.8 2.0 %shard_map.119 = (f32[2,272,128]{2,1,0:T(8,128)S(1)}, f32[4,256,128]{2,1,0:T(8,128)S(1)}, bf16[8,256,128]{2,1,0:T(8,128)(2,1)S(1)}, bf16[8,16,128]{2,1,0:T(8,128...) custom-call(bf16[8,256,128]{2,1,0:T(8,128)(2,1)S(1)} %get-tuple-elem, ...), custom_call_target="tpu_custom_call", output_to_operand_aliasing={{2}: (0, {}), {3}: (1, {})} | custom-call | tf_op jit(solution)/shard_map/pallas_call | solution.py:41
  27.8 1.3 %collective-permute-start.8 = (bf16[8,16,128]{2,1,0:T(8,128)(2,1)S(1)}, bf16[8,16,128]{2,1,0:T(8,128)(2,1)S(1)}, u32[]{:S(2)}, u32[]{:S(2)}) collective-permute-start(bf16[8,16,128]{2,1,0:T(8,128)(2,1)S(1)} %get-tuple-element.53), channel_id=1, source_target_pairs={{0,3},{1,2},{2,1},{3,0},{4,7},{5,6},{6,5},{7,4},{8,11},{9,10},{10,... | collective-permute-start | bytes 98312 | tf_op jit(solution)/shard_map/ppermute | solution.py:579
  29.1 2.2 %collective-permute-done.8.tail_ref = bf16[8,16,128]{2,1,0:T(8,128)(2,1)S(1)} collective-permute-done((bf16[8,16,128]{2,1,0:T(8,128)(2,1)S(1)}, bf16[8,16,128]{2,1,0:T(8,128)(2,1)S(1)}, u32[]{:S(2)}, u32[]{:S(2)}) %collective-permute-start.8) | collective-permute-done | bytes 32800 | tf_op jit(solution)/shard_map/ppermute | solution.py:579
  31.3 0.7 %collective-permute-start.9 = (bf16[2,272,128]{2,1,0:T(8,128)(2,1)S(1)}, bf16[2,272,128]{2,1,0:T(8,128)(2,1)S(1)}, u32[]{:S(2)}, u32[]{:S(2)}) collective-permute-start(bf16[2,272,128]{2,1,0:T(8,128)(2,1)S(1)} %shard_map.120), channel_id=1, source_target_pairs={{1,4},{4,1},{5,8},{8,5},{9,12},{12,9},{3,6},{6,3},{7,10},{10,7},{1... | collective-permute-start | bytes 417800 | tf_op jit(solution)/shard_map/ppermute | solution.py:571
  32.0 2.9 %shard_map.121 = (bf16[4,272,128]{2,1,0:T(8,128)(2,1)S(1)}, f32[2,2,128,128]{3,2,1,0:T(8,128)S(1)}) custom-call(bf16[8,256,128]{2,1,0:T(8,128)(2,1)S(1)} %get-tuple-element.52.x_ref, bf16[8,16,128]{2,1,0:T(8,128)(2,1)S(1)} %collective-permute-done.8.tail_ref, bf16[3,3,128,128]{3,2,1,0:T(8,128)(2,1)S(1)} %copy-done, bf16[3,3,128,128]{3,2,1,0:T(8,128)(2,1)S(1)} %copy-done.1, ...), custom_call_target="tpu_custom_call" | custom-call | tf_op jit(solution)/shard_map/pallas_call | solution.py:41
  34.9 0.0 collective-permute-done.9.halo_ref
  34.9 2.9 %collective-permute-start.10 = (bf16[2,272,128]{2,1,0:T(8,128)(2,1)S(1)}, bf16[2,272,128]{2,1,0:T(8,128)(2,1)S(1)}, u32[]{:S(2)}, u32[]{:S(2)}) collective-permute-start(bf16[2,272,128]{2,1,0:T(8,128)(2,1)S(1)} %collective-permute-done.9.halo_ref), channel_id=1, source_target_pairs={{0,1},{1,0},{2,3},{3,2},{4,5},{5,4},{6,7},{7,6},{8,9},{9,8},{10,11... | collective-permute-start | bytes 417800 | tf_op jit(solution)/shard_map/ppermute | solution.py:562
  37.8 1.5 %collective-permute-start.11 = (bf16[2,64,128]{2,1,0:T(8,128)(2,1)S(1)}, bf16[2,64,128]{2,1,0:T(8,128)(2,1)S(1)}, u32[]{:S(2)}, u32[]{:S(2)}) collective-permute-start(bf16[2,64,128]{2,1,0:T(8,128)(2,1)S(1)} %get-tuple-element.65), channel_id=1, source_target_pairs={{0,4},{4,0},{8,12},{12,8},{1,5},{5,1},{9,13},{13,9},{2,6},{6,2},{1... | collective-permute-start | bytes 98312 | tf_op jit(solution)/shard_map/ppermute | solution.py:122
  39.3 0.9 %collective-permute-start.12 = (bf16[2,64,128]{2,1,0:T(8,128)(2,1)S(1)}, bf16[2,64,128]{2,1,0:T(8,128)(2,1)S(1)}, u32[]{:S(2)}, u32[]{:S(2)}) collective-permute-start(bf16[2,64,128]{2,1,0:T(8,128)(2,1)S(1)} %get-tuple-element.66), channel_id=1, source_target_pairs={{0,8},{4,12},{8,0},{12,4},{1,9},{5,13},{9,1},{13,5},{2,10},{6,14},... | collective-permute-start | bytes 98312 | tf_op jit(solution)/shard_map/ppermute | solution.py:122
  40.3 2.0 %collective-permute-start.13 = (bf16[2,64,128]{2,1,0:T(8,128)(2,1)S(1)}, bf16[2,64,128]{2,1,0:T(8,128)(2,1)S(1)}, u32[]{:S(2)}, u32[]{:S(2)}) collective-permute-start(bf16[2,64,128]{2,1,0:T(8,128)(2,1)S(1)} %get-tuple-element.67), channel_id=1, source_target_pairs={{0,12},{4,8},{8,4},{12,0},{1,13},{5,9},{9,5},{13,1},{2,14},{6,10},... | collective-permute-start | bytes 98312 | tf_op jit(solution)/shard_map/ppermute | solution.py:122
  42.2 0.9 %shard_map.122.out_own_ref = f32[2,128,128]{2,1,0:T(8,128)S(1)} custom-call(bf16[8,256,128]{2,1,0:T(8,128)(2,1)S(1)} %get-tuple-element.52.x_ref, bf16[8,16,128]{2,1,0:T(8,128)(2,1)S(1)} %collective-permute-done.8.tail_ref, bf16[2,272,128]{2,1,0:T(8,128)(2,1)S(1)} %collective-permute-done.9.halo_ref, bf16[4,272,128]{2,1,0:T(8,128)(2,1)S(1)} %get-tuple-element.59.kept_ref, ...), custom_call_target="tpu_custom_call" | custom-call | tf_op jit(solution)/shard_map/pallas_call | solution.py:41
  43.1 0.0 collective-permute-done.11.refs_1_
  43.1 2.0 %collective-permute-done.12.refs_2_ = bf16[2,64,128]{2,1,0:T(8,128)(2,1)S(1)} collective-permute-done((bf16[2,64,128]{2,1,0:T(8,128)(2,1)S(1)}, bf16[2,64,128]{2,1,0:T(8,128)(2,1)S(1)}, u32[]{:S(2)}, u32[]{:S(2)}) %collective-permute-start.12) | collective-permute-done | bytes 32800 | tf_op jit(solution)/shard_map/ppermute | solution.py:122
  45.2 0.8 %collective-permute-done.13.refs_3_ = bf16[2,64,128]{2,1,0:T(8,128)(2,1)S(1)} collective-permute-done((bf16[2,64,128]{2,1,0:T(8,128)(2,1)S(1)}, bf16[2,64,128]{2,1,0:T(8,128)(2,1)S(1)}, u32[]{:S(2)}, u32[]{:S(2)}) %collective-permute-start.13) | collective-permute-done | bytes 32800 | tf_op jit(solution)/shard_map/ppermute | solution.py:122
  46.0 0.0 collective-permute-done.10.halo_ref
  46.0 2.3 %shard_map.123 = (f32[64,8,256]{2,1,0:T(8,128)}, bf16[4,64,128]{2,1,0:T(8,128)(2,1)}) custom-call(bf16[8,256,128]{2,1,0:T(8,128)(2,1)S(1)} %get-tuple-element.52.x_ref, bf16[8,16,128]{2,1,0:T(8,128)(2,1)S(1)} %collective-permute-done.8.tail_ref, bf16[2,272,128]{2,1,0:T(8,128)(2,1)S(1)} %collective-permute-done.10.halo_ref, ...), custom_call_target="tpu_custom_call" | custom-call | tf_op jit(solution)/shard_map/pallas_call | solution.py:41
  (3 shorter events, 0.0 us)
Async XLA Ops:
  0.6 1.9 %collective-permute-start = (bf16[64,8,256]{2,1,0:T(8,128)(2,1)}, bf16[64,8,256]{2,1,0:T(8,128)(2,1)S(1)}, u32[]{:S(2)}, u32[]{:S(2)}) collective-permute-start(bf16[64,8,256]{2,1,0:T(8,128)(2,1)} %noisy_hbm.1), channel_id=1, source_target_pairs={{0,1},{1,0},{2,3},{3,2},{4,5},{5,4},{6,7},{7,6},{8,9},{9,8},{10,11... | collective-permute-start | bytes 786440 | tf_op jit(solution)/shard_map/ppermute | solution.py:562
  2.9 4.3 %collective-permute-start.1 = (bf16[8,16,128]{2,1,0:T(8,128)(2,1)S(1)}, bf16[8,16,128]{2,1,0:T(8,128)(2,1)S(1)}, u32[]{:S(2)}, u32[]{:S(2)}) collective-permute-start(bf16[8,16,128]{2,1,0:T(8,128)(2,1)S(1)} %get-tuple-element.37), channel_id=1, source_target_pairs={{0,3},{1,2},{2,1},{3,0},{4,7},{5,6},{6,5},{7,4},{8,11},{9,10},{10,... | collective-permute-start | bytes 98312 | tf_op jit(solution)/shard_map/ppermute | solution.py:579
  7.1 14.0 %copy-start.1 = (bf16[3,3,128,128]{3,2,1,0:T(8,128)(2,1)S(1)}, bf16[3,3,128,128]{3,2,1,0:T(8,128)(2,1)}, u32[]{:S(2)}) copy-start(bf16[3,3,128,128]{3,2,1,0:T(8,128)(2,1)} %kout_ref.9) | copy-start | bytes 884740
  7.2 14.0 %copy-start = (bf16[3,3,128,128]{3,2,1,0:T(8,128)(2,1)S(1)}, bf16[3,3,128,128]{3,2,1,0:T(8,128)(2,1)}, u32[]{:S(2)}) copy-start(bf16[3,3,128,128]{3,2,1,0:T(8,128)(2,1)} %kin_ref.9) | copy-start | bytes 884740
  7.2 16.8 %collective-permute-start.2 = (bf16[2,272,128]{2,1,0:T(8,128)(2,1)S(1)}, bf16[2,272,128]{2,1,0:T(8,128)(2,1)S(1)}, u32[]{:S(2)}, u32[]{:S(2)}) collective-permute-start(bf16[2,272,128]{2,1,0:T(8,128)(2,1)S(1)} %shard_map.115), channel_id=1, source_target_pairs={{1,4},{4,1},{5,8},{8,5},{9,12},{12,9},{3,6},{6,3},{7,10},{10,7},{1... | collective-permute-start | bytes 417800 | tf_op jit(solution)/shard_map/ppermute | solution.py:571
  8.0 7.9 %collective-permute-start.3 = (bf16[272,128]{1,0:T(8,128)(2,1)S(1)}, bf16[272,128]{1,0:T(8,128)(2,1)S(1)}, u32[]{:S(2)}, u32[]{:S(2)}) collective-permute-start(bf16[272,128]{1,0:T(8,128)(2,1)S(1)} %get-tuple-element.39), channel_id=1, source_target_pairs={{0,4},{4,0},{8,12},{12,8},{1,5},{5,1},{9,13},{13,9},{2,6},{6,2},{1... | collective-permute-start | bytes 208904 | tf_op jit(solution)/shard_map/ppermute | solution.py:122
  11.4 5.5 %collective-permute-start.4 = (bf16[272,128]{1,0:T(8,128)(2,1)S(1)}, bf16[272,128]{1,0:T(8,128)(2,1)S(1)}, u32[]{:S(2)}, u32[]{:S(2)}) collective-permute-start(bf16[272,128]{1,0:T(8,128)(2,1)S(1)} %get-tuple-element.40), channel_id=1, source_target_pairs={{0,8},{4,12},{8,0},{12,4},{1,9},{5,13},{9,1},{13,5},{2,10},{6,14},... | collective-permute-start | bytes 208904 | tf_op jit(solution)/shard_map/ppermute | solution.py:122
  14.2 7.0 %collective-permute-start.5 = (bf16[272,128]{1,0:T(8,128)(2,1)S(1)}, bf16[272,128]{1,0:T(8,128)(2,1)S(1)}, u32[]{:S(2)}, u32[]{:S(2)}) collective-permute-start(bf16[272,128]{1,0:T(8,128)(2,1)S(1)} %get-tuple-element.41), channel_id=1, source_target_pairs={{0,12},{4,8},{8,4},{12,0},{1,13},{5,9},{9,5},{13,1},{2,14},{6,10},... | collective-permute-start | bytes 208904 | tf_op jit(solution)/shard_map/ppermute | solution.py:122
  21.2 0.7 %copy-start.2 = (f32[128]{0:T(128)S(1)}, f32[128]{0:T(128)}, u32[]{:S(2)}) copy-start(f32[128]{0:T(128)} %param.12) | copy-start | bytes 1540
  24.0 1.8 %collective-permute-start.7 = (bf16[4,272,128]{2,1,0:T(8,128)(2,1)S(1)}, bf16[4,272,128]{2,1,0:T(8,128)(2,1)S(1)}, u32[]{:S(2)}, u32[]{:S(2)}) collective-permute-start(bf16[4,272,128]{2,1,0:T(8,128)(2,1)S(1)} %shard_map.116.block_ref), channel_id=1, source_target_pairs={{0,1},{1,0},{2,3},{3,2},{4,5},{5,4},{6,7},{7,6},{8,9},{9,8},{10,11... | collective-permute-start | bytes 835592 | tf_op jit(solution)/shard_map/ppermute | solution.py:562
  24.1 1.7 %collective-permute-start.6 = (bf16[2,272,128]{2,1,0:T(8,128)(2,1)S(1)}, bf16[2,272,128]{2,1,0:T(8,128)(2,1)S(1)}, u32[]{:S(2)}, u32[]{:S(2)}) collective-permute-start(bf16[2,272,128]{2,1,0:T(8,128)(2,1)S(1)} %collective-permute-done.2.halo_ref), channel_id=1, source_target_pairs={{0,1},{1,0},{2,3},{3,2},{4,5},{5,4},{6,7},{7,6},{8,9},{9,8},{10,11... | collective-permute-start | bytes 417800 | tf_op jit(solution)/shard_map/ppermute | solution.py:562
  27.8 3.5 %collective-permute-start.8 = (bf16[8,16,128]{2,1,0:T(8,128)(2,1)S(1)}, bf16[8,16,128]{2,1,0:T(8,128)(2,1)S(1)}, u32[]{:S(2)}, u32[]{:S(2)}) collective-permute-start(bf16[8,16,128]{2,1,0:T(8,128)(2,1)S(1)} %get-tuple-element.53), channel_id=1, source_target_pairs={{0,3},{1,2},{2,1},{3,0},{4,7},{5,6},{6,5},{7,4},{8,11},{9,10},{10,... | collective-permute-start | bytes 98312 | tf_op jit(solution)/shard_map/ppermute | solution.py:579
  31.3 3.6 %collective-permute-start.9 = (bf16[2,272,128]{2,1,0:T(8,128)(2,1)S(1)}, bf16[2,272,128]{2,1,0:T(8,128)(2,1)S(1)}, u32[]{:S(2)}, u32[]{:S(2)}) collective-permute-start(bf16[2,272,128]{2,1,0:T(8,128)(2,1)S(1)} %shard_map.120), channel_id=1, source_target_pairs={{1,4},{4,1},{5,8},{8,5},{9,12},{12,9},{3,6},{6,3},{7,10},{10,7},{1... | collective-permute-start | bytes 417800 | tf_op jit(solution)/shard_map/ppermute | solution.py:571
  34.9 11.1 %collective-permute-start.10 = (bf16[2,272,128]{2,1,0:T(8,128)(2,1)S(1)}, bf16[2,272,128]{2,1,0:T(8,128)(2,1)S(1)}, u32[]{:S(2)}, u32[]{:S(2)}) collective-permute-start(bf16[2,272,128]{2,1,0:T(8,128)(2,1)S(1)} %collective-permute-done.9.halo_ref), channel_id=1, source_target_pairs={{0,1},{1,0},{2,3},{3,2},{4,5},{5,4},{6,7},{7,6},{8,9},{9,8},{10,11... | collective-permute-start | bytes 417800 | tf_op jit(solution)/shard_map/ppermute | solution.py:562
  37.8 5.3 %collective-permute-start.11 = (bf16[2,64,128]{2,1,0:T(8,128)(2,1)S(1)}, bf16[2,64,128]{2,1,0:T(8,128)(2,1)S(1)}, u32[]{:S(2)}, u32[]{:S(2)}) collective-permute-start(bf16[2,64,128]{2,1,0:T(8,128)(2,1)S(1)} %get-tuple-element.65), channel_id=1, source_target_pairs={{0,4},{4,0},{8,12},{12,8},{1,5},{5,1},{9,13},{13,9},{2,6},{6,2},{1... | collective-permute-start | bytes 98312 | tf_op jit(solution)/shard_map/ppermute | solution.py:122
  39.3 5.9 %collective-permute-start.12 = (bf16[2,64,128]{2,1,0:T(8,128)(2,1)S(1)}, bf16[2,64,128]{2,1,0:T(8,128)(2,1)S(1)}, u32[]{:S(2)}, u32[]{:S(2)}) collective-permute-start(bf16[2,64,128]{2,1,0:T(8,128)(2,1)S(1)} %get-tuple-element.66), channel_id=1, source_target_pairs={{0,8},{4,12},{8,0},{12,4},{1,9},{5,13},{9,1},{13,5},{2,10},{6,14},... | collective-permute-start | bytes 98312 | tf_op jit(solution)/shard_map/ppermute | solution.py:122
  40.3 5.7 %collective-permute-start.13 = (bf16[2,64,128]{2,1,0:T(8,128)(2,1)S(1)}, bf16[2,64,128]{2,1,0:T(8,128)(2,1)S(1)}, u32[]{:S(2)}, u32[]{:S(2)}) collective-permute-start(bf16[2,64,128]{2,1,0:T(8,128)(2,1)S(1)} %get-tuple-element.67), channel_id=1, source_target_pairs={{0,12},{4,8},{8,4},{12,0},{1,13},{5,9},{9,5},{13,1},{2,14},{6,10},... | collective-permute-start | bytes 98312 | tf_op jit(solution)/shard_map/ppermute | solution.py:122

commit v3 on v2

--- a/solution.py
+++ b/solution.py
@@ -119,8 +119,10 @@
 def sent(pieces):
     lats = len(pieces)
     if by_permutes(lats):
-        moved = [lax.ppermute(pieces[k], "lat", [(i, i ^ k) for i in range(lats)]) for k in range(1, lats)]
-        return [pieces[0], *moved]
+        moved = [pieces[0]]
+        for k in range(1, lats):
+            moved.append(lax.ppermute(pieces[k], "lat", [(i, i ^ k) for i in range(lats)]))
+        return moved
     whole = lax.all_to_all(jnp.stack(pieces), "lat", split_axis=0, concat_axis=0, tiled=True)
     return [whole[k] for k in range(lats)]
 
@@ -277,15 +279,13 @@
     kin_ref,
     kout_ref,
     bias_ref,
-    slope_hbm,
+    slope_ref,
     kept_ref,
     den_ref,
     ext_ref,
     hidden_ref,
     w1_ref,
     w2_ref,
-    slope_ref,
-    save_sem,
 ):
     rows, width, _ = x_ref.shape
     forward_taps(w1_ref, w2_ref, kin_ref, kout_ref)
@@ -297,15 +297,12 @@
             hidden, slope = activate(y, bias)
             slope_ref[2 * g + i] = slope
             hidden_ref[2 * g + i] = hidden.astype(BF16)
-    save = pltpu.make_async_copy(slope_ref, slope_hbm, save_sem)
-    save.start()
     for i in range(2):
         kept_ref[i] = hidden_ref[i]
         kept_ref[2 + i] = hidden_ref[rows - 4 + i]
     for g in range((rows - 4) // 2):
         for i, y in enumerate(row_pair(hidden_ref, w2_ref, 2 * g)):
             den_ref[2 * g + i] = (x_ref[2 + 2 * g + i].astype(F32) + y[0:width, :]).astype(BF16)
-    save.wait()
 
 
 def forward_end(end, x_ref, tail_ref, halo_ref, kept_ref, w1_ref, w2_ref, bias_ref, slope_ref, ext_ref, between_ref):
@@ -443,31 +440,20 @@
     kin_ref,
     kout_ref,
     base_ref,
-    slope_hbm,
+    slope_ref,
     kept_ref,
     out_ref,
     ext_ref,
     grad_ref,
     w3_ref,
     w4_ref,
-    slope_ref,
-    load_sems,
 ):
     rows = x_ref.shape[0]
-
-    def load(g):
-        at = pl.ds(2 * g, 2)
-        return pltpu.make_async_copy(slope_hbm.at[at], slope_ref.at[at], load_sems.at[g])
-
-    for g in range((rows - 2) // 2):
-        load(g).start()
     backward_taps(w3_ref, w4_ref, kin_ref, kout_ref)
     for h in range(rows):
         copy_row(ext_ref, h, x_ref, tail_ref, h)
     for g in range((rows - 2) // 2):
-        pair = row_pair(ext_ref, w3_ref, 2 * g)
-        load(g).wait()
-        for i, y in enumerate(pair):
+        for i, y in enumerate(row_pair(ext_ref, w3_ref, 2 * g)):
             grad_ref[2 * g + i] = (y * slope_ref[2 * g + i]).astype(BF16)
     for i in range(2):
         kept_ref[i] = grad_ref[i]
@@ -537,7 +523,7 @@
         for i in range(2):
             flat_ref[part, pl.ds(2 * pair + i, half, stride=rows), :] = plane[i * half : (i + 1) * half]
 
-    lax.fori_loop(0, inn_hbm.shape[0], give, 0)
+    lax.fori_loop(0, inn_hbm.shape[0], give, 0, unroll=inn_hbm.shape[0] <= 8)
     backward_taps(w3_ref, w4_ref, kin_ref, kout_ref)
     for part in range(parts):
         for g in range((rows - 4) // 2):
@@ -646,15 +632,14 @@
     own_taps = shape((4 * c, 3 * c), BF16)
     kept_shape = shape((4, wide, c), BF16)
     four_rows, most_rows, all_rows = VMEM((4, wide, c), BF16), VMEM((rows - 2, wide, c), BF16), VMEM((rows, wide, c), BF16)
-    most_slopes = VMEM((rows - 2, wide, c), F32)
     keep = lambda dims, dtype: VMEM(dims.shape, dtype)
 
     beside, mine = exchanged(x, tail)
     slope_middle, kept, den_middle = call(
         forward_middle_kernel,
-        [(shape((rows - 2, wide, c), F32), HBM), (kept_shape, VMEM), (shape((rows - 4, width, c), BF16), VMEM)],
+        [(shape((rows - 2, wide, c), F32), VMEM), (kept_shape, VMEM), (shape((rows - 4, width, c), BF16), VMEM)],
         [VMEM] * 5,
-        [all_rows, most_rows, keep(taps, BF16), keep(taps, BF16), most_slopes, pltpu.SemaphoreType.DMA],
+        [all_rows, most_rows, keep(taps, BF16), keep(taps, BF16)],
     )(x, beside, kernel_in, kernel_out, bias)
     (block,) = call(join_kernel, [(shape((lats, *piece), BF16), VMEM)], [VMEM] * lats, [])(*pieces)
     mine, block, kept, slope_middle, den_middle = lax.optimization_barrier((mine, block, kept, slope_middle, den_middle))
@@ -695,15 +680,8 @@
     kept, out_middle = call(
         backward_middle_kernel,
         [(kept_shape, VMEM), (shape(((rows - 4) // 2, parts, c, 128), F32), VMEM)],
-        [VMEM] * 5 + [HBM],
-        [
-            all_rows,
-            most_rows,
-            keep(taps, BF16),
-            keep(own_taps, BF16),
-            most_slopes,
-            pltpu.SemaphoreType.DMA(((rows - 2) // 2,)),
-        ],
+        [VMEM] * 6,
+        [all_rows, most_rows, keep(taps, BF16), keep(own_taps, BF16)],
     )(g, beside, kernel_in, kernel_out, base, slope_middle)
     mine, kept, out_middle = lax.optimization_barrier((mine, kept, out_middle))
     others = swapped(mine)

time: 48.5 us -> 47.3 us (0.975)
  Pallas kernels: 12.9 us -> 10.3 us
  starting transfers between devices: 20 us -> 21.5 us
    pallas_call x11, Pallas kernels: 12.9 us -> 10.3 us  [apply(): run(*(pltpu.with_memory_space_constraint(a, space) if space in (VMEM, HBM...]
    ppermute x4, starting transfers between devices: 4.05 us -> 5.53 us  [swapped(): return lax.ppermute(value, 'ch', [(0, 1), (1, 0)])]
  transfers between devices with their start and end apart: 14 -> 14, of which waited for: 9 -> 9; matrix products, arithmetic and copies ran while one was open for 0% -> 0% of each run, Pallas kernels for 17% -> 13%
where the time goes in v3:
time: 47.3 us; the launch traced here: 47.1 us
  starting transfers between devices  21.5 us (45%)
  waiting for transfers between devices  13.9 us (29%)
  Pallas kernels  10.3 us (22%)
  between operations  0.77 us (2%)
  local copies, waits for them, and re-layouts  0.64 us (1%)
    ppermute x6, starting transfers between devices, sent(): lax.ppermute(pieces[k], 'lat', [(i, i ^ k) for i in range(lats)])  10.6 us
    pallas_call x11, Pallas kernels, apply(): run(*(pltpu.with_memory_space_constraint(a, space) if space in (VMEM, HBM...  10.3 us
    ppermute x6, waiting for transfers between devices, sent(): lax.ppermute(pieces[k], 'lat', [(i, i ^ k) for i in range(lats)])  9.68 us
    ppermute x4, starting transfers between devices, swapped(): return lax.ppermute(value, 'ch', [(0, 1), (1, 0)])  5.53 us
    ppermute x2, starting transfers between devices, move(): return lax.ppermute(value, ('lon', 'ch'), pairs)  3.94 us
    ppermute x2, waiting for transfers between devices, move(): return lax.ppermute(value, ('lon', 'ch'), pairs)  3.77 us
    ppermute x2, starting transfers between devices, from_row_neighbour(): return lax.ppermute(value, ('lat', 'ch'), pairs)  1.47 us
  transfers between devices with their start and end apart: 14, of which 9 were waited for; matrix products, arithmetic and copies ran while one was open for 0% of the time, Pallas kernels for 13%

profile of v3, /device:TPU:0, one launch (start us, length us, event | category | flops | bytes accessed | tf_op | source)
XLA Modules:
  0.0 47.1 jit_solution(12523422845849938171)
XLA Ops:
  0.6 0.6 %collective-permute-start = (bf16[64,8,256]{2,1,0:T(8,128)(2,1)}, bf16[64,8,256]{2,1,0:T(8,128)(2,1)S(1)}, u32[]{:S(2)}, u32[]{:S(2)}) collective-permute-start(bf16[64,8,256]{2,1,0:T(8,128)(2,1)} %noisy_hbm.1), channel_id=1, source_target_pairs={{0,1},{1,0},{2,3},{3,2},{4,5},{5,4},{6,7},{7,6},{8,9},{9,8},{10,11... | collective-permute-start | bytes 786440 | tf_op jit(solution)/shard_map/ppermute | solution.py:548
  1.2 1.1 %shard_map.113 = (bf16[64,8,256]{2,1,0:T(8,128)(2,1)S(1)}, f32[4,128]{1,0:T(4,128)S(1)}, bf16[272,128]{1,0:T(8,128)(2,1)S(1)}, bf16[272,128]{1,0:T(8,128)(2,1)S(...) custom-call(s32[4]{0:T(128)} %dest_hbm.1, s32[4]{0:T(128)} %row_hbm.1, s32[4]{0:T(128)} %col_hbm.1, ...), custom_call_target="tpu_custom_call" | custom-call | tf_op jit(solution)/shard_map/pallas_call | solution.py:41
  2.3 0.2 collective-permute-done.other_ref
  2.6 0.3 shard_map.114
  2.9 2.7 %collective-permute-start.1 = (bf16[8,16,128]{2,1,0:T(8,128)(2,1)S(1)}, bf16[8,16,128]{2,1,0:T(8,128)(2,1)S(1)}, u32[]{:S(2)}, u32[]{:S(2)}) collective-permute-start(bf16[8,16,128]{2,1,0:T(8,128)(2,1)S(1)} %get-tuple-element.37), channel_id=1, source_target_pairs={{0,3},{1,2},{2,1},{3,0},{4,7},{5,6},{6,5},{7,4},{8,11},{9,10},{10,... | collective-permute-start | bytes 98312 | tf_op jit(solution)/shard_map/ppermute | solution.py:565
  5.5 1.6 %collective-permute-done.1.tail_ref = bf16[8,16,128]{2,1,0:T(8,128)(2,1)S(1)} collective-permute-done((bf16[8,16,128]{2,1,0:T(8,128)(2,1)S(1)}, bf16[8,16,128]{2,1,0:T(8,128)(2,1)S(1)}, u32[]{:S(2)}, u32[]{:S(2)}) %collective-permute-start.1) | collective-permute-done | bytes 32800 | tf_op jit(solution)/shard_map/ppermute | solution.py:565
  7.1 0.0 copy-start.1
  7.2 0.0 copy-start
  7.2 0.8 %collective-permute-start.2 = (bf16[2,272,128]{2,1,0:T(8,128)(2,1)S(1)}, bf16[2,272,128]{2,1,0:T(8,128)(2,1)S(1)}, u32[]{:S(2)}, u32[]{:S(2)}) collective-permute-start(bf16[2,272,128]{2,1,0:T(8,128)(2,1)S(1)} %shard_map.115), channel_id=1, source_target_pairs={{1,4},{4,1},{5,8},{8,5},{9,12},{12,9},{3,6},{6,3},{7,10},{10,7},{1... | collective-permute-start | bytes 417800 | tf_op jit(solution)/shard_map/ppermute | solution.py:557
  8.0 3.4 %collective-permute-start.3 = (bf16[272,128]{1,0:T(8,128)(2,1)S(1)}, bf16[272,128]{1,0:T(8,128)(2,1)S(1)}, u32[]{:S(2)}, u32[]{:S(2)}) collective-permute-start(bf16[272,128]{1,0:T(8,128)(2,1)S(1)} %get-tuple-element.39), channel_id=1, source_target_pairs={{0,4},{4,0},{8,12},{12,8},{1,5},{5,1},{9,13},{13,9},{2,6},{6,2},{1... | collective-permute-start | bytes 208904 | tf_op jit(solution)/shard_map/ppermute | solution.py:124
  11.4 2.8 %collective-permute-start.4 = (bf16[272,128]{1,0:T(8,128)(2,1)S(1)}, bf16[272,128]{1,0:T(8,128)(2,1)S(1)}, u32[]{:S(2)}, u32[]{:S(2)}) collective-permute-start(bf16[272,128]{1,0:T(8,128)(2,1)S(1)} %get-tuple-element.40), channel_id=1, source_target_pairs={{0,8},{4,12},{8,0},{12,4},{1,9},{5,13},{9,1},{13,5},{2,10},{6,14},... | collective-permute-start | bytes 208904 | tf_op jit(solution)/shard_map/ppermute | solution.py:124
  14.2 0.0 collective-permute-start.5
  14.2 1.7 %collective-permute-done.3.refs_1_ = bf16[272,128]{1,0:T(8,128)(2,1)S(1)} collective-permute-done((bf16[272,128]{1,0:T(8,128)(2,1)S(1)}, bf16[272,128]{1,0:T(8,128)(2,1)S(1)}, u32[]{:S(2)}, u32[]{:S(2)}) %collective-permute-start.3) | collective-permute-done | bytes 69664 | tf_op jit(solution)/shard_map/ppermute | solution.py:124
  15.8 1.1 %collective-permute-done.4.refs_2_ = bf16[272,128]{1,0:T(8,128)(2,1)S(1)} collective-permute-done((bf16[272,128]{1,0:T(8,128)(2,1)S(1)}, bf16[272,128]{1,0:T(8,128)(2,1)S(1)}, u32[]{:S(2)}, u32[]{:S(2)}) %collective-permute-start.4) | collective-permute-done | bytes 69664 | tf_op jit(solution)/shard_map/ppermute | solution.py:124
  16.9 4.2 %collective-permute-done.5.refs_3_ = bf16[272,128]{1,0:T(8,128)(2,1)S(1)} collective-permute-done((bf16[272,128]{1,0:T(8,128)(2,1)S(1)}, bf16[272,128]{1,0:T(8,128)(2,1)S(1)}, u32[]{:S(2)}, u32[]{:S(2)}) %collective-permute-start.5) | collective-permute-done | bytes 69664 | tf_op jit(solution)/shard_map/ppermute | solution.py:124
  21.2 0.0 copy-start.2
  21.2 0.0 copy-done.1
  21.2 0.0 copy-done
  21.2 0.6 %copy-done.2 = f32[128]{0:T(128)S(1)} copy-done((f32[128]{0:T(128)S(1)}, f32[128]{0:T(128)}, u32[]{:S(2)}) %copy-start.2) | copy-done | bytes 536
  21.8 1.6 %shard_map.117 = (f32[6,272,128]{2,1,0:T(8,128)S(1)}, bf16[4,272,128]{2,1,0:T(8,128)(2,1)S(1)}, bf16[4,256,128]{2,1,0:T(8,128)(2,1)S(1)}) custom-call(bf16[8,256,128]{2,1,0:T(8,128)(2,1)S(1)} %get-tuple-element.36.x_ref, bf16[8,16,128]{2,1,0:T(8,128)(2,1)S(1)} %collective-permute-done.1.tail_ref, bf16[3,3,128,128]{3,2,1,0:T(8,128)(2,1)S(1)} %copy-done, ...), custom_call_target="tpu_custom_call" | custom-call | tf_op jit(solution)/shard_map/pallas_call | solution.py:41
  23.5 0.0 collective-permute-done.2.halo_ref
  23.5 0.1 collective-permute-start.7
  23.6 0.5 %collective-permute-start.6 = (bf16[2,272,128]{2,1,0:T(8,128)(2,1)S(1)}, bf16[2,272,128]{2,1,0:T(8,128)(2,1)S(1)}, u32[]{:S(2)}, u32[]{:S(2)}) collective-permute-start(bf16[2,272,128]{2,1,0:T(8,128)(2,1)S(1)} %collective-permute-done.2.halo_ref), channel_id=1, source_target_pairs={{0,1},{1,0},{2,3},{3,2},{4,5},{5,4},{6,7},{7,6},{8,9},{9,8},{10,11... | collective-permute-start | bytes 417800 | tf_op jit(solution)/shard_map/ppermute | solution.py:548
  24.1 1.1 %shard_map.118 = (f32[2,272,128]{2,1,0:T(8,128)S(1)}, bf16[2,256,128]{2,1,0:T(8,128)(2,1)S(1)}, bf16[512,768]{1,0:T(8,128)(2,1)S(1)}, bf16[512,768]{1,0:T(8,128)(2,1)S(1)}) custom-call(bf16[8,256,128]{2,1,0:T(8,128)(2,1)S(1)} %get-tuple-element.36.x_ref, bf16[8,16,128]{2,1,0:T(8,128)(2,1)S(1)} %collective-permute-done.1.tail_ref, ...), custom_call_target="tpu_custom_call" | custom-call | tf_op jit(solution)/shard_map/pallas_call | solution.py:41
  25.1 0.2 collective-permute-done.6.halo_ref
  25.3 0.0 collective-permute-done.7.other_block_ref
  25.3 2.0 %shard_map.119 = (f32[2,272,128]{2,1,0:T(8,128)S(1)}, f32[4,256,128]{2,1,0:T(8,128)S(1)}, bf16[8,256,128]{2,1,0:T(8,128)(2,1)S(1)}, bf16[8,16,128]{2,1,0:T(8,128...) custom-call(bf16[8,256,128]{2,1,0:T(8,128)(2,1)S(1)} %get-tuple-elem, ...), custom_call_target="tpu_custom_call", output_to_operand_aliasing={{2}: (0, {}), {3}: (1, {})} | custom-call | tf_op jit(solution)/shard_map/pallas_call | solution.py:41
  27.3 1.3 %collective-permute-start.8 = (bf16[8,16,128]{2,1,0:T(8,128)(2,1)S(1)}, bf16[8,16,128]{2,1,0:T(8,128)(2,1)S(1)}, u32[]{:S(2)}, u32[]{:S(2)}) collective-permute-start(bf16[8,16,128]{2,1,0:T(8,128)(2,1)S(1)} %get-tuple-element.53), channel_id=1, source_target_pairs={{0,3},{1,2},{2,1},{3,0},{4,7},{5,6},{6,5},{7,4},{8,11},{9,10},{10,... | collective-permute-start | bytes 98312 | tf_op jit(solution)/shard_map/ppermute | solution.py:565
  28.6 2.2 %collective-permute-done.8.tail_ref = bf16[8,16,128]{2,1,0:T(8,128)(2,1)S(1)} collective-permute-done((bf16[8,16,128]{2,1,0:T(8,128)(2,1)S(1)}, bf16[8,16,128]{2,1,0:T(8,128)(2,1)S(1)}, u32[]{:S(2)}, u32[]{:S(2)}) %collective-permute-start.8) | collective-permute-done | bytes 32800 | tf_op jit(solution)/shard_map/ppermute | solution.py:565
  30.8 0.7 %collective-permute-start.9 = (bf16[2,272,128]{2,1,0:T(8,128)(2,1)S(1)}, bf16[2,272,128]{2,1,0:T(8,128)(2,1)S(1)}, u32[]{:S(2)}, u32[]{:S(2)}) collective-permute-start(bf16[2,272,128]{2,1,0:T(8,128)(2,1)S(1)} %shard_map.120), channel_id=1, source_target_pairs={{1,4},{4,1},{5,8},{8,5},{9,12},{12,9},{3,6},{6,3},{7,10},{10,7},{1... | collective-permute-start | bytes 417800 | tf_op jit(solution)/shard_map/ppermute | solution.py:557
  31.5 1.4 %shard_map.121 = (bf16[4,272,128]{2,1,0:T(8,128)(2,1)S(1)}, f32[2,2,128,128]{3,2,1,0:T(8,128)S(1)}) custom-call(bf16[8,256,128]{2,1,0:T(8,128)(2,1)S(1)} %get-tuple-element.52.x_ref, bf16[8,16,128]{2,1,0:T(8,128)(2,1)S(1)} %collective-permute-done.8.tail_ref, bf16[3,3,128,128]{3,2,1,0:T(8,128)(2,1)S(1)} %copy-done, bf16[3,3,128,128]{3,2,1,0:T(8,128)(2,1)S(1)} %copy-done.1, ...), custom_call_target="tpu_custom_call" | custom-call | tf_op jit(solution)/shard_map/pallas_call | solution.py:41
  32.9 0.0 collective-permute-done.9.halo_ref
  32.9 4.4 %collective-permute-start.10 = (bf16[2,272,128]{2,1,0:T(8,128)(2,1)S(1)}, bf16[2,272,128]{2,1,0:T(8,128)(2,1)S(1)}, u32[]{:S(2)}, u32[]{:S(2)}) collective-permute-start(bf16[2,272,128]{2,1,0:T(8,128)(2,1)S(1)} %collective-permute-done.9.halo_ref), channel_id=1, source_target_pairs={{0,1},{1,0},{2,3},{3,2},{4,5},{5,4},{6,7},{7,6},{8,9},{9,8},{10,11... | collective-permute-start | bytes 417800 | tf_op jit(solution)/shard_map/ppermute | solution.py:548
  37.3 1.5 %collective-permute-start.11 = (bf16[2,64,128]{2,1,0:T(8,128)(2,1)S(1)}, bf16[2,64,128]{2,1,0:T(8,128)(2,1)S(1)}, u32[]{:S(2)}, u32[]{:S(2)}) collective-permute-start(bf16[2,64,128]{2,1,0:T(8,128)(2,1)S(1)} %get-tuple-element.65), channel_id=1, source_target_pairs={{0,4},{4,0},{8,12},{12,8},{1,5},{5,1},{9,13},{13,9},{2,6},{6,2},{1... | collective-permute-start | bytes 98312 | tf_op jit(solution)/shard_map/ppermute | solution.py:124
  38.8 0.7 %collective-permute-start.12 = (bf16[2,64,128]{2,1,0:T(8,128)(2,1)S(1)}, bf16[2,64,128]{2,1,0:T(8,128)(2,1)S(1)}, u32[]{:S(2)}, u32[]{:S(2)}) collective-permute-start(bf16[2,64,128]{2,1,0:T(8,128)(2,1)S(1)} %get-tuple-element.66), channel_id=1, source_target_pairs={{0,8},{4,12},{8,0},{12,4},{1,9},{5,13},{9,1},{13,5},{2,10},{6,14},... | collective-permute-start | bytes 98312 | tf_op jit(solution)/shard_map/ppermute | solution.py:124
  39.5 2.2 %collective-permute-start.13 = (bf16[2,64,128]{2,1,0:T(8,128)(2,1)S(1)}, bf16[2,64,128]{2,1,0:T(8,128)(2,1)S(1)}, u32[]{:S(2)}, u32[]{:S(2)}) collective-permute-start(bf16[2,64,128]{2,1,0:T(8,128)(2,1)S(1)} %get-tuple-element.67), channel_id=1, source_target_pairs={{0,12},{4,8},{8,4},{12,0},{1,13},{5,9},{9,5},{13,1},{2,14},{6,10},... | collective-permute-start | bytes 98312 | tf_op jit(solution)/shard_map/ppermute | solution.py:124
  41.7 0.9 %shard_map.122.out_own_ref = f32[2,128,128]{2,1,0:T(8,128)S(1)} custom-call(bf16[8,256,128]{2,1,0:T(8,128)(2,1)S(1)} %get-tuple-element.52.x_ref, bf16[8,16,128]{2,1,0:T(8,128)(2,1)S(1)} %collective-permute-done.8.tail_ref, bf16[2,272,128]{2,1,0:T(8,128)(2,1)S(1)} %collective-permute-done.9.halo_ref, bf16[4,272,128]{2,1,0:T(8,128)(2,1)S(1)} %get-tuple-element.59.kept_ref, ...), custom_call_target="tpu_custom_call" | custom-call | tf_op jit(solution)/shard_map/pallas_call | solution.py:41
  42.6 0.0 collective-permute-done.11.refs_1_
  42.6 2.0 %collective-permute-done.12.refs_2_ = bf16[2,64,128]{2,1,0:T(8,128)(2,1)S(1)} collective-permute-done((bf16[2,64,128]{2,1,0:T(8,128)(2,1)S(1)}, bf16[2,64,128]{2,1,0:T(8,128)(2,1)S(1)}, u32[]{:S(2)}, u32[]{:S(2)}) %collective-permute-start.12) | collective-permute-done | bytes 32800 | tf_op jit(solution)/shard_map/ppermute | solution.py:124
  44.6 0.7 %collective-permute-done.13.refs_3_ = bf16[2,64,128]{2,1,0:T(8,128)(2,1)S(1)} collective-permute-done((bf16[2,64,128]{2,1,0:T(8,128)(2,1)S(1)}, bf16[2,64,128]{2,1,0:T(8,128)(2,1)S(1)}, u32[]{:S(2)}, u32[]{:S(2)}) %collective-permute-start.13) | collective-permute-done | bytes 32800 | tf_op jit(solution)/shard_map/ppermute | solution.py:124
  45.3 0.0 collective-permute-done.10.halo_ref
  45.3 1.8 %shard_map.123 = (f32[64,8,256]{2,1,0:T(8,128)}, bf16[4,64,128]{2,1,0:T(8,128)(2,1)}) custom-call(bf16[8,256,128]{2,1,0:T(8,128)(2,1)S(1)} %get-tuple-element.52.x_ref, bf16[8,16,128]{2,1,0:T(8,128)(2,1)S(1)} %collective-permute-done.8.tail_ref, bf16[2,272,128]{2,1,0:T(8,128)(2,1)S(1)} %collective-permute-done.10.halo_ref, ...), custom_call_target="tpu_custom_call" | custom-call | tf_op jit(solution)/shard_map/pallas_call | solution.py:41
  (3 shorter events, 0.0 us)
Async XLA Ops:
  0.6 1.9 %collective-permute-start = (bf16[64,8,256]{2,1,0:T(8,128)(2,1)}, bf16[64,8,256]{2,1,0:T(8,128)(2,1)S(1)}, u32[]{:S(2)}, u32[]{:S(2)}) collective-permute-start(bf16[64,8,256]{2,1,0:T(8,128)(2,1)} %noisy_hbm.1), channel_id=1, source_target_pairs={{0,1},{1,0},{2,3},{3,2},{4,5},{5,4},{6,7},{7,6},{8,9},{9,8},{10,11... | collective-permute-start | bytes 786440 | tf_op jit(solution)/shard_map/ppermute | solution.py:548
  2.9 4.3 %collective-permute-start.1 = (bf16[8,16,128]{2,1,0:T(8,128)(2,1)S(1)}, bf16[8,16,128]{2,1,0:T(8,128)(2,1)S(1)}, u32[]{:S(2)}, u32[]{:S(2)}) collective-permute-start(bf16[8,16,128]{2,1,0:T(8,128)(2,1)S(1)} %get-tuple-element.37), channel_id=1, source_target_pairs={{0,3},{1,2},{2,1},{3,0},{4,7},{5,6},{6,5},{7,4},{8,11},{9,10},{10,... | collective-permute-start | bytes 98312 | tf_op jit(solution)/shard_map/ppermute | solution.py:565
  7.1 14.0 %copy-start.1 = (bf16[3,3,128,128]{3,2,1,0:T(8,128)(2,1)S(1)}, bf16[3,3,128,128]{3,2,1,0:T(8,128)(2,1)}, u32[]{:S(2)}) copy-start(bf16[3,3,128,128]{3,2,1,0:T(8,128)(2,1)} %kout_ref.9) | copy-start | bytes 884740
  7.2 14.0 %copy-start = (bf16[3,3,128,128]{3,2,1,0:T(8,128)(2,1)S(1)}, bf16[3,3,128,128]{3,2,1,0:T(8,128)(2,1)}, u32[]{:S(2)}) copy-start(bf16[3,3,128,128]{3,2,1,0:T(8,128)(2,1)} %kin_ref.9) | copy-start | bytes 884740
  7.2 16.3 %collective-permute-start.2 = (bf16[2,272,128]{2,1,0:T(8,128)(2,1)S(1)}, bf16[2,272,128]{2,1,0:T(8,128)(2,1)S(1)}, u32[]{:S(2)}, u32[]{:S(2)}) collective-permute-start(bf16[2,272,128]{2,1,0:T(8,128)(2,1)S(1)} %shard_map.115), channel_id=1, source_target_pairs={{1,4},{4,1},{5,8},{8,5},{9,12},{12,9},{3,6},{6,3},{7,10},{10,7},{1... | collective-permute-start | bytes 417800 | tf_op jit(solution)/shard_map/ppermute | solution.py:557
  8.0 7.9 %collective-permute-start.3 = (bf16[272,128]{1,0:T(8,128)(2,1)S(1)}, bf16[272,128]{1,0:T(8,128)(2,1)S(1)}, u32[]{:S(2)}, u32[]{:S(2)}) collective-permute-start(bf16[272,128]{1,0:T(8,128)(2,1)S(1)} %get-tuple-element.39), channel_id=1, source_target_pairs={{0,4},{4,0},{8,12},{12,8},{1,5},{5,1},{9,13},{13,9},{2,6},{6,2},{1... | collective-permute-start | bytes 208904 | tf_op jit(solution)/shard_map/ppermute | solution.py:124
  11.4 5.5 %collective-permute-start.4 = (bf16[272,128]{1,0:T(8,128)(2,1)S(1)}, bf16[272,128]{1,0:T(8,128)(2,1)S(1)}, u32[]{:S(2)}, u32[]{:S(2)}) collective-permute-start(bf16[272,128]{1,0:T(8,128)(2,1)S(1)} %get-tuple-element.40), channel_id=1, source_target_pairs={{0,8},{4,12},{8,0},{12,4},{1,9},{5,13},{9,1},{13,5},{2,10},{6,14},... | collective-permute-start | bytes 208904 | tf_op jit(solution)/shard_map/ppermute | solution.py:124
  14.2 7.0 %collective-permute-start.5 = (bf16[272,128]{1,0:T(8,128)(2,1)S(1)}, bf16[272,128]{1,0:T(8,128)(2,1)S(1)}, u32[]{:S(2)}, u32[]{:S(2)}) collective-permute-start(bf16[272,128]{1,0:T(8,128)(2,1)S(1)} %get-tuple-element.41), channel_id=1, source_target_pairs={{0,12},{4,8},{8,4},{12,0},{1,13},{5,9},{9,5},{13,1},{2,14},{6,10},... | collective-permute-start | bytes 208904 | tf_op jit(solution)/shard_map/ppermute | solution.py:124
  21.2 0.7 %copy-start.2 = (f32[128]{0:T(128)S(1)}, f32[128]{0:T(128)}, u32[]{:S(2)}) copy-start(f32[128]{0:T(128)} %param.12) | copy-start | bytes 1540
  23.5 1.8 %collective-permute-start.7 = (bf16[4,272,128]{2,1,0:T(8,128)(2,1)S(1)}, bf16[4,272,128]{2,1,0:T(8,128)(2,1)S(1)}, u32[]{:S(2)}, u32[]{:S(2)}) collective-permute-start(bf16[4,272,128]{2,1,0:T(8,128)(2,1)S(1)} %shard_map.116.block_ref), channel_id=1, source_target_pairs={{0,1},{1,0},{2,3},{3,2},{4,5},{5,4},{6,7},{7,6},{8,9},{9,8},{10,11... | collective-permute-start | bytes 835592 | tf_op jit(solution)/shard_map/ppermute | solution.py:548
  23.6 1.7 %collective-permute-start.6 = (bf16[2,272,128]{2,1,0:T(8,128)(2,1)S(1)}, bf16[2,272,128]{2,1,0:T(8,128)(2,1)S(1)}, u32[]{:S(2)}, u32[]{:S(2)}) collective-permute-start(bf16[2,272,128]{2,1,0:T(8,128)(2,1)S(1)} %collective-permute-done.2.halo_ref), channel_id=1, source_target_pairs={{0,1},{1,0},{2,3},{3,2},{4,5},{5,4},{6,7},{7,6},{8,9},{9,8},{10,11... | collective-permute-start | bytes 417800 | tf_op jit(solution)/shard_map/ppermute | solution.py:548
  27.3 3.5 %collective-permute-start.8 = (bf16[8,16,128]{2,1,0:T(8,128)(2,1)S(1)}, bf16[8,16,128]{2,1,0:T(8,128)(2,1)S(1)}, u32[]{:S(2)}, u32[]{:S(2)}) collective-permute-start(bf16[8,16,128]{2,1,0:T(8,128)(2,1)S(1)} %get-tuple-element.53), channel_id=1, source_target_pairs={{0,3},{1,2},{2,1},{3,0},{4,7},{5,6},{6,5},{7,4},{8,11},{9,10},{10,... | collective-permute-start | bytes 98312 | tf_op jit(solution)/shard_map/ppermute | solution.py:565
  30.8 2.1 %collective-permute-start.9 = (bf16[2,272,128]{2,1,0:T(8,128)(2,1)S(1)}, bf16[2,272,128]{2,1,0:T(8,128)(2,1)S(1)}, u32[]{:S(2)}, u32[]{:S(2)}) collective-permute-start(bf16[2,272,128]{2,1,0:T(8,128)(2,1)S(1)} %shard_map.120), channel_id=1, source_target_pairs={{1,4},{4,1},{5,8},{8,5},{9,12},{12,9},{3,6},{6,3},{7,10},{10,7},{1... | collective-permute-start | bytes 417800 | tf_op jit(solution)/shard_map/ppermute | solution.py:557
  32.9 12.4 %collective-permute-start.10 = (bf16[2,272,128]{2,1,0:T(8,128)(2,1)S(1)}, bf16[2,272,128]{2,1,0:T(8,128)(2,1)S(1)}, u32[]{:S(2)}, u32[]{:S(2)}) collective-permute-start(bf16[2,272,128]{2,1,0:T(8,128)(2,1)S(1)} %collective-permute-done.9.halo_ref), channel_id=1, source_target_pairs={{0,1},{1,0},{2,3},{3,2},{4,5},{5,4},{6,7},{7,6},{8,9},{9,8},{10,11... | collective-permute-start | bytes 417800 | tf_op jit(solution)/shard_map/ppermute | solution.py:548
  37.3 5.3 %collective-permute-start.11 = (bf16[2,64,128]{2,1,0:T(8,128)(2,1)S(1)}, bf16[2,64,128]{2,1,0:T(8,128)(2,1)S(1)}, u32[]{:S(2)}, u32[]{:S(2)}) collective-permute-start(bf16[2,64,128]{2,1,0:T(8,128)(2,1)S(1)} %get-tuple-element.65), channel_id=1, source_target_pairs={{0,4},{4,0},{8,12},{12,8},{1,5},{5,1},{9,13},{13,9},{2,6},{6,2},{1... | collective-permute-start | bytes 98312 | tf_op jit(solution)/shard_map/ppermute | solution.py:124
  38.8 5.8 %collective-permute-start.12 = (bf16[2,64,128]{2,1,0:T(8,128)(2,1)S(1)}, bf16[2,64,128]{2,1,0:T(8,128)(2,1)S(1)}, u32[]{:S(2)}, u32[]{:S(2)}) collective-permute-start(bf16[2,64,128]{2,1,0:T(8,128)(2,1)S(1)} %get-tuple-element.66), channel_id=1, source_target_pairs={{0,8},{4,12},{8,0},{12,4},{1,9},{5,13},{9,1},{13,5},{2,10},{6,14},... | collective-permute-start | bytes 98312 | tf_op jit(solution)/shard_map/ppermute | solution.py:124
  39.5 5.8 %collective-permute-start.13 = (bf16[2,64,128]{2,1,0:T(8,128)(2,1)S(1)}, bf16[2,64,128]{2,1,0:T(8,128)(2,1)S(1)}, u32[]{:S(2)}, u32[]{:S(2)}) collective-permute-start(bf16[2,64,128]{2,1,0:T(8,128)(2,1)S(1)} %get-tuple-element.67), channel_id=1, source_target_pairs={{0,12},{4,8},{8,4},{12,0},{1,13},{5,9},{9,5},{13,1},{2,14},{6,10},... | collective-permute-start | bytes 98312 | tf_op jit(solution)/shard_map/ppermute | solution.py:124

commit v4 on v3

--- a/solution.py
+++ b/solution.py
@@ -282,10 +282,10 @@
     slope_ref,
     kept_ref,
     den_ref,
+    w1_ref,
+    w2_ref,
     ext_ref,
     hidden_ref,
-    w1_ref,
-    w2_ref,
 ):
     rows, width, _ = x_ref.shape
     forward_taps(w1_ref, w2_ref, kin_ref, kout_ref)
@@ -322,9 +322,8 @@
 
 
 def forward_own_kernel(
-    x_ref, tail_ref, halo_ref, kept_ref, kin_ref, kout_ref, bias_ref, slope_ref, den_ref, w1_ref, w2_ref, ext_ref, between_ref
+    x_ref, tail_ref, halo_ref, kept_ref, w1_ref, w2_ref, bias_ref, slope_ref, den_ref, ext_ref, between_ref
 ):
-    forward_taps(w1_ref, w2_ref, kin_ref, kout_ref)
     core = lax.axis_index("ch")
     den = forward_end(
         core, x_ref, tail_ref, halo_ref, kept_ref, w1_ref, w2_ref, bias_ref, slope_ref, ext_ref, between_ref
@@ -443,10 +442,10 @@
     slope_ref,
     kept_ref,
     out_ref,
+    w3_ref,
+    w4_ref,
     ext_ref,
     grad_ref,
-    w3_ref,
-    w4_ref,
 ):
     rows = x_ref.shape[0]
     backward_taps(w3_ref, w4_ref, kin_ref, kout_ref)
@@ -475,9 +474,8 @@
 
 
 def backward_own_kernel(
-    x_ref, tail_ref, halo_ref, kept_ref, kin_ref, kout_ref, base_ref, slope_ref, out_ref, ext_ref, between_ref, w3_ref, w4_ref
+    x_ref, tail_ref, halo_ref, kept_ref, w3_ref, w4_ref, base_ref, slope_ref, out_ref, ext_ref, between_ref
 ):
-    backward_taps(w3_ref, w4_ref, kin_ref, kout_ref)
     planes = backward_end(
         lax.axis_index("ch"), x_ref, tail_ref, halo_ref, kept_ref, w3_ref, w4_ref, base_ref, slope_ref, ext_ref, between_ref
     )
@@ -490,8 +488,8 @@
     tail_ref,
     halo_ref,
     kept_ref,
-    kin_ref,
-    kout_ref,
+    w3_ref,
+    w4_ref,
     base_ref,
     slope_ref,
     out_middle_ref,
@@ -499,7 +497,7 @@
     code_ref,
     *refs,
 ):
-    *back_refs, next_hbm, inn_hbm, ext_ref, between_ref, flat_ref, w3_ref, w4_ref, next_sems, inn_sems = refs
+    *back_refs, next_hbm, inn_hbm, ext_ref, between_ref, flat_ref, next_sems, inn_sems = refs
     core = lax.axis_index("ch")
     rows = x_ref.shape[0]
     half = next_hbm.shape[0]
@@ -524,7 +522,6 @@
             flat_ref[part, pl.ds(2 * pair + i, half, stride=rows), :] = plane[i * half : (i + 1) * half]
 
     lax.fori_loop(0, inn_hbm.shape[0], give, 0, unroll=inn_hbm.shape[0] <= 8)
-    backward_taps(w3_ref, w4_ref, kin_ref, kout_ref)
     for part in range(parts):
         for g in range((rows - 4) // 2):
             put(1 + g, part, out_middle_ref[g, part])
@@ -632,24 +629,28 @@
     own_taps = shape((4 * c, 3 * c), BF16)
     kept_shape = shape((4, wide, c), BF16)
     four_rows, most_rows, all_rows = VMEM((4, wide, c), BF16), VMEM((rows - 2, wide, c), BF16), VMEM((rows, wide, c), BF16)
-    keep = lambda dims, dtype: VMEM(dims.shape, dtype)
 
     beside, mine = exchanged(x, tail)
-    slope_middle, kept, den_middle = call(
+    slope_middle, kept, den_middle, w1, w2 = call(
         forward_middle_kernel,
-        [(shape((rows - 2, wide, c), F32), VMEM), (kept_shape, VMEM), (shape((rows - 4, width, c), BF16), VMEM)],
+        [
+            (shape((rows - 2, wide, c), F32), VMEM),
+            (kept_shape, VMEM),
+            (shape((rows - 4, width, c), BF16), VMEM),
+            (taps, VMEM),
+            (taps, VMEM),
+        ],
         [VMEM] * 5,
-        [all_rows, most_rows, keep(taps, BF16), keep(taps, BF16)],
+        [all_rows, most_rows],
     )(x, beside, kernel_in, kernel_out, bias)
+    pieces, kept = lax.optimization_barrier((pieces, kept))
     (block,) = call(join_kernel, [(shape((lats, *piece), BF16), VMEM)], [VMEM] * lats, [])(*pieces)
-    mine, block, kept, slope_middle, den_middle = lax.optimization_barrier((mine, block, kept, slope_middle, den_middle))
+    other_block = swapped(block)
+    mine, kept, slope_middle, den_middle = lax.optimization_barrier((mine, kept, slope_middle, den_middle))
     others = swapped(mine)
-    slope_own, den_own, w1, w2 = call(
-        forward_own_kernel,
-        [(pair, VMEM), (shape((2, width, c), BF16), VMEM), (taps, VMEM), (taps, VMEM)],
-        [VMEM] * 7,
-        [four_rows, four_rows],
-    )(x, beside, mine, kept, kernel_in, kernel_out, bias)
+    slope_own, den_own = call(
+        forward_own_kernel, [(pair, VMEM), (shape((2, width, c), BF16), VMEM)], [VMEM] * 7, [four_rows, four_rows]
+    )(x, beside, mine, kept, w1, w2, bias)
     slope_other, base, g, tail, *inn = call(
         forward_kernel,
         [
@@ -672,25 +673,27 @@
             SMEM((slots,), jnp.int32),
         ],
         {0: 2, 1: 3},
-    )(x, beside, others, kept, w1, w2, bias, den_middle, den_own, block, swapped(block))
+    )(x, beside, others, kept, w1, w2, bias, den_middle, den_own, block, other_block)
 
     back = sent(inn)
     beside, mine = exchanged(g, tail)
     parts = width // 128
-    kept, out_middle = call(
+    kept, out_middle, w3, w4 = call(
         backward_middle_kernel,
-        [(kept_shape, VMEM), (shape(((rows - 4) // 2, parts, c, 128), F32), VMEM)],
+        [
+            (kept_shape, VMEM),
+            (shape(((rows - 4) // 2, parts, c, 128), F32), VMEM),
+            (taps, VMEM),
+            (own_taps, VMEM),
+        ],
         [VMEM] * 6,
-        [all_rows, most_rows, keep(taps, BF16), keep(own_taps, BF16)],
+        [all_rows, most_rows],
     )(g, beside, kernel_in, kernel_out, base, slope_middle)
     mine, kept, out_middle = lax.optimization_barrier((mine, kept, out_middle))
     others = swapped(mine)
     (out_own,) = call(
-        backward_own_kernel,
-        [(shape((parts, c, 128), F32), VMEM)],
-        [VMEM] * 8,
-        [four_rows, four_rows, keep(taps, BF16), keep(own_taps, BF16)],
-    )(g, beside, mine, kept, kernel_in, kernel_out, base, slope_own)
+        backward_own_kernel, [(shape((parts, c, 128), F32), VMEM)], [VMEM] * 8, [four_rows, four_rows]
+    )(g, beside, mine, kept, w3, w4, base, slope_own)
     next_state, innovation = call(
         backward_kernel,
         [(shape((half, rows, width), F32), HBM), (shape(observed.shape, BF16), HBM)],
@@ -699,12 +702,10 @@
             four_rows,
             four_rows,
             VMEM((parts, half * rows, 128), F32),
-            keep(taps, BF16),
-            keep(own_taps, BF16),
             pltpu.SemaphoreType.DMA((parts,)),
             pltpu.SemaphoreType.DMA((blocks,)),
         ],
-    )(g, beside, others, kept, kernel_in, kernel_out, base, slope_other, out_middle, out_own, code, *back)
+    )(g, beside, others, kept, w3, w4, base, slope_other, out_middle, out_own, code, *back)
     return next_state, innovation
 
 

time: 47.3 us -> 43.2 us (0.913)
  waiting for transfers between devices: 13.9 us -> 9.09 us
  starting transfers between devices: 21.5 us -> 23 us
    ppermute x6, waiting for transfers between devices: 9.68 us -> 4.77 us  [sent(): lax.ppermute(pieces[k], 'lat', [(i, i ^ k) for i in range(lats)])]
    ppermute x4, starting transfers between devices: 5.53 us -> 9.31 us  [swapped(): return lax.ppermute(value, 'ch', [(0, 1), (1, 0)])]
    ppermute x2, starting transfers between devices: 3.94 us -> 2.6 us  [move(): return lax.ppermute(value, ('lon', 'ch'), pairs)]
    ppermute x6, starting transfers between devices: 10.6 us -> 9.62 us  [sent(): lax.ppermute(pieces[k], 'lat', [(i, i ^ k) for i in range(lats)])]
    ppermute x2, waiting for transfers between devices: 3.77 us -> 4.3 us  [move(): return lax.ppermute(value, ('lon', 'ch'), pairs)]
  transfers between devices with their start and end apart: 14 -> 14, of which waited for: 9 -> 4; matrix products, arithmetic and copies ran while one was open for 0% -> 0% of each run, Pallas kernels for 13% -> 15%
where the time goes in v4:
time: 43.2 us; the launch traced here: 43.1 us
  starting transfers between devices  23 us (53%)
  Pallas kernels  9.98 us (23%)
  waiting for transfers between devices  9.09 us (21%)
  between operations  0.78 us (2%)
    pallas_call x11, Pallas kernels, apply(): run(*(pltpu.with_memory_space_constraint(a, space) if space in (VMEM, HBM...  9.98 us
    ppermute x6, starting transfers between devices, sent(): lax.ppermute(pieces[k], 'lat', [(i, i ^ k) for i in range(lats)])  9.62 us
    ppermute x4, starting transfers between devices, swapped(): return lax.ppermute(value, 'ch', [(0, 1), (1, 0)])  9.31 us
    ppermute x6, waiting for transfers between devices, sent(): lax.ppermute(pieces[k], 'lat', [(i, i ^ k) for i in range(lats)])  4.77 us
    ppermute x2, waiting for transfers between devices, move(): return lax.ppermute(value, ('lon', 'ch'), pairs)  4.3 us
    ppermute x2, starting transfers between devices, move(): return lax.ppermute(value, ('lon', 'ch'), pairs)  2.6 us
    ppermute x2, starting transfers between devices, from_row_neighbour(): return lax.ppermute(value, ('lat', 'ch'), pairs)  1.47 us
  transfers between devices with their start and end apart: 14, of which 4 were waited for; matrix products, arithmetic and copies ran while one was open for 0% of the time, Pallas kernels for 15%

profile of v4, /device:TPU:0, one launch (start us, length us, event | category | flops | bytes accessed | tf_op | source)
XLA Modules:
  0.0 43.1 jit_solution(12646542460950200824)
XLA Ops:
  0.6 0.6 %collective-permute-start = (bf16[64,8,256]{2,1,0:T(8,128)(2,1)}, bf16[64,8,256]{2,1,0:T(8,128)(2,1)S(1)}, u32[]{:S(2)}, u32[]{:S(2)}) collective-permute-start(bf16[64,8,256]{2,1,0:T(8,128)(2,1)} %noisy_hbm.1), channel_id=1, source_target_pairs={{0,1},{1,0},{2,3},{3,2},{4,5},{5,4},{6,7},{7,6},{8,9},{9,8},{10,11... | collective-permute-start | bytes 786440 | tf_op jit(solution)/shard_map/ppermute | solution.py:545
  1.2 1.1 %shard_map.113 = (bf16[64,8,256]{2,1,0:T(8,128)(2,1)S(1)}, f32[4,128]{1,0:T(4,128)S(1)}, bf16[272,128]{1,0:T(8,128)(2,1)S(1)}, bf16[272,128]{1,0:T(8,128)(2,1)S(...) custom-call(s32[4]{0:T(128)} %dest_hbm.1, s32[4]{0:T(128)} %row_hbm.1, s32[4]{0:T(128)} %col_hbm.1, ...), custom_call_target="tpu_custom_call" | custom-call | tf_op jit(solution)/shard_map/pallas_call | solution.py:41
  2.3 2.6 %collective-permute-start.3 = (bf16[272,128]{1,0:T(8,128)(2,1)S(1)}, bf16[272,128]{1,0:T(8,128)(2,1)S(1)}, u32[]{:S(2)}, u32[]{:S(2)}) collective-permute-start(bf16[272,128]{1,0:T(8,128)(2,1)S(1)} %get-tuple-element.45), channel_id=1, source_target_pairs={{0,4},{4,0},{8,12},{12,8},{1,5},{5,1},{9,13},{13,9},{2,6},{6,2},{1... | collective-permute-start | bytes 208904 | tf_op jit(solution)/shard_map/ppermute | solution.py:124
  5.0 2.6 %collective-permute-start.4 = (bf16[272,128]{1,0:T(8,128)(2,1)S(1)}, bf16[272,128]{1,0:T(8,128)(2,1)S(1)}, u32[]{:S(2)}, u32[]{:S(2)}) collective-permute-start(bf16[272,128]{1,0:T(8,128)(2,1)S(1)} %get-tuple-element.46), channel_id=1, source_target_pairs={{0,8},{4,12},{8,0},{12,4},{1,9},{5,13},{9,1},{13,5},{2,10},{6,14},... | collective-permute-start | bytes 208904 | tf_op jit(solution)/shard_map/ppermute | solution.py:124
  7.6 0.0 collective-permute-start.5
  7.6 0.0 collective-permute-done.other_ref
  7.6 0.3 shard_map.114
  7.9 1.1 %collective-permute-start.1 = (bf16[8,16,128]{2,1,0:T(8,128)(2,1)S(1)}, bf16[8,16,128]{2,1,0:T(8,128)(2,1)S(1)}, u32[]{:S(2)}, u32[]{:S(2)}) collective-permute-start(bf16[8,16,128]{2,1,0:T(8,128)(2,1)S(1)} %get-tuple-element.43), channel_id=1, source_target_pairs={{0,3},{1,2},{2,1},{3,0},{4,7},{5,6},{6,5},{7,4},{8,11},{9,10},{10,... | collective-permute-start | bytes 98312 | tf_op jit(solution)/shard_map/ppermute | solution.py:562
  9.0 2.4 %collective-permute-done.1.tail_ref = bf16[8,16,128]{2,1,0:T(8,128)(2,1)S(1)} collective-permute-done((bf16[8,16,128]{2,1,0:T(8,128)(2,1)S(1)}, bf16[8,16,128]{2,1,0:T(8,128)(2,1)S(1)}, u32[]{:S(2)}, u32[]{:S(2)}) %collective-permute-start.1) | collective-permute-done | bytes 32800 | tf_op jit(solution)/shard_map/ppermute | solution.py:562
  11.4 0.0 copy-start
  11.4 0.0 copy-start.1
  11.4 0.0 copy-start.2
  11.4 0.8 %collective-permute-start.2 = (bf16[2,272,128]{2,1,0:T(8,128)(2,1)S(1)}, bf16[2,272,128]{2,1,0:T(8,128)(2,1)S(1)}, u32[]{:S(2)}, u32[]{:S(2)}) collective-permute-start(bf16[2,272,128]{2,1,0:T(8,128)(2,1)S(1)} %shard_map.115), channel_id=1, source_target_pairs={{1,4},{4,1},{5,8},{8,5},{9,12},{12,9},{3,6},{6,3},{7,10},{10,7},{1... | collective-permute-start | bytes 417800 | tf_op jit(solution)/shard_map/ppermute | solution.py:554
  12.2 0.1 copy-done
  12.3 0.1 copy-done.1
  12.4 0.0 copy-done.2
  12.4 1.6 %shard_map.116 = (f32[6,272,128]{2,1,0:T(8,128)S(1)}, bf16[4,272,128]{2,1,0:T(8,128)(2,1)S(1)}, bf16[4,256,128]{2,1,0:T(8,128)(2,1)S(1)}, bf16[512,768]{1,0:T(8,128)(2,1)S(1)}, bf16[512,768]{1,0:T(8,128)(2,1)S(1)}) custom-call(bf16[8,256,128]{2,1,0:T(8,128)(2,1)S(1)} %get-tuple-element.42.x_ref, bf16[8,16,128]{2,1,0:T(8,128)(2,1)S(1)} %collective-permute-done.1.tail_ref, ...), custom_call_target="tpu_custom_call" | custom-call | tf_op jit(solution)/shard_map/pallas_call | solution.py:41
  14.1 0.0 collective-permute-done.3.refs_1_
  14.1 0.0 collective-permute-done.4.refs_2_
  14.1 0.0 collective-permute-done.5.refs_3_
  14.1 2.4 %collective-permute-start.7 = (bf16[4,272,128]{2,1,0:T(8,128)(2,1)S(1)}, bf16[4,272,128]{2,1,0:T(8,128)(2,1)S(1)}, u32[]{:S(2)}, u32[]{:S(2)}) collective-permute-start(bf16[4,272,128]{2,1,0:T(8,128)(2,1)S(1)} %shard_map.118.block_ref), channel_id=1, source_target_pairs={{0,1},{1,0},{2,3},{3,2},{4,5},{5,4},{6,7},{7,6},{8,9},{9,8},{10,11... | collective-permute-start | bytes 835592 | tf_op jit(solution)/shard_map/ppermute | solution.py:545
  16.5 0.0 collective-permute-done.2.halo_ref
  16.5 1.8 %collective-permute-start.6 = (bf16[2,272,128]{2,1,0:T(8,128)(2,1)S(1)}, bf16[2,272,128]{2,1,0:T(8,128)(2,1)S(1)}, u32[]{:S(2)}, u32[]{:S(2)}) collective-permute-start(bf16[2,272,128]{2,1,0:T(8,128)(2,1)S(1)} %collective-permute-done.2.halo_ref), channel_id=1, source_target_pairs={{0,1},{1,0},{2,3},{3,2},{4,5},{5,4},{6,7},{7,6},{8,9},{9,8},{10,11... | collective-permute-start | bytes 417800 | tf_op jit(solution)/shard_map/ppermute | solution.py:545
  18.3 1.0 %shard_map.117 = (f32[2,272,128]{2,1,0:T(8,128)S(1)}, bf16[2,256,128]{2,1,0:T(8,128)(2,1)S(1)}) custom-call(bf16[8,256,128]{2,1,0:T(8,128)(2,1)S(1)} %get-tuple-element.42.x_ref, bf16[8,16,128]{2,1,0:T(8,128)(2,1)S(1)} %collective-permute-done.1.tail_ref, bf16[2,272,128]{2,1,0:T(8,128)(2,1)S(1)} %collective-permute-done.2.halo_ref, ...), custom_call_target="tpu_custom_call" | custom-call | tf_op jit(solution)/shard_map/pallas_call | solution.py:41
  19.3 0.0 collective-permute-done.7.other_block_ref
  19.3 0.0 collective-permute-done.6.halo_ref
  19.3 2.0 %shard_map.119 = (f32[2,272,128]{2,1,0:T(8,128)S(1)}, f32[4,256,128]{2,1,0:T(8,128)S(1)}, bf16[8,256,128]{2,1,0:T(8,128)(2,1)S(1)}, bf16[8,16,128]{2,1,0:T(8,128...) custom-call(bf16[8,256,128]{2,1,0:T(8,128)(2,1)S(1)} %get-tuple-elem, ...), custom_call_target="tpu_custom_call", output_to_operand_aliasing={{2}: (0, {}), {3}: (1, {})} | custom-call | tf_op jit(solution)/shard_map/pallas_call | solution.py:41
  21.3 1.5 %collective-permute-start.8 = (bf16[8,16,128]{2,1,0:T(8,128)(2,1)S(1)}, bf16[8,16,128]{2,1,0:T(8,128)(2,1)S(1)}, u32[]{:S(2)}, u32[]{:S(2)}) collective-permute-start(bf16[8,16,128]{2,1,0:T(8,128)(2,1)S(1)} %get-tuple-element.63), channel_id=1, source_target_pairs={{0,3},{1,2},{2,1},{3,0},{4,7},{5,6},{6,5},{7,4},{8,11},{9,10},{10,... | collective-permute-start | bytes 98312 | tf_op jit(solution)/shard_map/ppermute | solution.py:562
  22.8 1.9 %collective-permute-done.8.tail_ref = bf16[8,16,128]{2,1,0:T(8,128)(2,1)S(1)} collective-permute-done((bf16[8,16,128]{2,1,0:T(8,128)(2,1)S(1)}, bf16[8,16,128]{2,1,0:T(8,128)(2,1)S(1)}, u32[]{:S(2)}, u32[]{:S(2)}) %collective-permute-start.8) | collective-permute-done | bytes 32800 | tf_op jit(solution)/shard_map/ppermute | solution.py:562
  24.7 0.7 %collective-permute-start.9 = (bf16[2,272,128]{2,1,0:T(8,128)(2,1)S(1)}, bf16[2,272,128]{2,1,0:T(8,128)(2,1)S(1)}, u32[]{:S(2)}, u32[]{:S(2)}) collective-permute-start(bf16[2,272,128]{2,1,0:T(8,128)(2,1)S(1)} %shard_map.120), channel_id=1, source_target_pairs={{1,4},{4,1},{5,8},{8,5},{9,12},{12,9},{3,6},{6,3},{7,10},{10,7},{1... | collective-permute-start | bytes 417800 | tf_op jit(solution)/shard_map/ppermute | solution.py:554
  25.4 1.4 %shard_map.121 = (bf16[4,272,128]{2,1,0:T(8,128)(2,1)S(1)}, f32[2,2,128,128]{3,2,1,0:T(8,128)S(1)}, bf16[512,768]{1,0:T(8,128)(2,1)S(1)}, bf16[512,384]{1,0:T(8,128)(2,1)S(1)}) custom-call(bf16[8,256,128]{2,1,0:T(8,128)(2,1)S(1)} %get-tuple-element.62.x_ref, bf16[8,16,128]{2,1,0:T(8,128)(2,1)S(1)} %collective-permute-done.8.tail_ref, ...), custom_call_target="tpu_custom_call" | custom-call | tf_op jit(solution)/shard_map/pallas_call | solution.py:41
  26.9 0.0 collective-permute-done.9.halo_ref
  26.9 4.6 %collective-permute-start.10 = (bf16[2,272,128]{2,1,0:T(8,128)(2,1)S(1)}, bf16[2,272,128]{2,1,0:T(8,128)(2,1)S(1)}, u32[]{:S(2)}, u32[]{:S(2)}) collective-permute-start(bf16[2,272,128]{2,1,0:T(8,128)(2,1)S(1)} %collective-permute-done.9.halo_ref), channel_id=1, source_target_pairs={{0,1},{1,0},{2,3},{3,2},{4,5},{5,4},{6,7},{7,6},{8,9},{9,8},{10,11... | collective-permute-start | bytes 417800 | tf_op jit(solution)/shard_map/ppermute | solution.py:545
  31.5 1.2 %collective-permute-start.11 = (bf16[2,64,128]{2,1,0:T(8,128)(2,1)S(1)}, bf16[2,64,128]{2,1,0:T(8,128)(2,1)S(1)}, u32[]{:S(2)}, u32[]{:S(2)}) collective-permute-start(bf16[2,64,128]{2,1,0:T(8,128)(2,1)S(1)} %get-tuple-element.77), channel_id=1, source_target_pairs={{0,4},{4,0},{8,12},{12,8},{1,5},{5,1},{9,13},{13,9},{2,6},{6,2},{1... | collective-permute-start | bytes 98312 | tf_op jit(solution)/shard_map/ppermute | solution.py:124
  32.7 3.0 %collective-permute-start.12 = (bf16[2,64,128]{2,1,0:T(8,128)(2,1)S(1)}, bf16[2,64,128]{2,1,0:T(8,128)(2,1)S(1)}, u32[]{:S(2)}, u32[]{:S(2)}) collective-permute-start(bf16[2,64,128]{2,1,0:T(8,128)(2,1)S(1)} %get-tuple-element.78), channel_id=1, source_target_pairs={{0,8},{4,12},{8,0},{12,4},{1,9},{5,13},{9,1},{13,5},{2,10},{6,14},... | collective-permute-start | bytes 98312 | tf_op jit(solution)/shard_map/ppermute | solution.py:124
  35.7 0.2 collective-permute-start.13
  35.8 0.8 %shard_map.122.out_own_ref = f32[2,128,128]{2,1,0:T(8,128)S(1)} custom-call(bf16[8,256,128]{2,1,0:T(8,128)(2,1)S(1)} %get-tuple-element.62.x_ref, bf16[8,16,128]{2,1,0:T(8,128)(2,1)S(1)} %collective-permute-done.8.tail_ref, bf16[2,272,128]{2,1,0:T(8,128)(2,1)S(1)} %collective-permute-done.9.halo_ref, bf16[4,272,128]{2,1,0:T(8,128)(2,1)S(1)} %get-tuple-element.69.kept_ref, ...), custom_call_target="tpu_custom_call" | custom-call | tf_op jit(solution)/shard_map/pallas_call | solution.py:41
  36.6 0.0 collective-permute-done.11.refs_1_
  36.6 1.7 %collective-permute-done.12.refs_2_ = bf16[2,64,128]{2,1,0:T(8,128)(2,1)S(1)} collective-permute-done((bf16[2,64,128]{2,1,0:T(8,128)(2,1)S(1)}, bf16[2,64,128]{2,1,0:T(8,128)(2,1)S(1)}, u32[]{:S(2)}, u32[]{:S(2)}) %collective-permute-start.12) | collective-permute-done | bytes 32800 | tf_op jit(solution)/shard_map/ppermute | solution.py:124
  38.3 3.1 %collective-permute-done.13.refs_3_ = bf16[2,64,128]{2,1,0:T(8,128)(2,1)S(1)} collective-permute-done((bf16[2,64,128]{2,1,0:T(8,128)(2,1)S(1)}, bf16[2,64,128]{2,1,0:T(8,128)(2,1)S(1)}, u32[]{:S(2)}, u32[]{:S(2)}) %collective-permute-start.13) | collective-permute-done | bytes 32800 | tf_op jit(solution)/shard_map/ppermute | solution.py:124
  41.4 0.0 collective-permute-done.10.halo_ref
  41.4 1.7 %shard_map.123 = (f32[64,8,256]{2,1,0:T(8,128)}, bf16[4,64,128]{2,1,0:T(8,128)(2,1)}) custom-call(bf16[8,256,128]{2,1,0:T(8,128)(2,1)S(1)} %get-tuple-element.62.x_ref, bf16[8,16,128]{2,1,0:T(8,128)(2,1)S(1)} %collective-permute-done.8.tail_ref, bf16[2,272,128]{2,1,0:T(8,128)(2,1)S(1)} %collective-permute-done.10.halo_ref, ...), custom_call_target="tpu_custom_call" | custom-call | tf_op jit(solution)/shard_map/pallas_call | solution.py:41
  (3 shorter events, 0.0 us)
Async XLA Ops:
  0.6 6.9 %collective-permute-start = (bf16[64,8,256]{2,1,0:T(8,128)(2,1)}, bf16[64,8,256]{2,1,0:T(8,128)(2,1)S(1)}, u32[]{:S(2)}, u32[]{:S(2)}) collective-permute-start(bf16[64,8,256]{2,1,0:T(8,128)(2,1)} %noisy_hbm.1), channel_id=1, source_target_pairs={{0,1},{1,0},{2,3},{3,2},{4,5},{5,4},{6,7},{7,6},{8,9},{9,8},{10,11... | collective-permute-start | bytes 786440 | tf_op jit(solution)/shard_map/ppermute | solution.py:545
  2.3 11.8 %collective-permute-start.3 = (bf16[272,128]{1,0:T(8,128)(2,1)S(1)}, bf16[272,128]{1,0:T(8,128)(2,1)S(1)}, u32[]{:S(2)}, u32[]{:S(2)}) collective-permute-start(bf16[272,128]{1,0:T(8,128)(2,1)S(1)} %get-tuple-element.45), channel_id=1, source_target_pairs={{0,4},{4,0},{8,12},{12,8},{1,5},{5,1},{9,13},{13,9},{2,6},{6,2},{1... | collective-permute-start | bytes 208904 | tf_op jit(solution)/shard_map/ppermute | solution.py:124
  5.0 9.1 %collective-permute-start.4 = (bf16[272,128]{1,0:T(8,128)(2,1)S(1)}, bf16[272,128]{1,0:T(8,128)(2,1)S(1)}, u32[]{:S(2)}, u32[]{:S(2)}) collective-permute-start(bf16[272,128]{1,0:T(8,128)(2,1)S(1)} %get-tuple-element.46), channel_id=1, source_target_pairs={{0,8},{4,12},{8,0},{12,4},{1,9},{5,13},{9,1},{13,5},{2,10},{6,14},... | collective-permute-start | bytes 208904 | tf_op jit(solution)/shard_map/ppermute | solution.py:124
  7.6 6.5 %collective-permute-start.5 = (bf16[272,128]{1,0:T(8,128)(2,1)S(1)}, bf16[272,128]{1,0:T(8,128)(2,1)S(1)}, u32[]{:S(2)}, u32[]{:S(2)}) collective-permute-start(bf16[272,128]{1,0:T(8,128)(2,1)S(1)} %get-tuple-element.47), channel_id=1, source_target_pairs={{0,12},{4,8},{8,4},{12,0},{1,13},{5,9},{9,5},{13,1},{2,14},{6,10},... | collective-permute-start | bytes 208904 | tf_op jit(solution)/shard_map/ppermute | solution.py:124
  7.9 3.5 %collective-permute-start.1 = (bf16[8,16,128]{2,1,0:T(8,128)(2,1)S(1)}, bf16[8,16,128]{2,1,0:T(8,128)(2,1)S(1)}, u32[]{:S(2)}, u32[]{:S(2)}) collective-permute-start(bf16[8,16,128]{2,1,0:T(8,128)(2,1)S(1)} %get-tuple-element.43), channel_id=1, source_target_pairs={{0,3},{1,2},{2,1},{3,0},{4,7},{5,6},{6,5},{7,4},{8,11},{9,10},{10,... | collective-permute-start | bytes 98312 | tf_op jit(solution)/shard_map/ppermute | solution.py:562
  11.4 1.0 %copy-start = (bf16[3,3,128,128]{3,2,1,0:T(8,128)(2,1)S(1)}, bf16[3,3,128,128]{3,2,1,0:T(8,128)(2,1)}, u32[]{:S(2)}) copy-start(bf16[3,3,128,128]{3,2,1,0:T(8,128)(2,1)} %kin_ref.3) | copy-start | bytes 884740
  11.4 1.0 %copy-start.1 = (bf16[3,3,128,128]{3,2,1,0:T(8,128)(2,1)S(1)}, bf16[3,3,128,128]{3,2,1,0:T(8,128)(2,1)}, u32[]{:S(2)}) copy-start(bf16[3,3,128,128]{3,2,1,0:T(8,128)(2,1)} %kout_ref.3) | copy-start | bytes 884740
  11.4 1.0 %copy-start.2 = (f32[128]{0:T(128)S(1)}, f32[128]{0:T(128)}, u32[]{:S(2)}) copy-start(f32[128]{0:T(128)} %param.12) | copy-start | bytes 1540
  11.4 5.1 %collective-permute-start.2 = (bf16[2,272,128]{2,1,0:T(8,128)(2,1)S(1)}, bf16[2,272,128]{2,1,0:T(8,128)(2,1)S(1)}, u32[]{:S(2)}, u32[]{:S(2)}) collective-permute-start(bf16[2,272,128]{2,1,0:T(8,128)(2,1)S(1)} %shard_map.115), channel_id=1, source_target_pairs={{1,4},{4,1},{5,8},{8,5},{9,12},{12,9},{3,6},{6,3},{7,10},{10,7},{1... | collective-permute-start | bytes 417800 | tf_op jit(solution)/shard_map/ppermute | solution.py:554
  14.1 5.1 %collective-permute-start.7 = (bf16[4,272,128]{2,1,0:T(8,128)(2,1)S(1)}, bf16[4,272,128]{2,1,0:T(8,128)(2,1)S(1)}, u32[]{:S(2)}, u32[]{:S(2)}) collective-permute-start(bf16[4,272,128]{2,1,0:T(8,128)(2,1)S(1)} %shard_map.118.block_ref), channel_id=1, source_target_pairs={{0,1},{1,0},{2,3},{3,2},{4,5},{5,4},{6,7},{7,6},{8,9},{9,8},{10,11... | collective-permute-start | bytes 835592 | tf_op jit(solution)/shard_map/ppermute | solution.py:545
  16.5 2.8 %collective-permute-start.6 = (bf16[2,272,128]{2,1,0:T(8,128)(2,1)S(1)}, bf16[2,272,128]{2,1,0:T(8,128)(2,1)S(1)}, u32[]{:S(2)}, u32[]{:S(2)}) collective-permute-start(bf16[2,272,128]{2,1,0:T(8,128)(2,1)S(1)} %collective-permute-done.2.halo_ref), channel_id=1, source_target_pairs={{0,1},{1,0},{2,3},{3,2},{4,5},{5,4},{6,7},{7,6},{8,9},{9,8},{10,11... | collective-permute-start | bytes 417800 | tf_op jit(solution)/shard_map/ppermute | solution.py:545
  21.3 3.4 %collective-permute-start.8 = (bf16[8,16,128]{2,1,0:T(8,128)(2,1)S(1)}, bf16[8,16,128]{2,1,0:T(8,128)(2,1)S(1)}, u32[]{:S(2)}, u32[]{:S(2)}) collective-permute-start(bf16[8,16,128]{2,1,0:T(8,128)(2,1)S(1)} %get-tuple-element.63), channel_id=1, source_target_pairs={{0,3},{1,2},{2,1},{3,0},{4,7},{5,6},{6,5},{7,4},{8,11},{9,10},{10,... | collective-permute-start | bytes 98312 | tf_op jit(solution)/shard_map/ppermute | solution.py:562
  24.7 2.1 %collective-permute-start.9 = (bf16[2,272,128]{2,1,0:T(8,128)(2,1)S(1)}, bf16[2,272,128]{2,1,0:T(8,128)(2,1)S(1)}, u32[]{:S(2)}, u32[]{:S(2)}) collective-permute-start(bf16[2,272,128]{2,1,0:T(8,128)(2,1)S(1)} %shard_map.120), channel_id=1, source_target_pairs={{1,4},{4,1},{5,8},{8,5},{9,12},{12,9},{3,6},{6,3},{7,10},{10,7},{1... | collective-permute-start | bytes 417800 | tf_op jit(solution)/shard_map/ppermute | solution.py:554
  26.9 14.5 %collective-permute-start.10 = (bf16[2,272,128]{2,1,0:T(8,128)(2,1)S(1)}, bf16[2,272,128]{2,1,0:T(8,128)(2,1)S(1)}, u32[]{:S(2)}, u32[]{:S(2)}) collective-permute-start(bf16[2,272,128]{2,1,0:T(8,128)(2,1)S(1)} %collective-permute-done.9.halo_ref), channel_id=1, source_target_pairs={{0,1},{1,0},{2,3},{3,2},{4,5},{5,4},{6,7},{7,6},{8,9},{9,8},{10,11... | collective-permute-start | bytes 417800 | tf_op jit(solution)/shard_map/ppermute | solution.py:545
  31.5 5.2 %collective-permute-start.11 = (bf16[2,64,128]{2,1,0:T(8,128)(2,1)S(1)}, bf16[2,64,128]{2,1,0:T(8,128)(2,1)S(1)}, u32[]{:S(2)}, u32[]{:S(2)}) collective-permute-start(bf16[2,64,128]{2,1,0:T(8,128)(2,1)S(1)} %get-tuple-element.77), channel_id=1, source_target_pairs={{0,4},{4,0},{8,12},{12,8},{1,5},{5,1},{9,13},{13,9},{2,6},{6,2},{1... | collective-permute-start | bytes 98312 | tf_op jit(solution)/shard_map/ppermute | solution.py:124
  32.7 5.7 %collective-permute-start.12 = (bf16[2,64,128]{2,1,0:T(8,128)(2,1)S(1)}, bf16[2,64,128]{2,1,0:T(8,128)(2,1)S(1)}, u32[]{:S(2)}, u32[]{:S(2)}) collective-permute-start(bf16[2,64,128]{2,1,0:T(8,128)(2,1)S(1)} %get-tuple-element.78), channel_id=1, source_target_pairs={{0,8},{4,12},{8,0},{12,4},{1,9},{5,13},{9,1},{13,5},{2,10},{6,14},... | collective-permute-start | bytes 98312 | tf_op jit(solution)/shard_map/ppermute | solution.py:124
  35.7 5.7 %collective-permute-start.13 = (bf16[2,64,128]{2,1,0:T(8,128)(2,1)S(1)}, bf16[2,64,128]{2,1,0:T(8,128)(2,1)S(1)}, u32[]{:S(2)}, u32[]{:S(2)}) collective-permute-start(bf16[2,64,128]{2,1,0:T(8,128)(2,1)S(1)} %get-tuple-element.79), channel_id=1, source_target_pairs={{0,12},{4,8},{8,4},{12,0},{1,13},{5,9},{9,5},{13,1},{2,14},{6,10},... | collective-permute-start | bytes 98312 | tf_op jit(solution)/shard_map/ppermute | solution.py:124

commit v5 on v4

--- a/solution.py
+++ b/solution.py
@@ -10,7 +10,7 @@
 PW = 32
 CAP = 2
 TAIL = 16
-META = 16
+META = 8
 
 keep_rate = 0.6
 blend_rate = 0.4
@@ -423,13 +423,10 @@
         for cap in range(CAP):
             out_ref[cap] = inn_ref[source * CAP + cap]
 
-    for g in range(rows // 2):
-        base = []
-        for r in (2 * g, 2 * g + 1):
-            field = field_ref[r]
-            base.append(keep_rate * x_ref[r].astype(F32) + blend_rate * den_ref[r] - guide_rate * field)
-            g_ref[r] = field.astype(BF16)
-        base_ref[g] = own_pair(*base)
+    for r in range(rows):
+        field = field_ref[r]
+        base_ref[r] = keep_rate * x_ref[r].astype(F32) + blend_rate * den_ref[r] - guide_rate * field
+        g_ref[r] = field.astype(BF16)
     write_tails(g_ref, gtail_ref)
 
 
@@ -458,7 +455,7 @@
         kept_ref[i] = grad_ref[i]
         kept_ref[2 + i] = grad_ref[rows - 4 + i]
     for g in range((rows - 4) // 2):
-        for part, plane in enumerate(own_row_pair(grad_ref, w4_ref, base_ref[1 + g], 2 * g)):
+        for part, plane in enumerate(own_row_pair(grad_ref, w4_ref, own_pair(base_ref[2 + 2 * g], base_ref[3 + 2 * g]), 2 * g)):
             out_ref[g, part] = plane
 
 
@@ -470,7 +467,8 @@
         for i, y in enumerate(row_pair(ext_ref, w3_ref, 0))
     ]
     fill_between(between_ref, end, new, kept_ref)
-    return own_row_pair(between_ref, w4_ref, base_ref[(rows // 2 - 1) * end], 0)
+    base = own_pair(base_ref[(rows - 2) * end], base_ref[(rows - 2) * end + 1])
+    return own_row_pair(between_ref, w4_ref, base, 0)
 
 
 def backward_own_kernel(
@@ -521,7 +519,6 @@
         for i in range(2):
             flat_ref[part, pl.ds(2 * pair + i, half, stride=rows), :] = plane[i * half : (i + 1) * half]
 
-    lax.fori_loop(0, inn_hbm.shape[0], give, 0, unroll=inn_hbm.shape[0] <= 8)
     for part in range(parts):
         for g in range((rows - 4) // 2):
             put(1 + g, part, out_middle_ref[g, part])
@@ -536,6 +533,7 @@
         target = next_hbm.at[:, :, pl.ds(part * 128, 128)]
         copies.append(pltpu.make_async_copy(source, target, next_sems.at[part]))
         copies[-1].start()
+    lax.fori_loop(0, inn_hbm.shape[0], give, 0, unroll=inn_hbm.shape[0] <= 8)
     for copy in copies:
         copy.wait()
     lax.fori_loop(0, inn_hbm.shape[0], given, 0)
@@ -655,7 +653,7 @@
         forward_kernel,
         [
             (pair, VMEM),
-            (shape((rows // 2, width, c), F32), VMEM),
+            (shape((rows, width, c), F32), VMEM),
             (shape((rows, width, c), BF16), VMEM),
             (tail_shape, VMEM),
             *[(shape((CAP, half, obs), BF16), VMEM)] * lats,

time: 43.2 us -> 43 us (level)
  no operation moved by 1% of the time
where the time goes in v5:
time: 43 us; the launch traced here: 42.8 us
  starting transfers between devices  23 us (53%)
  Pallas kernels  9.81 us (23%)
  waiting for transfers between devices  9.04 us (21%)
  between operations  0.78 us (2%)
    pallas_call x11, Pallas kernels, apply(): run(*(pltpu.with_memory_space_constraint(a, space) if space in (VMEM, HBM...  9.81 us
    ppermute x6, starting transfers between devices, sent(): lax.ppermute(pieces[k], 'lat', [(i, i ^ k) for i in range(lats)])  9.62 us
    ppermute x4, starting transfers between devices, swapped(): return lax.ppermute(value, 'ch', [(0, 1), (1, 0)])  9.3 us
    ppermute x6, waiting for transfers between devices, sent(): lax.ppermute(pieces[k], 'lat', [(i, i ^ k) for i in range(lats)])  4.74 us
    ppermute x2, waiting for transfers between devices, move(): return lax.ppermute(value, ('lon', 'ch'), pairs)  4.29 us
    ppermute x2, starting transfers between devices, move(): return lax.ppermute(value, ('lon', 'ch'), pairs)  2.61 us
    ppermute x2, starting transfers between devices, from_row_neighbour(): return lax.ppermute(value, ('lat', 'ch'), pairs)  1.47 us
  transfers between devices with their start and end apart: 14, of which 4 were waited for; matrix products, arithmetic and copies ran while one was open for 0% of the time, Pallas kernels for 15%

profile of v5, /device:TPU:0, one launch (start us, length us, event | category | flops | bytes accessed | tf_op | source)
XLA Modules:
  0.0 42.8 jit_solution(1216202782415438842)
XLA Ops:
  0.6 0.6 %collective-permute-start = (bf16[64,8,256]{2,1,0:T(8,128)(2,1)}, bf16[64,8,256]{2,1,0:T(8,128)(2,1)S(1)}, u32[]{:S(2)}, u32[]{:S(2)}) collective-permute-start(bf16[64,8,256]{2,1,0:T(8,128)(2,1)} %noisy_hbm.1), channel_id=1, source_target_pairs={{0,1},{1,0},{2,3},{3,2},{4,5},{5,4},{6,7},{7,6},{8,9},{9,8},{10,11... | collective-permute-start | bytes 786440 | tf_op jit(solution)/shard_map/ppermute | solution.py:543
  1.2 1.1 %shard_map.113 = (bf16[64,8,256]{2,1,0:T(8,128)(2,1)S(1)}, f32[4,128]{1,0:T(4,128)S(1)}, bf16[264,128]{1,0:T(8,128)(2,1)S(1)}, bf16[264,128]{1,0:T(8,128)(2,1)S(...) custom-call(s32[4]{0:T(128)} %dest_hbm.1, s32[4]{0:T(128)} %row_hbm.1, s32[4]{0:T(128)} %col_hbm.1, ...), custom_call_target="tpu_custom_call" | custom-call | tf_op jit(solution)/shard_map/pallas_call | solution.py:41
  2.3 2.6 %collective-permute-start.3 = (bf16[264,128]{1,0:T(8,128)(2,1)S(1)}, bf16[264,128]{1,0:T(8,128)(2,1)S(1)}, u32[]{:S(2)}, u32[]{:S(2)}) collective-permute-start(bf16[264,128]{1,0:T(8,128)(2,1)S(1)} %get-tuple-element.45), channel_id=1, source_target_pairs={{0,4},{4,0},{8,12},{12,8},{1,5},{5,1},{9,13},{13,9},{2,6},{6,2},{1... | collective-permute-start | bytes 202760 | tf_op jit(solution)/shard_map/ppermute | solution.py:124
  5.0 2.6 %collective-permute-start.4 = (bf16[264,128]{1,0:T(8,128)(2,1)S(1)}, bf16[264,128]{1,0:T(8,128)(2,1)S(1)}, u32[]{:S(2)}, u32[]{:S(2)}) collective-permute-start(bf16[264,128]{1,0:T(8,128)(2,1)S(1)} %get-tuple-element.46), channel_id=1, source_target_pairs={{0,8},{4,12},{8,0},{12,4},{1,9},{5,13},{9,1},{13,5},{2,10},{6,14},... | collective-permute-start | bytes 202760 | tf_op jit(solution)/shard_map/ppermute | solution.py:124
  7.6 0.0 collective-permute-start.5
  7.6 0.0 collective-permute-done.other_ref
  7.6 0.3 shard_map.114
  7.9 1.1 %collective-permute-start.1 = (bf16[8,16,128]{2,1,0:T(8,128)(2,1)S(1)}, bf16[8,16,128]{2,1,0:T(8,128)(2,1)S(1)}, u32[]{:S(2)}, u32[]{:S(2)}) collective-permute-start(bf16[8,16,128]{2,1,0:T(8,128)(2,1)S(1)} %get-tuple-element.43), channel_id=1, source_target_pairs={{0,3},{1,2},{2,1},{3,0},{4,7},{5,6},{6,5},{7,4},{8,11},{9,10},{10,... | collective-permute-start | bytes 98312 | tf_op jit(solution)/shard_map/ppermute | solution.py:560
  9.0 2.4 %collective-permute-done.1.tail_ref = bf16[8,16,128]{2,1,0:T(8,128)(2,1)S(1)} collective-permute-done((bf16[8,16,128]{2,1,0:T(8,128)(2,1)S(1)}, bf16[8,16,128]{2,1,0:T(8,128)(2,1)S(1)}, u32[]{:S(2)}, u32[]{:S(2)}) %collective-permute-start.1) | collective-permute-done | bytes 32800 | tf_op jit(solution)/shard_map/ppermute | solution.py:560
  11.4 0.0 copy-start
  11.4 0.0 copy-start.1
  11.4 0.0 copy-start.2
  11.4 0.8 %collective-permute-start.2 = (bf16[2,272,128]{2,1,0:T(8,128)(2,1)S(1)}, bf16[2,272,128]{2,1,0:T(8,128)(2,1)S(1)}, u32[]{:S(2)}, u32[]{:S(2)}) collective-permute-start(bf16[2,272,128]{2,1,0:T(8,128)(2,1)S(1)} %shard_map.115), channel_id=1, source_target_pairs={{1,4},{4,1},{5,8},{8,5},{9,12},{12,9},{3,6},{6,3},{7,10},{10,7},{1... | collective-permute-start | bytes 417800 | tf_op jit(solution)/shard_map/ppermute | solution.py:552
  12.2 0.1 copy-done
  12.3 0.1 copy-done.1
  12.4 0.0 copy-done.2
  12.4 1.6 %shard_map.116 = (f32[6,272,128]{2,1,0:T(8,128)S(1)}, bf16[4,272,128]{2,1,0:T(8,128)(2,1)S(1)}, bf16[4,256,128]{2,1,0:T(8,128)(2,1)S(1)}, bf16[512,768]{1,0:T(8,128)(2,1)S(1)}, bf16[512,768]{1,0:T(8,128)(2,1)S(1)}) custom-call(bf16[8,256,128]{2,1,0:T(8,128)(2,1)S(1)} %get-tuple-element.42.x_ref, bf16[8,16,128]{2,1,0:T(8,128)(2,1)S(1)} %collective-permute-done.1.tail_ref, ...), custom_call_target="tpu_custom_call" | custom-call | tf_op jit(solution)/shard_map/pallas_call | solution.py:41
  14.1 0.0 collective-permute-done.3.refs_1_
  14.1 0.0 collective-permute-done.4.refs_2_
  14.1 0.0 collective-permute-done.5.refs_3_
  14.1 2.4 %collective-permute-start.7 = (bf16[4,264,128]{2,1,0:T(8,128)(2,1)S(1)}, bf16[4,264,128]{2,1,0:T(8,128)(2,1)S(1)}, u32[]{:S(2)}, u32[]{:S(2)}) collective-permute-start(bf16[4,264,128]{2,1,0:T(8,128)(2,1)S(1)} %shard_map.118.block_ref), channel_id=1, source_target_pairs={{0,1},{1,0},{2,3},{3,2},{4,5},{5,4},{6,7},{7,6},{8,9},{9,8},{10,11... | collective-permute-start | bytes 811016 | tf_op jit(solution)/shard_map/ppermute | solution.py:543
  16.5 0.0 collective-permute-done.2.halo_ref
  16.5 1.8 %collective-permute-start.6 = (bf16[2,272,128]{2,1,0:T(8,128)(2,1)S(1)}, bf16[2,272,128]{2,1,0:T(8,128)(2,1)S(1)}, u32[]{:S(2)}, u32[]{:S(2)}) collective-permute-start(bf16[2,272,128]{2,1,0:T(8,128)(2,1)S(1)} %collective-permute-done.2.halo_ref), channel_id=1, source_target_pairs={{0,1},{1,0},{2,3},{3,2},{4,5},{5,4},{6,7},{7,6},{8,9},{9,8},{10,11... | collective-permute-start | bytes 417800 | tf_op jit(solution)/shard_map/ppermute | solution.py:543
  18.3 1.0 %shard_map.117 = (f32[2,272,128]{2,1,0:T(8,128)S(1)}, bf16[2,256,128]{2,1,0:T(8,128)(2,1)S(1)}) custom-call(bf16[8,256,128]{2,1,0:T(8,128)(2,1)S(1)} %get-tuple-element.42.x_ref, bf16[8,16,128]{2,1,0:T(8,128)(2,1)S(1)} %collective-permute-done.1.tail_ref, bf16[2,272,128]{2,1,0:T(8,128)(2,1)S(1)} %collective-permute-done.2.halo_ref, ...), custom_call_target="tpu_custom_call" | custom-call | tf_op jit(solution)/shard_map/pallas_call | solution.py:41
  19.3 0.0 collective-permute-done.7.other_block_ref
  19.3 0.0 collective-permute-done.6.halo_ref
  19.3 1.8 %shard_map.119 = (f32[2,272,128]{2,1,0:T(8,128)S(1)}, f32[8,256,128]{2,1,0:T(8,128)S(1)}, bf16[8,256,128]{2,1,0:T(8,128)(2,1)S(1)}, bf16[8,16,128]{2,1,0:T(8,128...) custom-call(bf16[8,256,128]{2,1,0:T(8,128)(2,1)S(1)} %get-tuple-elem, ...), custom_call_target="tpu_custom_call", output_to_operand_aliasing={{2}: (0, {}), {3}: (1, {})} | custom-call | tf_op jit(solution)/shard_map/pallas_call | solution.py:41
  21.1 1.5 %collective-permute-start.8 = (bf16[8,16,128]{2,1,0:T(8,128)(2,1)S(1)}, bf16[8,16,128]{2,1,0:T(8,128)(2,1)S(1)}, u32[]{:S(2)}, u32[]{:S(2)}) collective-permute-start(bf16[8,16,128]{2,1,0:T(8,128)(2,1)S(1)} %get-tuple-element.63), channel_id=1, source_target_pairs={{0,3},{1,2},{2,1},{3,0},{4,7},{5,6},{6,5},{7,4},{8,11},{9,10},{10,... | collective-permute-start | bytes 98312 | tf_op jit(solution)/shard_map/ppermute | solution.py:560
  22.6 1.9 %collective-permute-done.8.tail_ref = bf16[8,16,128]{2,1,0:T(8,128)(2,1)S(1)} collective-permute-done((bf16[8,16,128]{2,1,0:T(8,128)(2,1)S(1)}, bf16[8,16,128]{2,1,0:T(8,128)(2,1)S(1)}, u32[]{:S(2)}, u32[]{:S(2)}) %collective-permute-start.8) | collective-permute-done | bytes 32800 | tf_op jit(solution)/shard_map/ppermute | solution.py:560
  24.5 0.7 %collective-permute-start.9 = (bf16[2,272,128]{2,1,0:T(8,128)(2,1)S(1)}, bf16[2,272,128]{2,1,0:T(8,128)(2,1)S(1)}, u32[]{:S(2)}, u32[]{:S(2)}) collective-permute-start(bf16[2,272,128]{2,1,0:T(8,128)(2,1)S(1)} %shard_map.120), channel_id=1, source_target_pairs={{1,4},{4,1},{5,8},{8,5},{9,12},{12,9},{3,6},{6,3},{7,10},{10,7},{1... | collective-permute-start | bytes 417800 | tf_op jit(solution)/shard_map/ppermute | solution.py:552
  25.2 1.4 %shard_map.121 = (bf16[4,272,128]{2,1,0:T(8,128)(2,1)S(1)}, f32[2,2,128,128]{3,2,1,0:T(8,128)S(1)}, bf16[512,768]{1,0:T(8,128)(2,1)S(1)}, bf16[512,384]{1,0:T(8,128)(2,1)S(1)}) custom-call(bf16[8,256,128]{2,1,0:T(8,128)(2,1)S(1)} %get-tuple-element.62.x_ref, bf16[8,16,128]{2,1,0:T(8,128)(2,1)S(1)} %collective-permute-done.8.tail_ref, ...), custom_call_target="tpu_custom_call" | custom-call | tf_op jit(solution)/shard_map/pallas_call | solution.py:41
  26.6 0.0 collective-permute-done.9.halo_ref
  26.7 4.6 %collective-permute-start.10 = (bf16[2,272,128]{2,1,0:T(8,128)(2,1)S(1)}, bf16[2,272,128]{2,1,0:T(8,128)(2,1)S(1)}, u32[]{:S(2)}, u32[]{:S(2)}) collective-permute-start(bf16[2,272,128]{2,1,0:T(8,128)(2,1)S(1)} %collective-permute-done.9.halo_ref), channel_id=1, source_target_pairs={{0,1},{1,0},{2,3},{3,2},{4,5},{5,4},{6,7},{7,6},{8,9},{9,8},{10,11... | collective-permute-start | bytes 417800 | tf_op jit(solution)/shard_map/ppermute | solution.py:543
  31.2 1.2 %collective-permute-start.11 = (bf16[2,64,128]{2,1,0:T(8,128)(2,1)S(1)}, bf16[2,64,128]{2,1,0:T(8,128)(2,1)S(1)}, u32[]{:S(2)}, u32[]{:S(2)}) collective-permute-start(bf16[2,64,128]{2,1,0:T(8,128)(2,1)S(1)} %get-tuple-element.77), channel_id=1, source_target_pairs={{0,4},{4,0},{8,12},{12,8},{1,5},{5,1},{9,13},{13,9},{2,6},{6,2},{1... | collective-permute-start | bytes 98312 | tf_op jit(solution)/shard_map/ppermute | solution.py:124
  32.4 3.0 %collective-permute-start.12 = (bf16[2,64,128]{2,1,0:T(8,128)(2,1)S(1)}, bf16[2,64,128]{2,1,0:T(8,128)(2,1)S(1)}, u32[]{:S(2)}, u32[]{:S(2)}) collective-permute-start(bf16[2,64,128]{2,1,0:T(8,128)(2,1)S(1)} %get-tuple-element.78), channel_id=1, source_target_pairs={{0,8},{4,12},{8,0},{12,4},{1,9},{5,13},{9,1},{13,5},{2,10},{6,14},... | collective-permute-start | bytes 98312 | tf_op jit(solution)/shard_map/ppermute | solution.py:124
  35.5 0.2 collective-permute-start.13
  35.6 0.8 %shard_map.122.out_own_ref = f32[2,128,128]{2,1,0:T(8,128)S(1)} custom-call(bf16[8,256,128]{2,1,0:T(8,128)(2,1)S(1)} %get-tuple-element.62.x_ref, bf16[8,16,128]{2,1,0:T(8,128)(2,1)S(1)} %collective-permute-done.8.tail_ref, bf16[2,272,128]{2,1,0:T(8,128)(2,1)S(1)} %collective-permute-done.9.halo_ref, bf16[4,272,128]{2,1,0:T(8,128)(2,1)S(1)} %get-tuple-element.69.kept_ref, ...), custom_call_target="tpu_custom_call" | custom-call | tf_op jit(solution)/shard_map/pallas_call | solution.py:41
  36.4 0.0 collective-permute-done.11.refs_1_
  36.4 1.7 %collective-permute-done.12.refs_2_ = bf16[2,64,128]{2,1,0:T(8,128)(2,1)S(1)} collective-permute-done((bf16[2,64,128]{2,1,0:T(8,128)(2,1)S(1)}, bf16[2,64,128]{2,1,0:T(8,128)(2,1)S(1)}, u32[]{:S(2)}, u32[]{:S(2)}) %collective-permute-start.12) | collective-permute-done | bytes 32800 | tf_op jit(solution)/shard_map/ppermute | solution.py:124
  38.1 3.1 %collective-permute-done.13.refs_3_ = bf16[2,64,128]{2,1,0:T(8,128)(2,1)S(1)} collective-permute-done((bf16[2,64,128]{2,1,0:T(8,128)(2,1)S(1)}, bf16[2,64,128]{2,1,0:T(8,128)(2,1)S(1)}, u32[]{:S(2)}, u32[]{:S(2)}) %collective-permute-start.13) | collective-permute-done | bytes 32800 | tf_op jit(solution)/shard_map/ppermute | solution.py:124
  41.2 0.0 collective-permute-done.10.halo_ref
  41.2 1.7 %shard_map.123 = (f32[64,8,256]{2,1,0:T(8,128)}, bf16[4,64,128]{2,1,0:T(8,128)(2,1)}) custom-call(bf16[8,256,128]{2,1,0:T(8,128)(2,1)S(1)} %get-tuple-element.62.x_ref, bf16[8,16,128]{2,1,0:T(8,128)(2,1)S(1)} %collective-permute-done.8.tail_ref, bf16[2,272,128]{2,1,0:T(8,128)(2,1)S(1)} %collective-permute-done.10.halo_ref, ...), custom_call_target="tpu_custom_call" | custom-call | tf_op jit(solution)/shard_map/pallas_call | solution.py:41
  (3 shorter events, 0.0 us)
Async XLA Ops:
  0.6 6.9 %collective-permute-start = (bf16[64,8,256]{2,1,0:T(8,128)(2,1)}, bf16[64,8,256]{2,1,0:T(8,128)(2,1)S(1)}, u32[]{:S(2)}, u32[]{:S(2)}) collective-permute-start(bf16[64,8,256]{2,1,0:T(8,128)(2,1)} %noisy_hbm.1), channel_id=1, source_target_pairs={{0,1},{1,0},{2,3},{3,2},{4,5},{5,4},{6,7},{7,6},{8,9},{9,8},{10,11... | collective-permute-start | bytes 786440 | tf_op jit(solution)/shard_map/ppermute | solution.py:543
  2.3 11.8 %collective-permute-start.3 = (bf16[264,128]{1,0:T(8,128)(2,1)S(1)}, bf16[264,128]{1,0:T(8,128)(2,1)S(1)}, u32[]{:S(2)}, u32[]{:S(2)}) collective-permute-start(bf16[264,128]{1,0:T(8,128)(2,1)S(1)} %get-tuple-element.45), channel_id=1, source_target_pairs={{0,4},{4,0},{8,12},{12,8},{1,5},{5,1},{9,13},{13,9},{2,6},{6,2},{1... | collective-permute-start | bytes 202760 | tf_op jit(solution)/shard_map/ppermute | solution.py:124
  5.0 9.1 %collective-permute-start.4 = (bf16[264,128]{1,0:T(8,128)(2,1)S(1)}, bf16[264,128]{1,0:T(8,128)(2,1)S(1)}, u32[]{:S(2)}, u32[]{:S(2)}) collective-permute-start(bf16[264,128]{1,0:T(8,128)(2,1)S(1)} %get-tuple-element.46), channel_id=1, source_target_pairs={{0,8},{4,12},{8,0},{12,4},{1,9},{5,13},{9,1},{13,5},{2,10},{6,14},... | collective-permute-start | bytes 202760 | tf_op jit(solution)/shard_map/ppermute | solution.py:124
  7.6 6.5 %collective-permute-start.5 = (bf16[264,128]{1,0:T(8,128)(2,1)S(1)}, bf16[264,128]{1,0:T(8,128)(2,1)S(1)}, u32[]{:S(2)}, u32[]{:S(2)}) collective-permute-start(bf16[264,128]{1,0:T(8,128)(2,1)S(1)} %get-tuple-element.47), channel_id=1, source_target_pairs={{0,12},{4,8},{8,4},{12,0},{1,13},{5,9},{9,5},{13,1},{2,14},{6,10},... | collective-permute-start | bytes 202760 | tf_op jit(solution)/shard_map/ppermute | solution.py:124
  7.9 3.5 %collective-permute-start.1 = (bf16[8,16,128]{2,1,0:T(8,128)(2,1)S(1)}, bf16[8,16,128]{2,1,0:T(8,128)(2,1)S(1)}, u32[]{:S(2)}, u32[]{:S(2)}) collective-permute-start(bf16[8,16,128]{2,1,0:T(8,128)(2,1)S(1)} %get-tuple-element.43), channel_id=1, source_target_pairs={{0,3},{1,2},{2,1},{3,0},{4,7},{5,6},{6,5},{7,4},{8,11},{9,10},{10,... | collective-permute-start | bytes 98312 | tf_op jit(solution)/shard_map/ppermute | solution.py:560
  11.4 1.0 %copy-start = (bf16[3,3,128,128]{3,2,1,0:T(8,128)(2,1)S(1)}, bf16[3,3,128,128]{3,2,1,0:T(8,128)(2,1)}, u32[]{:S(2)}) copy-start(bf16[3,3,128,128]{3,2,1,0:T(8,128)(2,1)} %kin_ref.3) | copy-start | bytes 884740
  11.4 1.0 %copy-start.1 = (bf16[3,3,128,128]{3,2,1,0:T(8,128)(2,1)S(1)}, bf16[3,3,128,128]{3,2,1,0:T(8,128)(2,1)}, u32[]{:S(2)}) copy-start(bf16[3,3,128,128]{3,2,1,0:T(8,128)(2,1)} %kout_ref.3) | copy-start | bytes 884740
  11.4 1.0 %copy-start.2 = (f32[128]{0:T(128)S(1)}, f32[128]{0:T(128)}, u32[]{:S(2)}) copy-start(f32[128]{0:T(128)} %param.12) | copy-start | bytes 1540
  11.4 5.1 %collective-permute-start.2 = (bf16[2,272,128]{2,1,0:T(8,128)(2,1)S(1)}, bf16[2,272,128]{2,1,0:T(8,128)(2,1)S(1)}, u32[]{:S(2)}, u32[]{:S(2)}) collective-permute-start(bf16[2,272,128]{2,1,0:T(8,128)(2,1)S(1)} %shard_map.115), channel_id=1, source_target_pairs={{1,4},{4,1},{5,8},{8,5},{9,12},{12,9},{3,6},{6,3},{7,10},{10,7},{1... | collective-permute-start | bytes 417800 | tf_op jit(solution)/shard_map/ppermute | solution.py:552
  14.1 5.1 %collective-permute-start.7 = (bf16[4,264,128]{2,1,0:T(8,128)(2,1)S(1)}, bf16[4,264,128]{2,1,0:T(8,128)(2,1)S(1)}, u32[]{:S(2)}, u32[]{:S(2)}) collective-permute-start(bf16[4,264,128]{2,1,0:T(8,128)(2,1)S(1)} %shard_map.118.block_ref), channel_id=1, source_target_pairs={{0,1},{1,0},{2,3},{3,2},{4,5},{5,4},{6,7},{7,6},{8,9},{9,8},{10,11... | collective-permute-start | bytes 811016 | tf_op jit(solution)/shard_map/ppermute | solution.py:543
  16.5 2.8 %collective-permute-start.6 = (bf16[2,272,128]{2,1,0:T(8,128)(2,1)S(1)}, bf16[2,272,128]{2,1,0:T(8,128)(2,1)S(1)}, u32[]{:S(2)}, u32[]{:S(2)}) collective-permute-start(bf16[2,272,128]{2,1,0:T(8,128)(2,1)S(1)} %collective-permute-done.2.halo_ref), channel_id=1, source_target_pairs={{0,1},{1,0},{2,3},{3,2},{4,5},{5,4},{6,7},{7,6},{8,9},{9,8},{10,11... | collective-permute-start | bytes 417800 | tf_op jit(solution)/shard_map/ppermute | solution.py:543
  21.1 3.4 %collective-permute-start.8 = (bf16[8,16,128]{2,1,0:T(8,128)(2,1)S(1)}, bf16[8,16,128]{2,1,0:T(8,128)(2,1)S(1)}, u32[]{:S(2)}, u32[]{:S(2)}) collective-permute-start(bf16[8,16,128]{2,1,0:T(8,128)(2,1)S(1)} %get-tuple-element.63), channel_id=1, source_target_pairs={{0,3},{1,2},{2,1},{3,0},{4,7},{5,6},{6,5},{7,4},{8,11},{9,10},{10,... | collective-permute-start | bytes 98312 | tf_op jit(solution)/shard_map/ppermute | solution.py:560
  24.5 2.1 %collective-permute-start.9 = (bf16[2,272,128]{2,1,0:T(8,128)(2,1)S(1)}, bf16[2,272,128]{2,1,0:T(8,128)(2,1)S(1)}, u32[]{:S(2)}, u32[]{:S(2)}) collective-permute-start(bf16[2,272,128]{2,1,0:T(8,128)(2,1)S(1)} %shard_map.120), channel_id=1, source_target_pairs={{1,4},{4,1},{5,8},{8,5},{9,12},{12,9},{3,6},{6,3},{7,10},{10,7},{1... | collective-permute-start | bytes 417800 | tf_op jit(solution)/shard_map/ppermute | solution.py:552
  26.7 14.5 %collective-permute-start.10 = (bf16[2,272,128]{2,1,0:T(8,128)(2,1)S(1)}, bf16[2,272,128]{2,1,0:T(8,128)(2,1)S(1)}, u32[]{:S(2)}, u32[]{:S(2)}) collective-permute-start(bf16[2,272,128]{2,1,0:T(8,128)(2,1)S(1)} %collective-permute-done.9.halo_ref), channel_id=1, source_target_pairs={{0,1},{1,0},{2,3},{3,2},{4,5},{5,4},{6,7},{7,6},{8,9},{9,8},{10,11... | collective-permute-start | bytes 417800 | tf_op jit(solution)/shard_map/ppermute | solution.py:543
  31.2 5.2 %collective-permute-start.11 = (bf16[2,64,128]{2,1,0:T(8,128)(2,1)S(1)}, bf16[2,64,128]{2,1,0:T(8,128)(2,1)S(1)}, u32[]{:S(2)}, u32[]{:S(2)}) collective-permute-start(bf16[2,64,128]{2,1,0:T(8,128)(2,1)S(1)} %get-tuple-element.77), channel_id=1, source_target_pairs={{0,4},{4,0},{8,12},{12,8},{1,5},{5,1},{9,13},{13,9},{2,6},{6,2},{1... | collective-permute-start | bytes 98312 | tf_op jit(solution)/shard_map/ppermute | solution.py:124
  32.4 5.7 %collective-permute-start.12 = (bf16[2,64,128]{2,1,0:T(8,128)(2,1)S(1)}, bf16[2,64,128]{2,1,0:T(8,128)(2,1)S(1)}, u32[]{:S(2)}, u32[]{:S(2)}) collective-permute-start(bf16[2,64,128]{2,1,0:T(8,128)(2,1)S(1)} %get-tuple-element.78), channel_id=1, source_target_pairs={{0,8},{4,12},{8,0},{12,4},{1,9},{5,13},{9,1},{13,5},{2,10},{6,14},... | collective-permute-start | bytes 98312 | tf_op jit(solution)/shard_map/ppermute | solution.py:124
  35.5 5.7 %collective-permute-start.13 = (bf16[2,64,128]{2,1,0:T(8,128)(2,1)S(1)}, bf16[2,64,128]{2,1,0:T(8,128)(2,1)S(1)}, u32[]{:S(2)}, u32[]{:S(2)}) collective-permute-start(bf16[2,64,128]{2,1,0:T(8,128)(2,1)S(1)} %get-tuple-element.79), channel_id=1, source_target_pairs={{0,12},{4,8},{8,4},{12,0},{1,13},{5,9},{9,5},{13,1},{2,14},{6,10},... | collective-permute-start | bytes 98312 | tf_op jit(solution)/shard_map/ppermute | solution.py:124
